TPU v7x, 256 devices: a whole 4x4x8 slice. The times are simulated.
256 devices in a mesh: row: 16 (over y_hi, z), col: 16 (over x, y_lo, core).
Axes of the slice: x: 4, y: 4 (y_hi: 2, y_lo: 2; y = y_hi * 2 + y_lo), z: 8, core: 2. Of those that a mesh axis runs over, the one named last changes fastest.
Arguments:
- fields: float32 [1, 4, 256, 256, 256], P(None, None, 'row', 'col'), may hold values from -6 to 6
- cotangent: float32 [1, 4, 256, 256, 256], P(None, None, 'row', 'col'), may hold values from -6 to 6
- spec_weights: float32 [2, 4, 4, 16, 16, 16], replicated, may hold values from -96 to 96
- point_weights: float32 [4, 4], replicated, may hold values from -3 to 3
- bias: float32 [4], replicated, may hold values from -3 to 3
Outputs:
- grad_fields: float32 [1, 4, 256, 256, 256], P(None, None, 'row', 'col')
- grad_spectral: float32 [2, 4, 4, 16, 16, 16], replicated
All inputs are finite; a program needn't handle non-finite values.
Results may differ from a plain program's by a relative error of at most 0.00011.
Values sent between devices are 32-bit elements; how exact they have to be, the bound alone decides.
No kernel may reach another device: no remote copies, remote signals or barrier semaphores. Data moves between devices by JAX's collectives and lax.ppermute only.
A program may use at most 64 MiB of HBM per device.

v0:
```python
import math

import jax
import jax.numpy as jnp
from jax import lax
from jax.sharding import PartitionSpec as P

C = 4
NX = 256
NY = 256
NZ = 256
MX = 16
MY = 16
MZ = 16


highest = lax.Precision.HIGHEST


def phase_tables(number, length, signed, start, count):
    wavenum = jnp.arange(number, dtype=jnp.int32)
    if signed:
        wavenum = jnp.where(wavenum < number // 2, wavenum, wavenum + length - number)
    points = start + jnp.arange(count, dtype=jnp.int32)
    angles = (
        2.0 * math.pi / length * (points[:, None] * wavenum[None, :] % length).astype(jnp.float32)
    )
    return (jnp.cos(angles), jnp.sin(angles))


def forward_table(number, length, start, count):
    cosine, sine = phase_tables(number, length, True, start, count)
    return jnp.stack([jnp.stack([cosine, -sine], 1), jnp.stack([sine, cosine], 1)], 0)


def inverse_table(number, length, start, count):
    cosine, sine = phase_tables(number, length, True, start, count)
    cosine = cosine.T
    sine = sine.T
    return jnp.stack([jnp.stack([cosine, sine], 1), jnp.stack([-sine, cosine], 1)], 0)


def first_table():
    cos_x, sin_x = phase_tables(MX, NX, False, 0, NX)
    return jnp.stack([cos_x, -sin_x], 1)


def last_table():
    cos_x, sin_x = phase_tables(MX, NX, False, 0, NX)
    wavenum = jnp.arange(MX, dtype=jnp.int32)
    weighting = jnp.where(wavenum == 0, 1.0, 2.0).astype(jnp.float32) / float(NX * NY * NZ)
    return jnp.stack([cos_x.T * weighting[:, None], -sin_x.T * weighting[:, None]], 0)


def to_modes(field):
    along_x = jnp.einsum("bcyzx,xtp->btpczy", field, first_table(), precision=highest)
    gathered = lax.all_to_all(along_x, "row", split_axis=2, concat_axis=5, tiled=True)
    along_y = jnp.einsum(
        "bspczy,sytq->btpcqz", gathered, forward_table(MY, NY, 0, NY), precision=highest
    )
    swapped = lax.all_to_all(along_y, "col", split_axis=4, concat_axis=5, tiled=True)
    return jnp.einsum(
        "bspcqz,sztr->btpcqr", swapped, forward_table(MZ, NZ, 0, NZ), precision=highest
    )


def from_modes(modes):
    along_z = jnp.einsum(
        "bspcqr,srtz->btpcqz", modes, inverse_table(MZ, NZ, 0, NZ), precision=highest
    )
    swapped = lax.all_to_all(along_z, "col", split_axis=5, concat_axis=4, tiled=True)
    along_y = jnp.einsum(
        "bspcqz,sqty->btpczy", swapped, inverse_table(MY, NY, 0, NY), precision=highest
    )
    gathered = lax.all_to_all(along_y, "row", split_axis=5, concat_axis=2, tiled=True)
    return jnp.einsum("btpczy,tpx->bcyzx", gathered, last_table(), precision=highest)


def per_device(fields, cotangent, spec_weights, point_weights, bias):
    row_pos = lax.axis_index("row")
    col_pos = lax.axis_index("col")
    zero_index = jnp.zeros((), jnp.int32)
    kx_local = MX // lax.axis_size("row")
    ky_local = MY // lax.axis_size("col")
    starts = (
        zero_index,
        zero_index,
        zero_index,
        row_pos * kx_local,
        col_pos * ky_local,
        zero_index,
    )
    owned_weights = lax.dynamic_slice(spec_weights, starts, (2, C, C, kx_local, ky_local, MZ))
    kx_start = row_pos * kx_local
    weight_real = owned_weights[0]
    weight_imag = owned_weights[1]
    spectrum_u = to_modes(fields)
    input_real = spectrum_u[:, 0]
    input_imag = spectrum_u[:, 1]
    mix_form = "bpiqr,iopqr->bpoqr"
    mixed_real = jnp.einsum(mix_form, input_real, weight_real, precision=highest) - jnp.einsum(
        mix_form, input_imag, weight_imag, precision=highest
    )
    mixed_imag = jnp.einsum(mix_form, input_real, weight_imag, precision=highest) + jnp.einsum(
        mix_form, input_imag, weight_real, precision=highest
    )
    spectral_term = from_modes(jnp.stack([mixed_real, mixed_imag], 1))
    local_term = jnp.einsum("bcyzx,co->boyzx", fields, point_weights, precision=highest)
    pre_activation = spectral_term + local_term + bias[None, :, None, None, None]
    gelu_slope = 0.5 * (1.0 + lax.erf(pre_activation / math.sqrt(2.0))) + pre_activation * jnp.exp(
        -0.5 * pre_activation * pre_activation
    ) / math.sqrt(2.0 * math.pi)
    upstream = cotangent * gelu_slope
    spectrum_h = to_modes(upstream)
    back_real = spectrum_h[:, 0]
    back_imag = spectrum_h[:, 1]
    grad_form = "bpiqr,bpoqr->iopqr"
    grad_real = jnp.einsum(grad_form, input_real, back_real, precision=highest) + jnp.einsum(
        grad_form, input_imag, back_imag, precision=highest
    )
    grad_imag = jnp.einsum(grad_form, input_real, back_imag, precision=highest) - jnp.einsum(
        grad_form, input_imag, back_real, precision=highest
    )
    wave_global = kx_start + jnp.arange(kx_local, dtype=jnp.int32)
    factor = jnp.where(wave_global == 0, 1.0, 2.0).astype(jnp.float32) / float(NX * NY * NZ)
    grad_block = jnp.stack([grad_real, grad_imag], 0) * factor[None, None, None, :, None, None]
    adj_form = "iopqr,bpoqr->bpiqr"
    adjoint_real = jnp.einsum(adj_form, weight_real, back_real, precision=highest) + jnp.einsum(
        adj_form, weight_imag, back_imag, precision=highest
    )
    adjoint_imag = jnp.einsum(adj_form, weight_real, back_imag, precision=highest) - jnp.einsum(
        adj_form, weight_imag, back_real, precision=highest
    )
    grad_fields = from_modes(jnp.stack([adjoint_real, adjoint_imag], 1))
    grad_fields = grad_fields + jnp.einsum(
        "boyzx,co->bcyzx", upstream, point_weights, precision=highest
    )
    full_grad = jnp.zeros((2, C, C, MX, MY, MZ), jnp.float32)
    full_grad = lax.dynamic_update_slice(full_grad, grad_block, starts)
    grad_spectral = lax.psum(full_grad, ("row", "col"))
    return (grad_fields, grad_spectral)


def solution(mesh):
    placed = (P(None, None, "row", "col", None), P(None, None, "row", "col", None), P(), P(), P())
    return jax.shard_map(
        per_device,
        mesh=mesh,
        in_specs=placed,
        out_specs=(P(None, None, "row", "col", None), P()),
        check_vma=False,
    )
```

profile of v0, /device:TPU:1, one launch (start us, length us, event | category | flops | bytes accessed | tf_op | source)
XLA Modules:
  0.0 426.7 jit_solution(5578637302729846114)
XLA Ops:
  7.3 1.1 copy-done
  8.4 4.4 %convolution_bitcast_fusion.3 = f32[1,2,16,4,16,16]{4,2,5,3,1,0:T(8,128)S(1)} fusion(f32[1,4,16,16,256]{4,3,2,1,0:T(8,128)S(1)} %copy-done, f32[256,1,16]{0,2,1:T(8,128)S(1)} %get-tuple-element.46, f32[256,1,16]{0,2,1:T(8,128)S(1)} %get-tuple-element.47), kind=kOutput, calls=%fused_computation.7 | convolution fusion | flops 100671488 | bytes 1212416 | tf_op jit(solution)/shard_map/bcyzx,xtp->btpczy/dot_general | solution.py:56
  13.2 1.0 reshape.708
  14.2 11.7 %all-to-all-start = ((f32[16,1,2048]{2,1,0:T(1,128)}), f32[16,1,2048]{2,1,0:T(1,128)S(1)}, u32[]{:S(2)}, u32[]{:S(2)}) async-start(f32[16,1,2048]{2,1,0:T(1,128)} %reshape.708), calls=%async_computation | async-start | bytes 262144 | tf_op jit(solution)/shard_map/all_to_all | solution.py:57
  26.3 8.6 %all-to-all-done = f32[16,1,2048]{2,1,0:T(1,128)S(1)} async-done(((f32[16,1,2048]{2,1,0:T(1,128)}), f32[16,1,2048]{2,1,0:T(1,128)S(1)}, u32[]{:S(2)}, u32[]{:S(2)}) %all-to-all-start) | async-done | bytes 131104 | tf_op jit(solution)/shard_map/all_to_all | solution.py:57
  35.4 0.9 reduce.16
  37.8 0.7 convolution_bitcast_fusion.7
  38.5 0.7 reshape.710
  39.2 6.5 %all-to-all-start.1 = ((f32[16,1,128]{2,1,0:T(1,128)}), f32[16,1,128]{2,1,0:T(1,128)S(1)}, u32[]{:S(2)}, u32[]{:S(2)}) async-start(f32[16,1,128]{2,1,0:T(1,128)} %reshape.710), calls=%async_computation.1 | async-start | bytes 16384 | tf_op jit(solution)/shard_map/all_to_all | solution.py:61
  45.7 0.9 constant_dynamic-slice_fusion.1
  46.6 4.6 %all-to-all-done.1 = f32[16,1,128]{2,1,0:T(1,128)S(1)} async-done(((f32[16,1,128]{2,1,0:T(1,128)}), f32[16,1,128]{2,1,0:T(1,128)S(1)}, u32[]{:S(2)}, u32[]{:S(2)}) %all-to-all-start.1) | async-done | bytes 8224 | tf_op jit(solution)/shard_map/all_to_all | solution.py:61
  51.1 0.6 reduce.17
  52.8 1.0 reshape.712
  53.8 3.9 all-to-all-start.2
  57.7 2.8 fusion.16
  60.5 2.7 all-to-all-done.2
  63.2 0.6 reduce.18
  65.4 1.5 reshape.714
  66.8 3.8 all-to-all-start.3
  70.7 8.7 %all-to-all-done.3 = f32[16,1,2048]{2,1,0:T(1,128)S(1)} async-done(((f32[16,1,2048]{2,1,0:T(1,128)}), f32[16,1,2048]{2,1,0:T(1,128)S(1)}, u32[]{:S(2)}, u32[]{:S(2)}) %all-to-all-start.3) | async-done | bytes 131104 | tf_op jit(solution)/shard_map/all_to_all | solution.py:75
  79.4 0.9 reduce.19
  80.3 0.7 reshape.715
  81.0 2.2 copy.86
  83.2 4.0 fusion.8
  87.2 4.2 convolution_bitcast_fusion.1
  92.2 12.3 %all_to_all.96 = f32[16,1,2048]{2,1,0:T(1,128)S(1)} all-to-all(f32[16,1,2048]{2,1,0:T(1,128)S(1)} %reshape.716), channel_id=1, replica_groups=mesh['row'=16,'col'=16] {'row'}, dimensions={0} | all-to-all | bytes 262144 | tf_op jit(solution)/shard_map/all_to_all | solution.py:57
  104.6 0.9 reduce.20
  105.9 1.1 bitcast_bitcast_fusion
  106.9 1.7 copy.188
  109.1 0.7 convolution_bitcast_fusion.6
  109.9 10.8 %all_to_all.97 = f32[16,1,128]{2,1,0:T(1,128)S(1)} all-to-all(f32[16,1,128]{2,1,0:T(1,128)S(1)} %reshape.718), channel_id=1, replica_groups=mesh['row'=16,'col'=16] {'col'}, dimensions={0} | all-to-all | bytes 16384 | tf_op jit(solution)/shard_map/all_to_all | solution.py:61
  120.7 0.6 reduce.21
  122.4 1.0 reshape.720
  123.3 3.9 all-to-all-start.6
  127.3 5.5 %all-to-all-done.6 = f32[16,1,128]{2,1,0:T(1,128)S(1)} async-done(((f32[16,1,128]{2,1,0:T(1,128)}), f32[16,1,128]{2,1,0:T(1,128)S(1)}, u32[]{:S(2)}, u32[]{:S(2)}) %all-to-all-start.6) | async-done | bytes 8224 | tf_op jit(solution)/shard_map/all_to_all | solution.py:71
  135.0 1.5 reshape.722
  136.4 3.5 all-to-all-start.7
  140.0 2.6 fusion.13
  142.6 2.5 broadcast_in_dim.14
  145.1 1.6 dynamic_update_slice.3
  146.8 2.2 all-to-all-done.7
  148.9 0.9 reduce.23
  149.9 1.7 reshape.723
  151.6 2.2 copy.103
  153.8 1.4 fusion
  155.2 1.6 copy.108
  156.8 258.4 %all-reduce.2.cloned.1.call-done = f32[2,4,4,16,16,16]{5,4,3,2,1,0:T(8,128)} async-done(((f32[2,4,4,16,16,16]{5,4,3,2,1,0:T(8,128)}), f32[2,4,4,16,16,16]{5,4,3,2,1,0:T(8,128)}) %all-reduce.2.cloned.1.call-update) | async-done | bytes 524304 | tf_op jit(solution)/shard_map/psum | solution.py:140
  415.2 4.7 %copy.228 = f32[2,4,4,16,16,16]{5,4,3,2,1,0:T(8,128)} copy(f32[2,4,4,16,16,16]{5,4,3,2,1,0:T(8,128)} %all-reduce.2.cloned.1.call-done) | data formatting | bytes 1048576
  (58 shorter events, 10.2 us)
Async XLA Ops:
  7.2 1.2 copy-start
  14.2 20.7 %all-to-all-start = ((f32[16,1,2048]{2,1,0:T(1,128)}), f32[16,1,2048]{2,1,0:T(1,128)S(1)}, u32[]{:S(2)}, u32[]{:S(2)}) async-start(f32[16,1,2048]{2,1,0:T(1,128)} %reshape.708), calls=%async_computation | async-start | bytes 262144 | tf_op jit(solution)/shard_map/all_to_all | solution.py:57
  35.4 22.3 %copy-start.1 = (f32[4,4]{1,0:T(4,128)S(1)}, f32[4,4]{1,0:T(4,128)}, u32[]{:S(2)}) copy-start(f32[4,4]{1,0:T(4,128)} %param.8) | copy-start | bytes 196
  39.2 12.0 %all-to-all-start.1 = ((f32[16,1,128]{2,1,0:T(1,128)}), f32[16,1,128]{2,1,0:T(1,128)S(1)}, u32[]{:S(2)}, u32[]{:S(2)}) async-start(f32[16,1,128]{2,1,0:T(1,128)} %reshape.710), calls=%async_computation.1 | async-start | bytes 16384 | tf_op jit(solution)/shard_map/all_to_all | solution.py:61
  53.8 9.4 %all-to-all-start.2 = ((f32[16,1,128]{2,1,0:T(1,128)}), f32[16,1,128]{2,1,0:T(1,128)S(1)}, u32[]{:S(2)}, u32[]{:S(2)}) async-start(f32[16,1,128]{2,1,0:T(1,128)} %reshape.712), calls=%async_computation.2 | async-start | bytes 16384 | tf_op jit(solution)/shard_map/all_to_all | solution.py:71
  57.7 25.5 %copy-start.2 = (f32[4]{0:T(128)S(1)}, f32[4]{0:T(128)}, u32[]{:S(2)}) copy-start(f32[4]{0:T(128)} %param.9) | copy-start | bytes 52
  66.8 12.5 %all-to-all-start.3 = ((f32[16,1,2048]{2,1,0:T(1,128)}), f32[16,1,2048]{2,1,0:T(1,128)S(1)}, u32[]{:S(2)}, u32[]{:S(2)}) async-start(f32[16,1,2048]{2,1,0:T(1,128)} %reshape.714), calls=%async_computation.3 | async-start | bytes 262144 | tf_op jit(solution)/shard_map/all_to_all | solution.py:75
  123.3 9.4 %all-to-all-start.6 = ((f32[16,1,128]{2,1,0:T(1,128)}), f32[16,1,128]{2,1,0:T(1,128)S(1)}, u32[]{:S(2)}, u32[]{:S(2)}) async-start(f32[16,1,128]{2,1,0:T(1,128)} %reshape.720), calls=%async_computation.6 | async-start | bytes 16384 | tf_op jit(solution)/shard_map/all_to_all | solution.py:71
  136.4 12.5 %all-to-all-start.7 = ((f32[16,1,2048]{2,1,0:T(1,128)}), f32[16,1,2048]{2,1,0:T(1,128)S(1)}, u32[]{:S(2)}, u32[]{:S(2)}) async-start(f32[16,1,2048]{2,1,0:T(1,128)} %reshape.722), calls=%async_computation.7 | async-start | bytes 262144 | tf_op jit(solution)/shard_map/all_to_all | solution.py:75
  140.0 275.2 %all-reduce.2.cloned.1.call-start = ((), (), s32[]{:S(2)}) async-start(), calls=%async_computation.8 | async-start | bytes 8388608 | tf_op jit(solution)/shard_map/psum | solution.py:140
Sparse Core Ops, SparseCore 0:
  146.9 268.2 all-reduce.1
where the time goes:
time: 428 us; the launch traced here: 427 us
  waiting for transfers between devices  291 us (68%)
  local copies, waits for them, and re-layouts  35.6 us (8%)
  starting transfers between devices  33.5 us (8%)
  blocking collectives  23.2 us (5%)
  matrix products  22.5 us (5%)
  between operations  14.5 us (3%)
  other arithmetic  6.94 us (2%)
    psum x1, waiting for transfers between devices, per_device(): grad_spectral = lax.psum(full_grad, ('row', 'col'))  258 us
    unnamed x26, local copies, waits for them, and re-layouts  18.6 us
    all_to_all x1, blocking collectives, to_modes(): lax.all_to_all(along_x, 'row', split_axis=2, concat_axis=5, tiled=True)  12.3 us
    all_to_all x1, starting transfers between devices, to_modes(): lax.all_to_all(along_x, 'row', split_axis=2, concat_axis=5, tiled=True)  11.7 us
    all_to_all x1, blocking collectives, to_modes(): lax.all_to_all(along_y, 'col', split_axis=4, concat_axis=5, tiled=True)  10.8 us
    all_to_all x2, waiting for transfers between devices, from_modes(): lax.all_to_all(along_y, 'row', split_axis=5, concat_axis=2, tiled=True)  10.8 us
    dot_general x2, matrix products, to_modes(): jnp.einsum('bcyzx,xtp->btpczy', field, first_table(), precision=highest)  8.67 us
    all_to_all x1, waiting for transfers between devices, to_modes(): lax.all_to_all(along_x, 'row', split_axis=2, concat_axis=5, tiled=True)  8.57 us
  transfers between devices with their start and end apart: 7, of which 7 were waited for; matrix products, arithmetic and copies ran while one was open for 4% of the time, Pallas kernels for 0%

commit v1 on v0

v1 whole, which is shorter than its diff:
```python
import functools
import math

import jax
import jax.numpy as jnp
import numpy as np
from jax import lax
from jax.experimental import pallas as pl
from jax.experimental.pallas import tpu as pltpu
from jax.sharding import PartitionSpec as P

C = 4
N = 256
K = 16
LOCAL = 16
CELLS = LOCAL * LOCAL
MODES = K * K
ROWS = 2 * C * K

VMEM = pl.BlockSpec(memory_space=pltpu.VMEM)
SMEM = pl.BlockSpec(memory_space=pltpu.SMEM)
NT = (((1,), (1,)), ((), ()))
NN = (((1,), (0,)), ((), ()))
TN = (((0,), (0,)), ((), ()))


def two_parts(table):
    high = np.asarray(table, jnp.bfloat16)
    low = np.asarray(table - np.asarray(high, np.float64), jnp.bfloat16)
    return np.stack([high, low])


def signed_waves():
    index = np.arange(K)
    return np.where(index < K // 2, index, index - K)


def tables():
    angle = 2.0 * np.pi / N * (np.arange(K)[:, None] * np.arange(N)[None, :] % N)
    forward_x = np.concatenate([np.cos(angle), -np.sin(angle)], 0)
    weighting = np.where(np.arange(K) == 0, 1.0, 2.0)[:, None] / float(N) ** 3
    inverse_x = np.concatenate([np.cos(angle) * weighting, -np.sin(angle) * weighting], 0)
    one = np.arange(LOCAL)[:, None] * signed_waves()[None, :]
    both = one[:, None, :, None] + one[None, :, None, :]
    angle = 2.0 * np.pi / N * (both.reshape(CELLS, MODES) % N)
    plane = np.concatenate([np.cos(angle), -np.sin(angle)], 1)
    return two_parts(forward_x), two_parts(inverse_x), two_parts(plane)


def split(value):
    high = value.astype(jnp.bfloat16)
    low = (value - high.astype(jnp.float32)).astype(jnp.bfloat16)
    return high, low


def dot3(left, right, dims):
    dot = functools.partial(
        lax.dot_general, dimension_numbers=dims, preferred_element_type=jnp.float32
    )
    return dot(left[0], right[0]) + (dot(left[0], right[1]) + dot(left[1], right[0]))


def analyse(channel, phase, forward_x, plane):
    real, imag = [], []
    for c in range(C):
        along_x = dot3(forward_x, split(channel(c)), NT)
        real.append(along_x[:K])
        imag.append(along_x[K:])
    both = dot3(split(jnp.concatenate(real + imag, 0)), plane, NN)
    half = ROWS // 2
    part_re = both[:half, :MODES] - both[half:, MODES:]
    part_im = both[:half, MODES:] + both[half:, :MODES]
    cosine, sine = phase[0:1, :], phase[1:2, :]
    return part_re * cosine - part_im * sine, part_re * sine + part_im * cosine


def synthesise(modes_re, modes_im, phase, inverse_x, plane):
    cosine, sine = phase[0:1, :], phase[1:2, :]
    here_re = modes_re * cosine + modes_im * sine
    here_im = modes_im * cosine - modes_re * sine
    left = jnp.concatenate(
        [jnp.concatenate([here_re, here_im], 1), jnp.concatenate([here_im, -here_re], 1)], 0
    )
    lines = dot3(split(left), plane, NT)
    half = ROWS // 2
    out = []
    for c in range(C):
        pair = jnp.concatenate([lines[c * K : (c + 1) * K], lines[half + c * K :][:K]], 0)
        out.append(dot3(split(pair), inverse_x, TN))
    return out


def parts(ref):
    return ref[0], ref[1]


def analysis_kernel(fields, phase, forward_x, plane, out):
    result = analyse(lambda c: fields[c], phase[...], parts(forward_x), parts(plane))
    out[: ROWS // 2] = result[0]
    out[ROWS // 2 :] = result[1]


def spread_kernel(pieces, out):
    total = jnp.sum(pieces[...], axis=0)
    out[...] = jnp.broadcast_to(total[None], out.shape)


def take(ref, t, c):
    start = (t * C + c) * K
    return ref[start : start + K]


def forward_kernel(
    modes, weights, fields, cotangent, point, bias, phase, forward_x, inverse_x, plane, up, out
):
    mixed_re, mixed_im = [], []
    for o in range(C):
        re = im = None
        for i in range(C):
            a, b = take(modes, 0, i), take(modes, 1, i)
            w, v = weights[0, i, o], weights[1, i, o]
            re = a * w - b * v if re is None else re + (a * w - b * v)
            im = a * v + b * w if im is None else im + (a * v + b * w)
        mixed_re.append(re)
        mixed_im.append(im)
    term = synthesise(
        jnp.concatenate(mixed_re, 0),
        jnp.concatenate(mixed_im, 0),
        phase[...],
        parts(inverse_x),
        parts(plane),
    )
    for o in range(C):
        pre = term[o] + bias[o]
        for i in range(C):
            pre = pre + point[i, o] * fields[i]
        slope = 0.5 * (1.0 + lax.erf(pre * math.sqrt(0.5))) + pre * jnp.exp(
            -0.5 * pre * pre
        ) * (1.0 / math.sqrt(2.0 * math.pi))
        up[o] = cotangent[o] * slope
    result = analyse(lambda c: up[c], phase[...], parts(forward_x), parts(plane))
    out[: ROWS // 2] = result[0]
    out[ROWS // 2 :] = result[1]


def backward_kernel(
    modes, back, weights, up, point, phase, inverse_x, plane, factor, grad_fields, grad_spectral
):
    adjoint_re, adjoint_im = [], []
    for i in range(C):
        re = im = None
        for o in range(C):
            a, b = take(back, 0, o), take(back, 1, o)
            w, v = weights[0, i, o], weights[1, i, o]
            re = a * w + b * v if re is None else re + (a * w + b * v)
            im = b * w - a * v if im is None else im + (b * w - a * v)
        adjoint_re.append(re)
        adjoint_im.append(im)
    term = synthesise(
        jnp.concatenate(adjoint_re, 0),
        jnp.concatenate(adjoint_im, 0),
        phase[...],
        parts(inverse_x),
        parts(plane),
    )
    for i in range(C):
        total = term[i]
        for o in range(C):
            total = total + point[i, o] * up[o]
        grad_fields[i] = total
    for o in range(C):
        a, b = take(back, 0, o) * factor[...], take(back, 1, o) * factor[...]
        for i in range(C):
            u, w = take(modes, 0, i), take(modes, 1, i)
            grad_spectral[0, i, o] = u * a + w * b
            grad_spectral[1, i, o] = u * b - w * a


def position_phase():
    lane = jnp.arange(MODES, dtype=jnp.int32)
    steps = (lane // K) * lax.axis_index("row") + (lane % K) * lax.axis_index("col")
    angle = (steps % K).astype(jnp.float32) * (2.0 * math.pi / K)
    return jnp.stack([jnp.cos(angle), -jnp.sin(angle)], 0)


def swap(pieces, axis):
    return lax.all_to_all(pieces, axis, 0, 0, tiled=True)


def total_modes(partial):
    shape = jax.ShapeDtypeStruct((K, ROWS // K, MODES), jnp.float32)
    spread = pl.pallas_call(spread_kernel, out_shape=shape, in_specs=[VMEM], out_specs=VMEM)
    pieces = swap(partial.reshape(shape.shape), "col")
    pieces = swap(spread(pieces), "row")
    pieces = swap(spread(pieces), "col")
    return pieces.reshape(ROWS, MODES)


def per_device(fields, cotangent, spec_weights, point_weights, bias):
    forward_x, inverse_x, plane = [jnp.asarray(t) for t in tables()]
    factor = np.where(np.arange(K) == 0, 1.0, 2.0) / float(N) ** 3
    factor = jnp.asarray(np.broadcast_to(factor[:, None], (K, MODES)), jnp.float32)
    cells = (C, CELLS, N)
    shape = fields.shape
    fields = fields.reshape(cells)
    cotangent = cotangent.reshape(cells)
    weights = spec_weights.reshape(2, C, C, K, MODES)
    phase = position_phase()
    float_of = functools.partial(jax.ShapeDtypeStruct, dtype=jnp.float32)
    partial = pl.pallas_call(
        analysis_kernel,
        out_shape=float_of((ROWS, MODES)),
        in_specs=[VMEM] * 4,
        out_specs=VMEM,
    )(fields, phase, forward_x, plane)
    modes = total_modes(partial)
    upstream, partial = pl.pallas_call(
        forward_kernel,
        out_shape=(float_of(cells), float_of((ROWS, MODES))),
        in_specs=[VMEM] * 4 + [SMEM] * 2 + [VMEM] * 4,
        out_specs=(VMEM, VMEM),
    )(
        modes, weights, fields, cotangent, point_weights, bias, phase, forward_x, inverse_x, plane
    )
    back = total_modes(partial)
    grad_fields, grad_spectral = pl.pallas_call(
        backward_kernel,
        out_shape=(float_of(cells), float_of((2, C, C, K, MODES))),
        in_specs=[VMEM] * 4 + [SMEM] + [VMEM] * 4,
        out_specs=(VMEM, VMEM),
    )(modes, back, weights, upstream, point_weights, phase, inverse_x, plane, factor)
    return grad_fields.reshape(shape), grad_spectral.reshape(spec_weights.shape)


def solution(mesh):
    placed = P(None, None, "row", "col", None)
    return jax.shard_map(
        per_device,
        mesh=mesh,
        in_specs=(placed, placed, P(), P(), P()),
        out_specs=(placed, P()),
        check_vma=False,
    )
```

time: 428 us -> 105 us (0.25)
  waiting for transfers between devices: 291 us -> 2 us
  blocking collectives: 23.2 us -> 68.4 us
  starting transfers between devices: 33.5 us -> 5.36 us
  local copies, waits for them, and re-layouts: 35.6 us -> 8.52 us
  matrix products: 22.5 us -> 0 us
  Pallas kernels: 0 us -> 18.3 us
  between operations: 14.5 us -> 0.65 us
  other arithmetic: 6.94 us -> 0.67 us
    psum x1 -> x0, waiting for transfers between devices: 258 us -> none  [per_device(): grad_spectral = lax.psum(full_grad, ('row', 'col'))]
    all_to_all x2 -> x5, blocking collectives: 23.2 us -> 68.4 us  [swap(): return lax.all_to_all(pieces, axis, 0, 0, tiled=True)]
    all_to_all x6 -> x1, waiting for transfers between devices: 32.1 us -> 2 us  [swap(): return lax.all_to_all(pieces, axis, 0, 0, tiled=True)]
    all_to_all x6 -> x1, starting transfers between devices: 33.4 us -> 5.36 us  [swap(): return lax.all_to_all(pieces, axis, 0, 0, tiled=True)]
    dot_general x14 -> x0, matrix products: 22.5 us -> none  [the longest x2 8.67 us: to_modes(): jnp.einsum('bcyzx,xtp->btpczy', field, first_table(), precision=highest)]
    pallas_call x0 -> x7, Pallas kernels: none -> 18.3 us  [the longest x1 4.8 us: per_device(): pl.pallas_call(forward_kernel, out_shape=(float_of(cells), float_of((ROWS...]
    unnamed x26 -> x2, local copies, waits for them, and re-layouts: 18.6 us -> 0.64 us
    reshape x0 -> x2, local copies, waits for them, and re-layouts: none -> 7.88 us  [the longest x1 4.2 us: per_device(): weights = spec_weights.reshape(2, C, C, K, MODES)]
  transfers between devices with their start and end apart: 7 -> 1, of which waited for: 7 -> 1; matrix products, arithmetic and copies ran while one was open for 4% -> 4% of each run, Pallas kernels for 0% -> 0%
where the time goes in v1:
time: 105 us; the launch traced here: 104 us
  blocking collectives  68.4 us (65%)
  Pallas kernels  18.3 us (17%)
  local copies, waits for them, and re-layouts  8.52 us (8%)
  starting transfers between devices  5.36 us (5%)
  waiting for transfers between devices  2 us (2%)
    all_to_all x5, blocking collectives, swap(): return lax.all_to_all(pieces, axis, 0, 0, tiled=True)  68.4 us
    all_to_all x1, starting transfers between devices, swap(): return lax.all_to_all(pieces, axis, 0, 0, tiled=True)  5.36 us
    pallas_call x1, Pallas kernels, per_device(): pl.pallas_call(forward_kernel, out_shape=(float_of(cells), float_of((ROWS...  4.8 us
    pallas_call x1, Pallas kernels, per_device(): pl.pallas_call(backward_kernel, out_shape=(float_of(cells), float_of((2,...  4.2 us
    reshape x1, local copies, waits for them, and re-layouts, per_device(): weights = spec_weights.reshape(2, C, C, K, MODES)  4.2 us
    reshape x1, local copies, waits for them, and re-layouts, per_device(): grad_spectral.reshape(spec_weights.shape)  3.68 us
    pallas_call x2, Pallas kernels, total_modes(): pieces = swap(spread(pieces), 'row')  3.17 us
    pallas_call x2, Pallas kernels, total_modes(): pieces = swap(spread(pieces), 'col')  3.17 us
  transfers between devices with their start and end apart: 1, of which 1 were waited for; matrix products, arithmetic and copies ran while one was open for 4% of the time, Pallas kernels for 0%

profile of v1, /device:TPU:1, one launch (start us, length us, event | category | flops | bytes accessed | tf_op | source)
XLA Modules:
  0.0 103.9 jit_solution(6846339974929295753)
XLA Ops:
  0.6 0.1 sine_negate_fusion
  0.7 0.6 pad_maximum_fusion.phase
  1.3 2.9 %shard_map.104 = f32[128,256]{1,0:T(8,128)} custom-call(f32[4,256,256]{2,1,0:T(8,128)} %bitcast.11, f32[2,256]{1,0:T(2,128)} %pad_maximum_fusion.phase, bf16[2,32,256]{2,1,0:T(8,128)(2,1)} %constant.55.clone.forward_x, bf16[2,256,512]{2,1,0:T(8,128)(2,1)} %constant.57.clone.plane), custom_call_target="tpu_custom_call" | custom-call | tf_op jit(solution)/shard_map/pallas_call | solution.py:210
  4.2 13.4 %all_to_all.30.pieces = f32[16,8,256]{2,1,0:T(8,128)} all-to-all(f32[16,8,256]{2,1,0:T(8,128)} %bitcast.17), channel_id=1, replica_groups=mesh['row'=16,'col'=16] {'col'}, dimensions={0} | all-to-all | bytes 262144 | tf_op jit(solution)/shard_map/all_to_all | solution.py:187
  17.6 1.6 %shard_map.105 = f32[16,8,256]{2,1,0:T(8,128)} custom-call(f32[16,8,256]{2,1,0:T(8,128)} %all_to_all.30.pieces), custom_call_target="tpu_custom_call" | custom-call | tf_op jit(solution)/shard_map/pallas_call | solution.py:194
  19.2 19.3 %all_to_all.31.pieces = f32[16,8,256]{2,1,0:T(8,128)} all-to-all(f32[16,8,256]{2,1,0:T(8,128)} %shard_map.105), channel_id=1, replica_groups=mesh['row'=16,'col'=16] {'row'}, dimensions={0} | all-to-all | bytes 262144 | tf_op jit(solution)/shard_map/all_to_all | solution.py:187
  38.6 1.6 %shard_map.106 = f32[16,8,256]{2,1,0:T(8,128)} custom-call(f32[16,8,256]{2,1,0:T(8,128)} %all_to_all.31.pieces), custom_call_target="tpu_custom_call" | custom-call | tf_op jit(solution)/shard_map/pallas_call | solution.py:195
  40.1 5.4 %all-to-all-start.2 = ((f32[16,8,256]{2,1,0:T(8,128)}), f32[16,8,256]{2,1,0:T(8,128)S(1)}, u32[]{:S(2)}, u32[]{:S(2)}) async-start(f32[16,8,256]{2,1,0:T(8,128)} %shard_map.106), calls=%async_computation.2 | async-start | bytes 262144 | tf_op jit(solution)/shard_map/all_to_all | solution.py:187
  45.5 4.2 %reshape.141.weights = f32[2,4,4,16,256]{4,3,2,1,0:T(8,128)} reshape(f32[2,4,4,16,16,16]{5,4,3,2,1,0:T(8,128)} %param.11) | data formatting | bytes 1048576 | tf_op jit(solution)/shard_map/reshape | solution.py:207
  49.7 2.0 %all-to-all-done.2 = f32[16,8,256]{2,1,0:T(8,128)S(1)} async-done(((f32[16,8,256]{2,1,0:T(8,128)}), f32[16,8,256]{2,1,0:T(8,128)S(1)}, u32[]{:S(2)}, u32[]{:S(2)}) %all-to-all-start.2) | async-done | bytes 131104 | tf_op jit(solution)/shard_map/all_to_all | solution.py:187
  51.7 0.0 copy-start
  51.7 0.6 copy-done
  52.3 4.8 %shard_map.107 = (f32[4,256,256]{2,1,0:T(8,128)}, f32[128,256]{1,0:T(8,128)}) custom-call(f32[128,256]{1,0:T(8,128)} %bitcast.13, f32[2,4,4,16,256]{4,3,2,1,0:T(8,128)} %reshape.141.weights, f32[4,256,256]{2,1,0:T(8,128)} %bitcast.12, f32[4,256,256]{2,1,0:T(8,128)} %bitcast.15, f32[4,4]{1,0:T(4,128)} %point.3, f32[4]{0:T(128)} %bias.1, ...), custom_call_target="tpu_custom_call" | custom-call | tf_op jit(solution)/shard_map/pallas_call | solution.py:217
  57.1 10.6 %all_to_all.32.pieces = f32[16,8,256]{2,1,0:T(8,128)} all-to-all(f32[16,8,256]{2,1,0:T(8,128)} %bitcast.18), channel_id=1, replica_groups=mesh['row'=16,'col'=16] {'col'}, dimensions={0} | all-to-all | bytes 262144 | tf_op jit(solution)/shard_map/all_to_all | solution.py:187
  67.8 1.6 %shard_map.108 = f32[16,8,256]{2,1,0:T(8,128)} custom-call(f32[16,8,256]{2,1,0:T(8,128)} %all_to_all.32.pieces), custom_call_target="tpu_custom_call" | custom-call | tf_op jit(solution)/shard_map/pallas_call | solution.py:194
  69.4 13.2 %all_to_all.33.pieces = f32[16,8,256]{2,1,0:T(8,128)} all-to-all(f32[16,8,256]{2,1,0:T(8,128)} %shard_map.108), channel_id=1, replica_groups=mesh['row'=16,'col'=16] {'row'}, dimensions={0} | all-to-all | bytes 262144 | tf_op jit(solution)/shard_map/all_to_all | solution.py:187
  82.6 1.6 %shard_map.109 = f32[16,8,256]{2,1,0:T(8,128)} custom-call(f32[16,8,256]{2,1,0:T(8,128)} %all_to_all.33.pieces), custom_call_target="tpu_custom_call" | custom-call | tf_op jit(solution)/shard_map/pallas_call | solution.py:195
  84.1 11.9 %all_to_all.34 = f32[16,8,256]{2,1,0:T(8,128)} all-to-all(f32[16,8,256]{2,1,0:T(8,128)} %shard_map.109), channel_id=1, replica_groups=mesh['row'=16,'col'=16] {'col'}, dimensions={0} | all-to-all | bytes 262144 | tf_op jit(solution)/shard_map/all_to_all | solution.py:187
  96.0 4.2 %shard_map.110 = (f32[4,256,256]{2,1,0:T(8,128)}, f32[2,4,4,16,256]{4,3,2,1,0:T(8,128)}) custom-call(f32[128,256]{1,0:T(8,128)} %bitcast.14, f32[128,256]{1,0:T(8,128)} %bitcast.16, f32[2,4,4,16,256]{4,3,2,1,0:T(8,128)} %reshape.141.weights, f32[4,256,256]{2,1,0:T(8,128)} %get-tuple-element.7.up, f32[4,4]{1,0:T(4,128)} %point.3, ...), custom_call_target="tpu_custom_call" | custom-call | tf_op jit(solution)/shard_map/pallas_call | solution.py:226
  100.2 3.7 %reshape.146 = f32[2,4,4,16,16,16]{5,4,3,2,1,0:T(8,128)} reshape(f32[2,4,4,16,256]{4,3,2,1,0:T(8,128)} %get-tuple-element.9) | data formatting | bytes 1048576 | tf_op jit(solution)/shard_map/reshape | solution.py:232
Async XLA Ops:
  40.1 11.6 %all-to-all-start.2 = ((f32[16,8,256]{2,1,0:T(8,128)}), f32[16,8,256]{2,1,0:T(8,128)S(1)}, u32[]{:S(2)}, u32[]{:S(2)}) async-start(f32[16,8,256]{2,1,0:T(8,128)} %shard_map.106), calls=%async_computation.2 | async-start | bytes 262144 | tf_op jit(solution)/shard_map/all_to_all | solution.py:187
  51.7 0.6 copy-start

commit v2 on v1

--- a/solution.py
+++ b/solution.py
@@ -19,6 +19,7 @@
 
 VMEM = pl.BlockSpec(memory_space=pltpu.VMEM)
 SMEM = pl.BlockSpec(memory_space=pltpu.SMEM)
+PARAMS = pltpu.CompilerParams(vmem_limit_bytes=24 << 20)
 NT = (((1,), (1,)), ((), ()))
 NN = (((1,), (0,)), ((), ()))
 TN = (((0,), (0,)), ((), ()))
@@ -183,17 +184,31 @@
     return jnp.stack([jnp.cos(angle), -jnp.sin(angle)], 0)
 
 
+def near(value):
+    return pltpu.with_memory_space_constraint(value, pltpu.VMEM)
+
+
+def near_out(shape):
+    return pltpu.VMEM(shape, jnp.float32)
+
+
 def swap(pieces, axis):
     return lax.all_to_all(pieces, axis, 0, 0, tiled=True)
 
 
 def total_modes(partial):
-    shape = jax.ShapeDtypeStruct((K, ROWS // K, MODES), jnp.float32)
-    spread = pl.pallas_call(spread_kernel, out_shape=shape, in_specs=[VMEM], out_specs=VMEM)
-    pieces = swap(partial.reshape(shape.shape), "col")
-    pieces = swap(spread(pieces), "row")
-    pieces = swap(spread(pieces), "col")
-    return pieces.reshape(ROWS, MODES)
+    shape = (K, ROWS // K, MODES)
+    spread = pl.pallas_call(
+        spread_kernel,
+        out_shape=near_out(shape),
+        in_specs=[VMEM],
+        out_specs=VMEM,
+        compiler_params=PARAMS,
+    )
+    pieces = swap(partial.reshape(shape), "col")
+    pieces = swap(spread(near(pieces)), "row")
+    pieces = swap(spread(near(pieces)), "col")
+    return near(pieces.reshape(ROWS, MODES))
 
 
 def per_device(fields, cotangent, spec_weights, point_weights, bias):
@@ -206,19 +221,23 @@
     cotangent = cotangent.reshape(cells)
     weights = spec_weights.reshape(2, C, C, K, MODES)
     phase = position_phase()
+    fields, cotangent, weights, phase = [near(v) for v in (fields, cotangent, weights, phase)]
+    forward_x, inverse_x, plane = [near(v) for v in (forward_x, inverse_x, plane)]
     float_of = functools.partial(jax.ShapeDtypeStruct, dtype=jnp.float32)
     partial = pl.pallas_call(
         analysis_kernel,
-        out_shape=float_of((ROWS, MODES)),
+        out_shape=near_out((ROWS, MODES)),
         in_specs=[VMEM] * 4,
         out_specs=VMEM,
+        compiler_params=PARAMS,
     )(fields, phase, forward_x, plane)
     modes = total_modes(partial)
     upstream, partial = pl.pallas_call(
         forward_kernel,
-        out_shape=(float_of(cells), float_of((ROWS, MODES))),
+        out_shape=(near_out(cells), near_out((ROWS, MODES))),
         in_specs=[VMEM] * 4 + [SMEM] * 2 + [VMEM] * 4,
         out_specs=(VMEM, VMEM),
+        compiler_params=PARAMS,
     )(
         modes, weights, fields, cotangent, point_weights, bias, phase, forward_x, inverse_x, plane
     )
@@ -228,7 +247,8 @@
         out_shape=(float_of(cells), float_of((2, C, C, K, MODES))),
         in_specs=[VMEM] * 4 + [SMEM] + [VMEM] * 4,
         out_specs=(VMEM, VMEM),
-    )(modes, back, weights, upstream, point_weights, phase, inverse_x, plane, factor)
+        compiler_params=PARAMS,
+    )(modes, back, weights, near(upstream), point_weights, phase, inverse_x, plane, factor)
     return grad_fields.reshape(shape), grad_spectral.reshape(spec_weights.shape)
 
 

time: 105 us -> 89.7 us (0.85)
  Pallas kernels: 18.3 us -> 7.52 us
  blocking collectives: 68.4 us -> 63.6 us
    pallas_call x6, Pallas kernels: 14.1 us -> 4.52 us  [the longest x1 2.84 us: per_device(): pl.pallas_call(forward_kernel, out_shape=(near_out(cells), near_out((ROWS...]
    all_to_all x5, blocking collectives: 68.4 us -> 63.6 us  [swap(): return lax.all_to_all(pieces, axis, 0, 0, tiled=True)]
    unnamed x2 -> x22, local copies, waits for them, and re-layouts: 0.64 us -> 3.05 us
    pallas_call x1, Pallas kernels: 4.2 us -> 3 us  [per_device(): pl.pallas_call(backward_kernel, out_shape=(float_of(cells), float_of((2,...]
where the time goes in v2:
time: 89.7 us; the launch traced here: 89.2 us
  blocking collectives  63.6 us (71%)
  local copies, waits for them, and re-layouts  9.2 us (10%)
  Pallas kernels  7.52 us (8%)
  starting transfers between devices  5.36 us (6%)
  waiting for transfers between devices  2.69 us (3%)
    all_to_all x5, blocking collectives, swap(): return lax.all_to_all(pieces, axis, 0, 0, tiled=True)  63.6 us
    all_to_all x1, starting transfers between devices, swap(): return lax.all_to_all(pieces, axis, 0, 0, tiled=True)  5.36 us
    reshape x1, local copies, waits for them, and re-layouts, per_device(): weights = spec_weights.reshape(2, C, C, K, MODES)  3.49 us
    unnamed x22, local copies, waits for them, and re-layouts  3.05 us
    pallas_call x1, Pallas kernels, per_device(): pl.pallas_call(backward_kernel, out_shape=(float_of(cells), float_of((2,...  3 us
    pallas_call x1, Pallas kernels, per_device(): pl.pallas_call(forward_kernel, out_shape=(near_out(cells), near_out((ROWS...  2.84 us
    all_to_all x1, waiting for transfers between devices, swap(): return lax.all_to_all(pieces, axis, 0, 0, tiled=True)  2.69 us
    reshape x1, local copies, waits for them, and re-layouts, per_device(): grad_spectral.reshape(spec_weights.shape)  2.66 us
  transfers between devices with their start and end apart: 1, of which 1 were waited for; matrix products, arithmetic and copies ran while one was open for 4% of the time, Pallas kernels for 0%

profile of v2, /device:TPU:1, one launch (start us, length us, event | category | flops | bytes accessed | tf_op | source)
XLA Modules:
  0.0 89.2 jit_solution(1504949911539692671)
XLA Ops:
  0.6 0.0 copy-start.9
  0.6 0.0 copy-start.10
  0.7 0.1 sine_negate_fusion
  0.7 0.0 copy-start
  0.7 1.0 %copy-done = bf16[2,256,512]{2,1,0:T(8,128)(2,1)S(1)} copy-done((bf16[2,256,512]{2,1,0:T(8,128)(2,1)S(1)}, bf16[2,256,512]{2,1,0:T(8,128)(2,1)}, u32[]{:S(2)}) %copy-start) | copy-done | bytes 524312
  1.8 0.0 copy-start.2
  1.8 1.2 %copy-done.2 = f32[1,4,16,16,256]{4,3,2,1,0:T(8,128)S(1)} copy-done((f32[1,4,16,16,256]{4,3,2,1,0:T(8,128)S(1)}, f32[1,4,16,16,256]{4,3,2,1,0:T(8,128)}, u32[]{:S(2)}) %copy-start.2) | copy-done | bytes 1048600
  3.0 0.0 copy-start.6
  3.0 0.8 copy-done.6
  3.8 0.0 copy-start.1
  3.8 0.0 copy-start.3
  3.8 0.0 copy-start.4
  3.8 0.0 copy-start.5
  3.8 0.0 copy-start.7
  3.8 0.9 %shard_map.104 = f32[128,256]{1,0:T(8,128)S(1)} custom-call(f32[4,256,256]{2,1,0:T(8,128)S(1)} %bitcast.11, f32[2,256]{1,0:T(2,128)S(1)} %pad_maximum_fusion.phase, bf16[2,32,256]{2,1,0:T(8,128)(2,1)S(1)} %copy-done.6, bf16[2,256,512]{2,1,0:T(8,128)(2,1)S(1)} %copy-done), custom_call_target="tpu_custom_call" | custom-call | tf_op jit(solution)/shard_map/pallas_call | solution.py:227
  4.7 12.7 %all_to_all.30.pieces = f32[16,8,256]{2,1,0:T(8,128)S(1)} all-to-all(f32[16,8,256]{2,1,0:T(8,128)S(1)} %bitcast.17), channel_id=1, replica_groups=mesh['row'=16,'col'=16] {'col'}, dimensions={0} | all-to-all | bytes 262144 | tf_op jit(solution)/shard_map/all_to_all | solution.py:196
  17.5 19.4 %all_to_all.31.pieces = f32[16,8,256]{2,1,0:T(8,128)S(1)} all-to-all(f32[16,8,256]{2,1,0:T(8,128)S(1)} %shard_map.105), channel_id=1, replica_groups=mesh['row'=16,'col'=16] {'row'}, dimensions={0} | all-to-all | bytes 262144 | tf_op jit(solution)/shard_map/all_to_all | solution.py:196
  36.9 0.7 shard_map.106
  37.5 5.4 %all-to-all-start.2 = ((f32[16,8,256]{2,1,0:T(8,128)}), f32[16,8,256]{2,1,0:T(8,128)S(1)}, u32[]{:S(2)}, u32[]{:S(2)}) async-start(f32[16,8,256]{2,1,0:T(8,128)} %shard_map.106), calls=%async_computation.2 | async-start | bytes 262144 | tf_op jit(solution)/shard_map/all_to_all | solution.py:196
  42.9 0.0 copy-start.8
  42.9 3.5 %reshape.141.weights = f32[2,4,4,16,256]{4,3,2,1,0:T(8,128)S(1)} reshape(f32[2,4,4,16,16,16]{5,4,3,2,1,0:T(8,128)} %param.11) | data formatting | bytes 1048576 | tf_op jit(solution)/shard_map/reshape | solution.py:222
  46.4 2.7 %all-to-all-done.2 = f32[16,8,256]{2,1,0:T(8,128)S(1)} async-done(((f32[16,8,256]{2,1,0:T(8,128)}), f32[16,8,256]{2,1,0:T(8,128)S(1)}, u32[]{:S(2)}, u32[]{:S(2)}) %all-to-all-start.2) | async-done | bytes 131104 | tf_op jit(solution)/shard_map/all_to_all | solution.py:196
  49.1 0.0 copy-done.9
  49.1 0.0 copy-done.10
  49.1 0.0 copy-done.1
  49.1 0.0 copy-done.3
  49.1 0.0 copy-done.4
  49.1 0.0 copy-done.5
  49.1 0.0 copy-done.7
  49.1 2.8 %shard_map.107 = (f32[4,256,256]{2,1,0:T(8,128)S(1)}, f32[128,256]{1,0:T(8,128)S(1)}) custom-call(f32[128,256]{1,0:T(8,128)S(1)} %bitcast.13, f32[2,4,4,16,256]{4,3,2,1,0:T(8,128)S(1)} %reshape.141.weights, f32[4,256,256]{2,1,0:T(8,128)S(1)} %bitcast.12, f32[4,256,256]{2,1,0:T(8,128)S(1)} %bitcast.15, f32[4,4]{1,0:T(4,128)S(1)} %copy-done.9, ...), custom_call_target="tpu_custom_call" | custom-call | tf_op jit(solution)/shard_map/pallas_call | solution.py:235
  52.0 9.1 %all_to_all.32.pieces = f32[16,8,256]{2,1,0:T(8,128)S(1)} all-to-all(f32[16,8,256]{2,1,0:T(8,128)S(1)} %bitcast.18), channel_id=1, replica_groups=mesh['row'=16,'col'=16] {'col'}, dimensions={0} | all-to-all | bytes 262144 | tf_op jit(solution)/shard_map/all_to_all | solution.py:196
  61.1 11.7 %all_to_all.33.pieces = f32[16,8,256]{2,1,0:T(8,128)S(1)} all-to-all(f32[16,8,256]{2,1,0:T(8,128)S(1)} %shard_map.108), channel_id=1, replica_groups=mesh['row'=16,'col'=16] {'row'}, dimensions={0} | all-to-all | bytes 262144 | tf_op jit(solution)/shard_map/all_to_all | solution.py:196
  72.9 10.7 %all_to_all.34 = f32[16,8,256]{2,1,0:T(8,128)S(1)} all-to-all(f32[16,8,256]{2,1,0:T(8,128)S(1)} %shard_map.109), channel_id=1, replica_groups=mesh['row'=16,'col'=16] {'col'}, dimensions={0} | all-to-all | bytes 262144 | tf_op jit(solution)/shard_map/all_to_all | solution.py:196
  83.6 0.0 copy-done.8
  83.6 3.0 %shard_map.110 = (f32[4,256,256]{2,1,0:T(8,128)}, f32[2,4,4,16,256]{4,3,2,1,0:T(8,128)S(1)}) custom-call(f32[128,256]{1,0:T(8,128)S(1)} %bitcast.14, f32[128,256]{1,0:T(8,128)S(1)} %bitcast.16, f32[2,4,4,16,256]{4,3,2,1,0:T(8,128)S(1)} %reshape.141.weights, f32[4,256,256]{2,1,0:T(8,128)S(1)} %get-tuple-element.7.up, f32[4,4]{1,0:T(4,128)S(1)} %copy-done.9, ...), custom_call_target="tpu_custom_call" | custom-call | tf_op jit(solution)/shard_map/pallas_call | solution.py:245
  86.6 2.7 %reshape.146 = f32[2,4,4,16,16,16]{5,4,3,2,1,0:T(8,128)} reshape(f32[2,4,4,16,256]{4,3,2,1,0:T(8,128)S(1)} %get-tuple-element.9) | data formatting | bytes 1048576 | tf_op jit(solution)/shard_map/reshape | solution.py:252
  (4 shorter events, 0.1 us)
Async XLA Ops:
  0.6 48.5 %copy-start.9 = (f32[4,4]{1,0:T(4,128)S(1)}, f32[4,4]{1,0:T(4,128)}, u32[]{:S(2)}) copy-start(f32[4,4]{1,0:T(4,128)} %point.3) | copy-start | bytes 196
  0.6 48.5 %copy-start.10 = (f32[4]{0:T(128)S(1)}, f32[4]{0:T(128)}, u32[]{:S(2)}) copy-start(f32[4]{0:T(128)} %bias.1) | copy-start | bytes 52
  0.7 1.0 %copy-start = (bf16[2,256,512]{2,1,0:T(8,128)(2,1)S(1)}, bf16[2,256,512]{2,1,0:T(8,128)(2,1)}, u32[]{:S(2)}) copy-start(bf16[2,256,512]{2,1,0:T(8,128)(2,1)} %constant.57.clone.plane) | copy-start | bytes 1572868
  1.8 1.2 %copy-start.2 = (f32[1,4,16,16,256]{4,3,2,1,0:T(8,128)S(1)}, f32[1,4,16,16,256]{4,3,2,1,0:T(8,128)}, u32[]{:S(2)}) copy-start(f32[1,4,16,16,256]{4,3,2,1,0:T(8,128)} %param.9) | copy-start | bytes 3145732
  3.0 0.8 copy-start.6
  3.8 45.3 %copy-start.1 = (bf16[2,256,512]{2,1,0:T(8,128)(2,1)S(1)}, bf16[2,256,512]{2,1,0:T(8,128)(2,1)}, u32[]{:S(2)}) copy-start(bf16[2,256,512]{2,1,0:T(8,128)(2,1)} %constant.57.clone.plane) | copy-start | bytes 1572868
  3.8 45.3 %copy-start.3 = (f32[1,4,16,16,256]{4,3,2,1,0:T(8,128)S(1)}, f32[1,4,16,16,256]{4,3,2,1,0:T(8,128)}, u32[]{:S(2)}) copy-start(f32[1,4,16,16,256]{4,3,2,1,0:T(8,128)} %param.9) | copy-start | bytes 3145732
  3.8 45.4 %copy-start.4 = (f32[1,4,16,16,256]{4,3,2,1,0:T(8,128)S(1)}, f32[1,4,16,16,256]{4,3,2,1,0:T(8,128)}, u32[]{:S(2)}) copy-start(f32[1,4,16,16,256]{4,3,2,1,0:T(8,128)} %param.10) | copy-start | bytes 3145732
  3.8 45.4 %copy-start.5 = (bf16[2,32,256]{2,1,0:T(8,128)(2,1)S(1)}, bf16[2,32,256]{2,1,0:T(8,128)(2,1)}, u32[]{:S(2)}) copy-start(bf16[2,32,256]{2,1,0:T(8,128)(2,1)} %constant.56.clone.inverse_x) | copy-start | bytes 98308
  3.8 45.4 %copy-start.7 = (bf16[2,32,256]{2,1,0:T(8,128)(2,1)S(1)}, bf16[2,32,256]{2,1,0:T(8,128)(2,1)}, u32[]{:S(2)}) copy-start(bf16[2,32,256]{2,1,0:T(8,128)(2,1)} %constant.55.clone.forward_x) | copy-start | bytes 98308
  37.5 11.6 %all-to-all-start.2 = ((f32[16,8,256]{2,1,0:T(8,128)}), f32[16,8,256]{2,1,0:T(8,128)S(1)}, u32[]{:S(2)}, u32[]{:S(2)}) async-start(f32[16,8,256]{2,1,0:T(8,128)} %shard_map.106), calls=%async_computation.2 | async-start | bytes 262144 | tf_op jit(solution)/shard_map/all_to_all | solution.py:196
  42.9 40.7 %copy-start.8 = (f32[16,256]{1,0:T(8,128)S(1)}, f32[16,256]{1,0:T(8,128)}, u32[]{:S(2)}) copy-start(f32[16,256]{1,0:T(8,128)} %constant.58.clone.factor) | copy-start | bytes 49156

commit v3 on v1

v3 whole, which is shorter than its diff:
```python
import functools
import math

import jax
import jax.numpy as jnp
import numpy as np
from jax import lax
from jax.experimental import pallas as pl
from jax.experimental.pallas import tpu as pltpu
from jax.sharding import PartitionSpec as P

C = 4
N = 256
K = 16
LOCAL = 16
CELLS = LOCAL * LOCAL
MODES = K * K
ROWS = 2 * C * K

VMEM = pl.BlockSpec(memory_space=pltpu.VMEM)
HBM = pl.BlockSpec(memory_space=pltpu.HBM)
SMEM = pl.BlockSpec(memory_space=pltpu.SMEM)
PARAMS = pltpu.CompilerParams(vmem_limit_bytes=24 << 20)
NT = (((1,), (1,)), ((), ()))
NN = (((1,), (0,)), ((), ()))
TN = (((0,), (0,)), ((), ()))


def two_parts(table):
    high = np.asarray(table, jnp.bfloat16)
    low = np.asarray(table - np.asarray(high, np.float64), jnp.bfloat16)
    return np.stack([high, low])


def signed_waves():
    index = np.arange(K)
    return np.where(index < K // 2, index, index - K)


def tables():
    angle = 2.0 * np.pi / N * (np.arange(K)[:, None] * np.arange(N)[None, :] % N)
    forward_x = np.concatenate([np.cos(angle), -np.sin(angle)], 0)
    weighting = np.where(np.arange(K) == 0, 1.0, 2.0)[:, None] / float(N) ** 3
    inverse_x = np.concatenate([np.cos(angle) * weighting, -np.sin(angle) * weighting], 0)
    one = np.arange(LOCAL)[:, None] * signed_waves()[None, :]
    both = one[:, None, :, None] + one[None, :, None, :]
    angle = 2.0 * np.pi / N * (both.reshape(CELLS, MODES) % N)
    plane = np.concatenate([np.cos(angle), -np.sin(angle)], 1)
    return two_parts(forward_x), two_parts(inverse_x), two_parts(plane)


def split(value):
    high = value.astype(jnp.bfloat16)
    low = (value - high.astype(jnp.float32)).astype(jnp.bfloat16)
    return high, low


def dot3(left, right, dims):
    dot = functools.partial(
        lax.dot_general, dimension_numbers=dims, preferred_element_type=jnp.float32
    )
    return dot(left[0], right[0]) + (dot(left[0], right[1]) + dot(left[1], right[0]))


def analyse(channel, phase, forward_x, plane, out, ready=None):
    real, imag = [], []
    for c in range(C):
        along_x = dot3(forward_x, split(channel(c)), NT)
        real.append(along_x[:K])
        imag.append(along_x[K:])
    if ready is not None:
        ready()
    both = dot3(split(jnp.concatenate(real + imag, 0)), parts(plane), NN)
    half = ROWS // 2
    part_re = both[:half, :MODES] - both[half:, MODES:]
    part_im = both[:half, MODES:] + both[half:, :MODES]
    cosine, sine = phase[0:1, :], phase[1:2, :]
    for t, part in enumerate(
        (part_re * cosine - part_im * sine, part_re * sine + part_im * cosine)
    ):
        for c in range(C):
            out[:, t * C + c, :] = part[c * K : (c + 1) * K]


def synthesise(modes_re, modes_im, phase, inverse_x, plane):
    cosine, sine = phase[0:1, :], phase[1:2, :]
    here_re = modes_re * cosine + modes_im * sine
    here_im = modes_im * cosine - modes_re * sine
    left = jnp.concatenate(
        [jnp.concatenate([here_re, here_im], 1), jnp.concatenate([here_im, -here_re], 1)], 0
    )
    lines = dot3(split(left), plane, NT)
    half = ROWS // 2
    out = []
    for c in range(C):
        pair = jnp.concatenate([lines[c * K : (c + 1) * K], lines[half + c * K :][:K]], 0)
        out.append(dot3(split(pair), inverse_x, TN))
    return out


def parts(ref):
    return ref[0], ref[1]


def own_wave():
    flip = 2 * (lax.axis_index("row") // (K // 2))
    return jnp.bitwise_xor(lax.axis_index("col"), flip)


def analysis_kernel(
    fields, forward_x, plane, stored, phase, out, cells, weights, lines, square, slab, arrived
):
    table = pltpu.make_async_copy(forward_x, lines, arrived.at[C])
    table.start()
    copies = [
        pltpu.make_async_copy(fields.at[c], cells.at[c], arrived.at[c]) for c in range(C)
    ]
    for copy in copies:
        copy.start()
    second = pltpu.make_async_copy(plane, square, arrived.at[C + 1])
    second.start()
    third = pltpu.make_async_copy(stored.at[:, own_wave()], slab, arrived.at[C + 2])
    third.start()
    table.wait()

    def channel(c):
        copies[c].wait()
        return cells[c]

    analyse(channel, phase[...], parts(lines), square, out, second.wait)
    third.wait()
    weights[...] = jnp.concatenate([slab[:, q, :] for q in range(K)], 1)


def spread_kernel(pieces, out):
    total = jnp.sum(pieces[...], axis=0)
    out[...] = jnp.broadcast_to(total[None], out.shape)


def forward_mix_kernel(pieces, weights, out):
    total = jnp.sum(pieces[...], axis=0)
    re = im = 0.0
    for i in range(C):
        a, b = total[i : i + 1], total[C + i : C + i + 1]
        w, v = weights[i * C : (i + 1) * C], weights[C * C + i * C :][:C]
        re = re + (a * w - b * v)
        im = im + (a * v + b * w)
    both = jnp.concatenate([re, im, total], 0)
    out[...] = jnp.broadcast_to(both[None], out.shape)


def backward_mix_kernel(pieces, weights, out):
    total = jnp.sum(pieces[...], axis=0)
    re = im = 0.0
    for o in range(C):
        a, b = total[o : o + 1], total[C + o : C + o + 1]
        w, v = [
            jnp.concatenate([weights[pl.ds((t * C + i) * C + o, 1), :] for i in range(C)], 0)
            for t in range(2)
        ]
        re = re + (a * w + b * v)
        im = im + (b * w - a * v)
    both = jnp.concatenate([re, im, total], 0)
    out[...] = jnp.broadcast_to(both[None], out.shape)


def take(ref, row):
    return ref[:, row, :]


def take_mixed(ref):
    return [
        jnp.concatenate([take(ref, t * C + c) for c in range(C)], 0) for t in range(2)
    ]


def forward_kernel(
    modes, fields, cotangent, point, bias, phase, forward_x, inverse_x, plane, up, out
):
    term = synthesise(*take_mixed(modes), phase[...], parts(inverse_x), parts(plane))
    for o in range(C):
        pre = term[o] + bias[o]
        for i in range(C):
            pre = pre + point[i, o] * fields[i]
        slope = 0.5 * (1.0 + lax.erf(pre * math.sqrt(0.5))) + pre * jnp.exp(
            -0.5 * pre * pre
        ) * (1.0 / math.sqrt(2.0 * math.pi))
        up[o] = cotangent[o] * slope
    analyse(lambda c: up[c], phase[...], parts(forward_x), plane, out)


def backward_kernel(
    modes,
    back,
    up,
    point,
    phase,
    inverse_x,
    plane,
    factor,
    grad_fields,
    grad_spectral,
    cells,
    stored,
    sent,
):
    copies = []

    def send(source, target):
        copies.append(pltpu.make_async_copy(source, target, sent.at[len(copies)]))
        copies[-1].start()

    scaled = [
        [take(back, (2 + t) * C + o) * factor[...] for t in range(2)] for o in range(C)
    ]
    for i in range(C):
        u, w = take(modes, 2 * C + i), take(modes, 3 * C + i)
        for o in range(C):
            a, b = scaled[o]
            for t, value in enumerate((u * a + w * b, u * b - w * a)):
                for q in range(K):
                    stored[t, i, o, :, q, :] = value[:, q * K : (q + 1) * K]
        for t in range(2):
            send(stored.at[t, i], grad_spectral.at[t, i])
    term = synthesise(*take_mixed(back), phase[...], parts(inverse_x), parts(plane))
    for i in range(C):
        total = term[i]
        for o in range(C):
            total = total + point[i, o] * up[o]
        cells[i] = total
        send(cells.at[i], grad_fields.at[i])
    for copy in copies:
        copy.wait()


def position_phase():
    lane = jnp.arange(MODES, dtype=jnp.int32)
    steps = (lane // K) * lax.axis_index("row") + (lane % K) * lax.axis_index("col")
    angle = (steps % K).astype(jnp.float32) * (2.0 * math.pi / K)
    return jnp.stack([jnp.cos(angle), -jnp.sin(angle)], 0)


def near(value):
    return pltpu.with_memory_space_constraint(value, pltpu.VMEM)


def far(value):
    return pltpu.with_memory_space_constraint(value, pltpu.HBM)


def near_out(shape):
    return pltpu.VMEM(shape, jnp.float32)


def groups():
    index = np.arange(256).reshape(2, 8, 4, 2, 2)
    index[1] = index[1, :, :, ::-1]
    index = index.reshape(K, K)
    return index.tolist(), index.T.tolist()


def swap(pieces, members):
    return lax.all_to_all(
        pieces, ("row", "col"), 0, 0, tiled=True, axis_index_groups=members
    )


def call(kernel, out_shape, in_specs, scratch_shapes=()):
    where = [VMEM if not isinstance(o, jax.ShapeDtypeStruct) else HBM for o in out_shape]
    return pl.pallas_call(
        kernel,
        out_shape=tuple(out_shape),
        in_specs=in_specs,
        out_specs=tuple(where),
        scratch_shapes=scratch_shapes,
        compiler_params=PARAMS,
    )


def summed_modes(partial, weights, mix_kernel):
    shape = (K, 2 * C, MODES)
    near_by, alike = groups()
    pieces = near(swap(partial, near_by))
    (pieces,) = call(spread_kernel, [near_out(shape)], [VMEM])(pieces)
    pieces = near(swap(pieces, alike))
    shape = (K, 4 * C, MODES)
    (pieces,) = call(mix_kernel, [near_out(shape)], [VMEM] * 2)(pieces, weights)
    return near(swap(pieces, near_by))


def per_device(fields, cotangent, spec_weights, point_weights, bias):
    forward_x, inverse_x, plane = [jnp.asarray(t) for t in tables()]
    factor = np.where(np.arange(K) == 0, 1.0, 2.0) / float(N) ** 3
    factor = jnp.asarray(np.broadcast_to(factor[:, None], (K, MODES)), jnp.float32)
    shape = fields.shape
    cells = (C, CELLS, N)
    phase = near(position_phase())
    partial, fields, weights = call(
        analysis_kernel,
        [near_out((K, 2 * C, MODES)), near_out(cells), near_out((2 * C * C, MODES))],
        [HBM] * 4 + [VMEM],
        [
            pltpu.VMEM((2, 2 * K, N), jnp.bfloat16),
            pltpu.VMEM((2, CELLS, 2 * MODES), jnp.bfloat16),
            pltpu.VMEM((2 * C * C, K, K), jnp.float32),
            pltpu.SemaphoreType.DMA((C + 3,)),
        ],
    )(
        far(fields.reshape(cells)),
        far(forward_x),
        far(plane),
        far(spec_weights.reshape(2 * C * C, K, K, K)),
        phase,
    )
    weights = near(weights)
    forward_x, inverse_x, plane = [near(v) for v in (forward_x, inverse_x, plane)]
    modes = summed_modes(partial, weights, forward_mix_kernel)
    upstream, partial = call(
        forward_kernel,
        [near_out(cells), near_out((K, 2 * C, MODES))],
        [VMEM] * 3 + [SMEM] * 2 + [VMEM] * 4,
    )(
        modes,
        near(fields),
        near(cotangent.reshape(cells)),
        point_weights,
        bias,
        phase,
        forward_x,
        inverse_x,
        plane,
    )
    back = summed_modes(partial, weights, backward_mix_kernel)
    grad_fields, grad_spectral = call(
        backward_kernel,
        [
            jax.ShapeDtypeStruct(cells, jnp.float32),
            jax.ShapeDtypeStruct((2, C, C, K, K, K), jnp.float32),
        ],
        [VMEM] * 3 + [SMEM] + [VMEM] * 4,
        [
            pltpu.VMEM(cells, jnp.float32),
            pltpu.VMEM((2, C, C, K, K, K), jnp.float32),
            pltpu.SemaphoreType.DMA((3 * C,)),
        ],
    )(
        modes,
        back,
        near(upstream),
        point_weights,
        phase,
        inverse_x,
        plane,
        near(factor),
    )
    return grad_fields.reshape(shape), grad_spectral


def solution(mesh):
    placed = P(None, None, "row", "col", None)
    return jax.shard_map(
        per_device,
        mesh=mesh,
        in_specs=(placed, placed, P(), P(), P()),
        out_specs=(placed, P()),
        check_vma=False,
    )
```

time: 105 us -> 92.7 us (0.88)
  local copies, waits for them, and re-layouts: 8.52 us -> 0.04 us
  blocking collectives: 68.4 us -> 75.4 us
  starting transfers between devices: 5.36 us -> 0 us
  Pallas kernels: 18.3 us -> 16.1 us
  waiting for transfers between devices: 2 us -> 0 us
    reshape x2 -> x0, local copies, waits for them, and re-layouts: 7.88 us -> none  [the longest x1 4.2 us: per_device(): weights = spec_weights.reshape(2, C, C, K, MODES)]
    all_to_all x5 -> x6, blocking collectives: 68.4 us -> 75.4 us  [swap(): lax.all_to_all(pieces, ('row', 'col'), 0, 0, tiled=True, axis_index_group...]
    all_to_all x1 -> x0, starting transfers between devices: 5.36 us -> none  [swap(): return lax.all_to_all(pieces, axis, 0, 0, tiled=True)]
    pallas_call x7, Pallas kernels: 18.3 us -> 16.1 us  [the longest x1 10.1 us: per_device(): call(backward_kernel, [jax.ShapeDtypeStruct(cells, jnp.float32), jax.Shap...]
    all_to_all x1 -> x0, waiting for transfers between devices: 2 us -> none  [swap(): return lax.all_to_all(pieces, axis, 0, 0, tiled=True)]
  transfers between devices with their start and end apart: 1 -> 0, of which waited for: 1 -> 0; matrix products, arithmetic and copies ran while one was open for 4% -> 0% of each run, Pallas kernels for 0% -> 0%
where the time goes in v3:
time: 92.7 us; the launch traced here: 92.4 us
  blocking collectives  75.4 us (81%)
  Pallas kernels  16.1 us (17%)
    all_to_all x6, blocking collectives, swap(): lax.all_to_all(pieces, ('row', 'col'), 0, 0, tiled=True, axis_index_group...  75.4 us
    pallas_call x1, Pallas kernels, per_device(): call(backward_kernel, [jax.ShapeDtypeStruct(cells, jnp.float32), jax.Shap...  10.1 us
    pallas_call x1, Pallas kernels, per_device(): call(analysis_kernel, [near_out((K, 2 * C, MODES)), near_out(cells), near...  2.95 us
    pallas_call x1, Pallas kernels, per_device(): call(forward_kernel, [near_out(cells), near_out((K, 2 * C, MODES))], [VME...  2.89 us

profile of v3, /device:TPU:1, one launch (start us, length us, event | category | flops | bytes accessed | tf_op | source)
XLA Modules:
  0.0 92.4 jit_solution(556915746549862025)
XLA Ops:
  0.6 0.0 copy-start
  0.6 0.0 copy-start.3
  0.7 0.0 copy-start.2
  0.7 0.0 copy-start.5
  0.7 0.0 copy-start.6
  0.7 0.0 copy-start.1
  0.7 0.1 sine_negate_fusion
  0.8 2.9 %shard_map.104 = (f32[16,8,256]{2,1,0:T(8,128)S(1)}, f32[4,256,256]{2,1,0:T(8,128)S(1)}, f32[32,256]{1,0:T(8,128)S(1)}) custom-call(f32[4,256,256]{2,1,0:T(8,128)} %bitcast.6, bf16[2,32,256]{2,1,0:T(8,128)(2,1)} %constant.55.clone.forward_x, bf16[2,256,512]{2,1,0:T(8,128)(2,1)} %constant.57.clone.plane, f32[32,16,16,16]{3,2,1,0:T(8,128)} %bitcast.5, ...), custom_call_target="tpu_custom_call" | custom-call | tf_op jit(solution)/shard_map/pallas_call | solution.py:298
  3.7 0.0 copy-start.4
  3.8 12.7 %all_to_all.30.pieces = f32[16,8,256]{2,1,0:T(8,128)S(1)} all-to-all(f32[16,8,256]{2,1,0:T(8,128)S(1)} %get-tuple-element.9), channel_id=1, replica_groups={{0,1,2,3,4,5,6,7,8,9,10,11,12,13,14,15},{16,17,18,19,20,21,22,23,24,25,..., dimensions={0} | all-to-all | bytes 262144 | tf_op jit(solution)/shard_map/all_to_all | solution.py:263
  16.5 18.4 %all_to_all.31.pieces = f32[16,8,256]{2,1,0:T(8,128)S(1)} all-to-all(f32[16,8,256]{2,1,0:T(8,128)S(1)} %shard_map.105), channel_id=1, replica_groups={{0,16,32,48,64,80,96,112,130,146,162,178,194,210,226,242},{1,17,33,49,6..., dimensions={0} | all-to-all | bytes 262144 | tf_op jit(solution)/shard_map/all_to_all | solution.py:263
  34.9 11.9 %all_to_all.32.modes = f32[16,16,256]{2,1,0:T(8,128)S(1)} all-to-all(f32[16,16,256]{2,1,0:T(8,128)S(1)} %shard_map.106), channel_id=1, replica_groups={{0,1,2,3,4,5,6,7,8,9,10,11,12,13,14,15},{16,17,18,19,20,21,22,23,24,25,..., dimensions={0} | all-to-all | bytes 524288 | tf_op jit(solution)/shard_map/all_to_all | solution.py:263
  46.8 0.0 copy-done
  46.8 0.0 copy-done.3
  46.8 0.0 copy-done.2
  46.8 0.0 copy-done.5
  46.9 0.0 copy-done.6
  46.9 0.0 copy-done.1
  46.9 2.9 %shard_map.107 = (f32[4,256,256]{2,1,0:T(8,128)S(1)}, f32[16,8,256]{2,1,0:T(8,128)S(1)}) custom-call(f32[16,16,256]{2,1,0:T(8,128)S(1)} %all_to_all.32.modes, f32[4,256,256]{2,1,0:T(8,128)S(1)} %get-tuple-element.11.fields, f32[4,256,256]{2,1,0:T(8,128)S(1)} %bitcast.4, f32[4,4]{1,0:T(4,128)S(1)} %copy-done.5, f32[4]{0:T(128)S(1)} %copy-done.6, ...), custom_call_target="tpu_custom_call" | custom-call | tf_op jit(solution)/shard_map/pallas_call | solution.py:318
  49.8 9.0 %all_to_all.33.pieces = f32[16,8,256]{2,1,0:T(8,128)S(1)} all-to-all(f32[16,8,256]{2,1,0:T(8,128)S(1)} %get-tuple-element.12), channel_id=1, replica_groups={{0,1,2,3,4,5,6,7,8,9,10,11,12,13,14,15},{16,17,18,19,20,21,22,23,24,25,..., dimensions={0} | all-to-all | bytes 262144 | tf_op jit(solution)/shard_map/all_to_all | solution.py:263
  58.8 11.4 %all_to_all.34.pieces = f32[16,8,256]{2,1,0:T(8,128)S(1)} all-to-all(f32[16,8,256]{2,1,0:T(8,128)S(1)} %shard_map.108), channel_id=1, replica_groups={{0,16,32,48,64,80,96,112,130,146,162,178,194,210,226,242},{1,17,33,49,6..., dimensions={0} | all-to-all | bytes 262144 | tf_op jit(solution)/shard_map/all_to_all | solution.py:263
  70.3 11.9 %all_to_all.35.back = f32[16,16,256]{2,1,0:T(8,128)S(1)} all-to-all(f32[16,16,256]{2,1,0:T(8,128)S(1)} %shard_map.109), channel_id=1, replica_groups={{0,1,2,3,4,5,6,7,8,9,10,11,12,13,14,15},{16,17,18,19,20,21,22,23,24,25,..., dimensions={0} | all-to-all | bytes 524288 | tf_op jit(solution)/shard_map/all_to_all | solution.py:263
  82.3 0.0 copy-done.4
  82.3 10.1 %shard_map.110 = (f32[4,256,256]{2,1,0:T(8,128)}, f32[2,4,4,16,16,16]{5,4,3,2,1,0:T(8,128)}) custom-call(f32[16,16,256]{2,1,0:T(8,128)S(1)} %all_to_all.32.modes, f32[16,16,256]{2,1,0:T(8,128)S(1)} %all_to_all.35.back, f32[4,256,256]{2,1,0:T(8,128)S(1)} %get-tuple-element.13.up, f32[4,4]{1,0:T(4,128)S(1)} %copy-done.5, f32[2,256]{1,0:T(2,128)S(1)} %pad_maximum_fusion.phase, ...), custom_call_target="tpu_custom_call" | custom-call | tf_op jit(solution)/shard_map/pallas_call | solution.py:334
  (5 shorter events, 0.1 us)
Async XLA Ops:
  0.6 46.2 %copy-start = (bf16[2,256,512]{2,1,0:T(8,128)(2,1)S(1)}, bf16[2,256,512]{2,1,0:T(8,128)(2,1)}, u32[]{:S(2)}) copy-start(bf16[2,256,512]{2,1,0:T(8,128)(2,1)} %constant.57.clone.plane) | copy-start | bytes 1572868
  0.6 46.2 %copy-start.3 = (bf16[2,32,256]{2,1,0:T(8,128)(2,1)S(1)}, bf16[2,32,256]{2,1,0:T(8,128)(2,1)}, u32[]{:S(2)}) copy-start(bf16[2,32,256]{2,1,0:T(8,128)(2,1)} %constant.55.clone.forward_x) | copy-start | bytes 98308
  0.7 46.2 %copy-start.2 = (bf16[2,32,256]{2,1,0:T(8,128)(2,1)S(1)}, bf16[2,32,256]{2,1,0:T(8,128)(2,1)}, u32[]{:S(2)}) copy-start(bf16[2,32,256]{2,1,0:T(8,128)(2,1)} %constant.56.clone.inverse_x) | copy-start | bytes 98308
  0.7 46.2 %copy-start.5 = (f32[4,4]{1,0:T(4,128)S(1)}, f32[4,4]{1,0:T(4,128)}, u32[]{:S(2)}) copy-start(f32[4,4]{1,0:T(4,128)} %point.3) | copy-start | bytes 196
  0.7 46.2 %copy-start.6 = (f32[4]{0:T(128)S(1)}, f32[4]{0:T(128)}, u32[]{:S(2)}) copy-start(f32[4]{0:T(128)} %bias.1) | copy-start | bytes 52
  0.7 46.2 %copy-start.1 = (f32[1,4,16,16,256]{4,3,2,1,0:T(8,128)S(1)}, f32[1,4,16,16,256]{4,3,2,1,0:T(8,128)}, u32[]{:S(2)}) copy-start(f32[1,4,16,16,256]{4,3,2,1,0:T(8,128)} %param.10) | copy-start | bytes 3145732
  3.7 78.5 %copy-start.4 = (f32[16,256]{1,0:T(8,128)S(1)}, f32[16,256]{1,0:T(8,128)}, u32[]{:S(2)}) copy-start(f32[16,256]{1,0:T(8,128)} %constant.58.clone.factor) | copy-start | bytes 49156

commit v4 on v3

--- a/solution.py
+++ b/solution.py
@@ -102,14 +102,7 @@
     return ref[0], ref[1]
 
 
-def own_wave():
-    flip = 2 * (lax.axis_index("row") // (K // 2))
-    return jnp.bitwise_xor(lax.axis_index("col"), flip)
-
-
-def analysis_kernel(
-    fields, forward_x, plane, stored, phase, out, cells, weights, lines, square, slab, arrived
-):
+def analysis_kernel(fields, forward_x, plane, phase, out, cells, lines, square, arrived):
     table = pltpu.make_async_copy(forward_x, lines, arrived.at[C])
     table.start()
     copies = [
@@ -119,8 +112,6 @@
         copy.start()
     second = pltpu.make_async_copy(plane, square, arrived.at[C + 1])
     second.start()
-    third = pltpu.make_async_copy(stored.at[:, own_wave()], slab, arrived.at[C + 2])
-    third.start()
     table.wait()
 
     def channel(c):
@@ -128,8 +119,6 @@
         return cells[c]
 
     analyse(channel, phase[...], parts(lines), square, out, second.wait)
-    third.wait()
-    weights[...] = jnp.concatenate([slab[:, q, :] for q in range(K)], 1)
 
 
 def spread_kernel(pieces, out):
@@ -137,47 +126,26 @@
     out[...] = jnp.broadcast_to(total[None], out.shape)
 
 
-def forward_mix_kernel(pieces, weights, out):
-    total = jnp.sum(pieces[...], axis=0)
-    re = im = 0.0
-    for i in range(C):
-        a, b = total[i : i + 1], total[C + i : C + i + 1]
-        w, v = weights[i * C : (i + 1) * C], weights[C * C + i * C :][:C]
-        re = re + (a * w - b * v)
-        im = im + (a * v + b * w)
-    both = jnp.concatenate([re, im, total], 0)
-    out[...] = jnp.broadcast_to(both[None], out.shape)
-
-
-def backward_mix_kernel(pieces, weights, out):
-    total = jnp.sum(pieces[...], axis=0)
-    re = im = 0.0
+def forward_kernel(
+    modes, weights, fields, cotangent, point, bias, phase, forward_x, inverse_x, plane, up, out
+):
+    mixed_re, mixed_im = [], []
     for o in range(C):
-        a, b = total[o : o + 1], total[C + o : C + o + 1]
-        w, v = [
-            jnp.concatenate([weights[pl.ds((t * C + i) * C + o, 1), :] for i in range(C)], 0)
-            for t in range(2)
-        ]
-        re = re + (a * w + b * v)
-        im = im + (b * w - a * v)
-    both = jnp.concatenate([re, im, total], 0)
-    out[...] = jnp.broadcast_to(both[None], out.shape)
-
-
-def take(ref, row):
-    return ref[:, row, :]
-
-
-def take_mixed(ref):
-    return [
-        jnp.concatenate([take(ref, t * C + c) for c in range(C)], 0) for t in range(2)
-    ]
-
-
-def forward_kernel(
-    modes, fields, cotangent, point, bias, phase, forward_x, inverse_x, plane, up, out
-):
-    term = synthesise(*take_mixed(modes), phase[...], parts(inverse_x), parts(plane))
+        re = im = 0.0
+        for i in range(C):
+            a, b = modes[:, i, :], modes[:, C + i, :]
+            w, v = weights[0, i, o], weights[1, i, o]
+            re = re + (a * w - b * v)
+            im = im + (a * v + b * w)
+        mixed_re.append(re)
+        mixed_im.append(im)
+    term = synthesise(
+        jnp.concatenate(mixed_re, 0),
+        jnp.concatenate(mixed_im, 0),
+        phase[...],
+        parts(inverse_x),
+        parts(plane),
+    )
     for o in range(C):
         pre = term[o] + bias[o]
         for i in range(C):
@@ -189,15 +157,27 @@
     analyse(lambda c: up[c], phase[...], parts(forward_x), plane, out)
 
 
+def slabs(rows, start):
+    lane = lax.broadcasted_iota(jnp.int32, (8, 128), 1)
+    source = (8 - lane // K) % 8 * K + lane % K
+    half = jnp.take_along_axis(
+        rows[:, start : start + 128], source, axis=1, mode="promise_in_bounds"
+    )
+    return [
+        pltpu.roll(jnp.broadcast_to(half[k : k + 1], (8, 128)), 0, 1, stride=K, stride_axis=0)
+        for k in range(2 * C)
+    ]
+
+
 def backward_kernel(
     modes,
     back,
+    weights,
     up,
     point,
     phase,
     inverse_x,
     plane,
-    factor,
     grad_fields,
     grad_spectral,
     cells,
@@ -210,19 +190,40 @@
         copies.append(pltpu.make_async_copy(source, target, sent.at[len(copies)]))
         copies[-1].start()
 
-    scaled = [
-        [take(back, (2 + t) * C + o) * factor[...] for t in range(2)] for o in range(C)
-    ]
+    def one_wave(p):
+        factor = (1.0 if p == 0 else 2.0) / float(N) ** 3
+        first, second = modes[p], back[p] * factor
+        for half in range(2):
+            u, h = slabs(first, half * 128), slabs(second, half * 128)
+            for i in range(C):
+                for o in range(C):
+                    re = u[i] * h[o] + u[C + i] * h[C + o]
+                    im = u[i] * h[C + o] - u[C + i] * h[o]
+                    stored[0, i, o, p, half * 8 : half * 8 + 8, :] = re[:, :K]
+                    stored[1, i, o, p, half * 8 : half * 8 + 8, :] = im[:, :K]
+
+    for p in range(K):
+        one_wave(p)
+        if p % 4 == 3:
+            some = pl.ds(p - 3, 4)
+            send(stored.at[:, :, :, some], grad_spectral.at[:, :, :, some])
+    adjoint_re, adjoint_im = [], []
     for i in range(C):
-        u, w = take(modes, 2 * C + i), take(modes, 3 * C + i)
+        re = im = 0.0
         for o in range(C):
-            a, b = scaled[o]
-            for t, value in enumerate((u * a + w * b, u * b - w * a)):
-                for q in range(K):
-                    stored[t, i, o, :, q, :] = value[:, q * K : (q + 1) * K]
-        for t in range(2):
-            send(stored.at[t, i], grad_spectral.at[t, i])
-    term = synthesise(*take_mixed(back), phase[...], parts(inverse_x), parts(plane))
+            a, b = back[:, o, :], back[:, C + o, :]
+            w, v = weights[0, i, o], weights[1, i, o]
+            re = re + (a * w + b * v)
+            im = im + (b * w - a * v)
+        adjoint_re.append(re)
+        adjoint_im.append(im)
+    term = synthesise(
+        jnp.concatenate(adjoint_re, 0),
+        jnp.concatenate(adjoint_im, 0),
+        phase[...],
+        parts(inverse_x),
+        parts(plane),
+    )
     for i in range(C):
         total = term[i]
         for o in range(C):
@@ -277,50 +278,41 @@
     )
 
 
-def summed_modes(partial, weights, mix_kernel):
+def total_modes(partial):
     shape = (K, 2 * C, MODES)
     near_by, alike = groups()
     pieces = near(swap(partial, near_by))
     (pieces,) = call(spread_kernel, [near_out(shape)], [VMEM])(pieces)
     pieces = near(swap(pieces, alike))
-    shape = (K, 4 * C, MODES)
-    (pieces,) = call(mix_kernel, [near_out(shape)], [VMEM] * 2)(pieces, weights)
+    (pieces,) = call(spread_kernel, [near_out(shape)], [VMEM])(pieces)
     return near(swap(pieces, near_by))
 
 
 def per_device(fields, cotangent, spec_weights, point_weights, bias):
     forward_x, inverse_x, plane = [jnp.asarray(t) for t in tables()]
-    factor = np.where(np.arange(K) == 0, 1.0, 2.0) / float(N) ** 3
-    factor = jnp.asarray(np.broadcast_to(factor[:, None], (K, MODES)), jnp.float32)
     shape = fields.shape
     cells = (C, CELLS, N)
     phase = near(position_phase())
-    partial, fields, weights = call(
+    partial, fields = call(
         analysis_kernel,
-        [near_out((K, 2 * C, MODES)), near_out(cells), near_out((2 * C * C, MODES))],
-        [HBM] * 4 + [VMEM],
+        [near_out((K, 2 * C, MODES)), near_out(cells)],
+        [HBM] * 3 + [VMEM],
         [
             pltpu.VMEM((2, 2 * K, N), jnp.bfloat16),
             pltpu.VMEM((2, CELLS, 2 * MODES), jnp.bfloat16),
-            pltpu.VMEM((2 * C * C, K, K), jnp.float32),
-            pltpu.SemaphoreType.DMA((C + 3,)),
+            pltpu.SemaphoreType.DMA((C + 2,)),
         ],
-    )(
-        far(fields.reshape(cells)),
-        far(forward_x),
-        far(plane),
-        far(spec_weights.reshape(2 * C * C, K, K, K)),
-        phase,
-    )
-    weights = near(weights)
+    )(far(fields.reshape(cells)), far(forward_x), far(plane), phase)
     forward_x, inverse_x, plane = [near(v) for v in (forward_x, inverse_x, plane)]
-    modes = summed_modes(partial, weights, forward_mix_kernel)
+    weights = near(spec_weights.reshape(2, C, C, K, MODES))
+    modes = total_modes(partial)
     upstream, partial = call(
         forward_kernel,
         [near_out(cells), near_out((K, 2 * C, MODES))],
-        [VMEM] * 3 + [SMEM] * 2 + [VMEM] * 4,
+        [VMEM] * 4 + [SMEM] * 2 + [VMEM] * 4,
     )(
         modes,
+        weights,
         near(fields),
         near(cotangent.reshape(cells)),
         point_weights,
@@ -330,29 +322,20 @@
         inverse_x,
         plane,
     )
-    back = summed_modes(partial, weights, backward_mix_kernel)
+    back = total_modes(partial)
     grad_fields, grad_spectral = call(
         backward_kernel,
         [
             jax.ShapeDtypeStruct(cells, jnp.float32),
             jax.ShapeDtypeStruct((2, C, C, K, K, K), jnp.float32),
         ],
-        [VMEM] * 3 + [SMEM] + [VMEM] * 4,
+        [VMEM] * 4 + [SMEM] + [VMEM] * 3,
         [
             pltpu.VMEM(cells, jnp.float32),
             pltpu.VMEM((2, C, C, K, K, K), jnp.float32),
-            pltpu.SemaphoreType.DMA((3 * C,)),
+            pltpu.SemaphoreType.DMA((8,)),
         ],
-    )(
-        modes,
-        back,
-        near(upstream),
-        point_weights,
-        phase,
-        inverse_x,
-        plane,
-        near(factor),
-    )
+    )(modes, back, weights, near(upstream), point_weights, phase, inverse_x, plane)
     return grad_fields.reshape(shape), grad_spectral
 
 

time: 92.7 us -> 87.7 us (0.946)
  blocking collectives: 75.4 us -> 62.3 us
  starting transfers between devices: 0 us -> 5.36 us
  Pallas kernels: 16.1 us -> 12.6 us
  local copies, waits for them, and re-layouts: 0.04 us -> 3.52 us
  waiting for transfers between devices: 0 us -> 2.7 us
    all_to_all x6 -> x5, blocking collectives: 75.4 us -> 62.3 us  [swap(): lax.all_to_all(pieces, ('row', 'col'), 0, 0, tiled=True, axis_index_group...]
    all_to_all x0 -> x1, starting transfers between devices: none -> 5.36 us  [swap(): lax.all_to_all(pieces, ('row', 'col'), 0, 0, tiled=True, axis_index_group...]
    pallas_call x1, Pallas kernels: 10.1 us -> 6.2 us  [per_device(): call(backward_kernel, [jax.ShapeDtypeStruct(cells, jnp.float32), jax.Shap...]
    reshape x0 -> x1, local copies, waits for them, and re-layouts: none -> 3.49 us  [per_device(): weights = near(spec_weights.reshape(2, C, C, K, MODES))]
    all_to_all x0 -> x1, waiting for transfers between devices: none -> 2.7 us  [swap(): lax.all_to_all(pieces, ('row', 'col'), 0, 0, tiled=True, axis_index_group...]
  transfers between devices with their start and end apart: 0 -> 1, of which waited for: 0 -> 1; matrix products, arithmetic and copies ran while one was open for 0% -> 4% of each run, Pallas kernels for 0% -> 0%
where the time goes in v4:
time: 87.7 us; the launch traced here: 87.3 us
  blocking collectives  62.3 us (71%)
  Pallas kernels  12.6 us (14%)
  starting transfers between devices  5.36 us (6%)
  local copies, waits for them, and re-layouts  3.52 us (4%)
  waiting for transfers between devices  2.7 us (3%)
    all_to_all x5, blocking collectives, swap(): lax.all_to_all(pieces, ('row', 'col'), 0, 0, tiled=True, axis_index_group...  62.3 us
    pallas_call x1, Pallas kernels, per_device(): call(backward_kernel, [jax.ShapeDtypeStruct(cells, jnp.float32), jax.Shap...  6.2 us
    all_to_all x1, starting transfers between devices, swap(): lax.all_to_all(pieces, ('row', 'col'), 0, 0, tiled=True, axis_index_group...  5.36 us
    reshape x1, local copies, waits for them, and re-layouts, per_device(): weights = near(spec_weights.reshape(2, C, C, K, MODES))  3.49 us
    pallas_call x1, Pallas kernels, per_device(): call(forward_kernel, [near_out(cells), near_out((K, 2 * C, MODES))], [VME...  2.93 us
    pallas_call x1, Pallas kernels, per_device(): call(analysis_kernel, [near_out((K, 2 * C, MODES)), near_out(cells)], [HB...  2.75 us
    all_to_all x1, waiting for transfers between devices, swap(): lax.all_to_all(pieces, ('row', 'col'), 0, 0, tiled=True, axis_index_group...  2.7 us
  transfers between devices with their start and end apart: 1, of which 1 were waited for; matrix products, arithmetic and copies ran while one was open for 4% of the time, Pallas kernels for 0%

profile of v4, /device:TPU:1, one launch (start us, length us, event | category | flops | bytes accessed | tf_op | source)
XLA Modules:
  0.0 87.3 jit_solution(4517057300329444623)
XLA Ops:
  0.6 0.0 copy-start
  0.6 0.0 copy-start.3
  0.7 0.0 copy-start.2
  0.7 0.0 copy-start.4
  0.7 0.0 copy-start.5
  0.7 0.0 copy-start.1
  0.7 0.1 sine_negate_fusion
  0.8 2.7 %shard_map.95 = (f32[16,8,256]{2,1,0:T(8,128)S(1)}, f32[4,256,256]{2,1,0:T(8,128)S(1)}) custom-call(f32[4,256,256]{2,1,0:T(8,128)} %bitcast.6, bf16[2,32,256]{2,1,0:T(8,128)(2,1)} %constant.53.clone.forward_x, bf16[2,256,512]{2,1,0:T(8,128)(2,1)} %constant.55.clone.plane, f32[2,256]{1,0:T(2,128)S(1)} %pad_maximum_fusion.phase), custom_call_target="tpu_custom_call" | custom-call | tf_op jit(solution)/shard_map/pallas_call | solution.py:296
  3.5 12.8 %all_to_all.30.pieces = f32[16,8,256]{2,1,0:T(8,128)S(1)} all-to-all(f32[16,8,256]{2,1,0:T(8,128)S(1)} %get-tuple-element.8), channel_id=1, replica_groups={{0,1,2,3,4,5,6,7,8,9,10,11,12,13,14,15},{16,17,18,19,20,21,22,23,24,25,..., dimensions={0} | all-to-all | bytes 262144 | tf_op jit(solution)/shard_map/all_to_all | solution.py:264
  16.3 18.3 %all_to_all.31.pieces = f32[16,8,256]{2,1,0:T(8,128)S(1)} all-to-all(f32[16,8,256]{2,1,0:T(8,128)S(1)} %shard_map.96), channel_id=1, replica_groups={{0,16,32,48,64,80,96,112,130,146,162,178,194,210,226,242},{1,17,33,49,6..., dimensions={0} | all-to-all | bytes 262144 | tf_op jit(solution)/shard_map/all_to_all | solution.py:264
  34.7 0.7 shard_map.97
  35.3 5.4 %all-to-all-start.2 = ((f32[16,8,256]{2,1,0:T(8,128)}), f32[16,8,256]{2,1,0:T(8,128)S(1)}, u32[]{:S(2)}, u32[]{:S(2)}) async-start(f32[16,8,256]{2,1,0:T(8,128)} %shard_map.97), calls=%async_computation.2 | async-start | bytes 262144 | tf_op jit(solution)/shard_map/all_to_all | solution.py:264
  40.7 3.5 %reshape.124.weights = f32[2,4,4,16,256]{4,3,2,1,0:T(8,128)S(1)} reshape(f32[2,4,4,16,16,16]{5,4,3,2,1,0:T(8,128)} %param.10) | data formatting | bytes 1048576 | tf_op jit(solution)/shard_map/reshape | solution.py:307
  44.2 2.7 %all-to-all-done.2.modes = f32[16,8,256]{2,1,0:T(8,128)S(1)} async-done(((f32[16,8,256]{2,1,0:T(8,128)}), f32[16,8,256]{2,1,0:T(8,128)S(1)}, u32[]{:S(2)}, u32[]{:S(2)}) %all-to-all-start.2) | async-done | bytes 131104 | tf_op jit(solution)/shard_map/all_to_all | solution.py:264
  46.9 0.0 copy-done
  46.9 0.0 copy-done.3
  46.9 0.0 copy-done.2
  46.9 0.0 copy-done.4
  46.9 0.0 copy-done.5
  46.9 0.0 copy-done.1
  47.0 2.9 %shard_map.98 = (f32[4,256,256]{2,1,0:T(8,128)S(1)}, f32[16,8,256]{2,1,0:T(8,128)S(1)}) custom-call(f32[16,8,256]{2,1,0:T(8,128)S(1)} %all-to-all-done.2.modes, f32[2,4,4,16,256]{4,3,2,1,0:T(8,128)S(1)} %reshape.124.weights, f32[4,256,256]{2,1,0:T(8,128)S(1)} %get-tuple-element.9.fields, f32[4,256,256]{2,1,0:T(8,128)S(1)} %bitcast.5, f32[4,4]{1,0:T(4,128)S(1)} %copy-done.4, ...), custom_call_target="tpu_custom_call" | custom-call | tf_op jit(solution)/shard_map/pallas_call | solution.py:309
  49.9 9.1 %all_to_all.32.pieces = f32[16,8,256]{2,1,0:T(8,128)S(1)} all-to-all(f32[16,8,256]{2,1,0:T(8,128)S(1)} %get-tuple-element.10), channel_id=1, replica_groups={{0,1,2,3,4,5,6,7,8,9,10,11,12,13,14,15},{16,17,18,19,20,21,22,23,24,25,..., dimensions={0} | all-to-all | bytes 262144 | tf_op jit(solution)/shard_map/all_to_all | solution.py:264
  59.0 11.4 %all_to_all.33.pieces = f32[16,8,256]{2,1,0:T(8,128)S(1)} all-to-all(f32[16,8,256]{2,1,0:T(8,128)S(1)} %shard_map.99), channel_id=1, replica_groups={{0,16,32,48,64,80,96,112,130,146,162,178,194,210,226,242},{1,17,33,49,6..., dimensions={0} | all-to-all | bytes 262144 | tf_op jit(solution)/shard_map/all_to_all | solution.py:264
  70.5 10.7 %all_to_all.34.back = f32[16,8,256]{2,1,0:T(8,128)S(1)} all-to-all(f32[16,8,256]{2,1,0:T(8,128)S(1)} %shard_map.100), channel_id=1, replica_groups={{0,1,2,3,4,5,6,7,8,9,10,11,12,13,14,15},{16,17,18,19,20,21,22,23,24,25,..., dimensions={0} | all-to-all | bytes 262144 | tf_op jit(solution)/shard_map/all_to_all | solution.py:264
  81.1 6.2 %shard_map.101 = (f32[4,256,256]{2,1,0:T(8,128)}, f32[2,4,4,16,16,16]{5,4,3,2,1,0:T(8,128)}) custom-call(f32[16,8,256]{2,1,0:T(8,128)S(1)} %all-to-all-done.2.modes, f32[16,8,256]{2,1,0:T(8,128)S(1)} %all_to_all.34.back, f32[2,4,4,16,256]{4,3,2,1,0:T(8,128)S(1)} %reshape.124.weights, f32[4,256,256]{2,1,0:T(8,128)S(1)} %get-tuple-element.11.up, ...), custom_call_target="tpu_custom_call" | custom-call | tf_op jit(solution)/shard_map/pallas_call | solution.py:326
  (4 shorter events, 0.1 us)
Async XLA Ops:
  0.6 46.3 %copy-start = (bf16[2,256,512]{2,1,0:T(8,128)(2,1)S(1)}, bf16[2,256,512]{2,1,0:T(8,128)(2,1)}, u32[]{:S(2)}) copy-start(bf16[2,256,512]{2,1,0:T(8,128)(2,1)} %constant.55.clone.plane) | copy-start | bytes 1572868
  0.6 46.3 %copy-start.3 = (bf16[2,32,256]{2,1,0:T(8,128)(2,1)S(1)}, bf16[2,32,256]{2,1,0:T(8,128)(2,1)}, u32[]{:S(2)}) copy-start(bf16[2,32,256]{2,1,0:T(8,128)(2,1)} %constant.53.clone.forward_x) | copy-start | bytes 98308
  0.7 46.3 %copy-start.2 = (bf16[2,32,256]{2,1,0:T(8,128)(2,1)S(1)}, bf16[2,32,256]{2,1,0:T(8,128)(2,1)}, u32[]{:S(2)}) copy-start(bf16[2,32,256]{2,1,0:T(8,128)(2,1)} %constant.54.clone.inverse_x) | copy-start | bytes 98308
  0.7 46.3 %copy-start.4 = (f32[4,4]{1,0:T(4,128)S(1)}, f32[4,4]{1,0:T(4,128)}, u32[]{:S(2)}) copy-start(f32[4,4]{1,0:T(4,128)} %point.3) | copy-start | bytes 196
  0.7 46.3 %copy-start.5 = (f32[4]{0:T(128)S(1)}, f32[4]{0:T(128)}, u32[]{:S(2)}) copy-start(f32[4]{0:T(128)} %bias.1) | copy-start | bytes 52
  0.7 46.3 %copy-start.1 = (f32[1,4,16,16,256]{4,3,2,1,0:T(8,128)S(1)}, f32[1,4,16,16,256]{4,3,2,1,0:T(8,128)}, u32[]{:S(2)}) copy-start(f32[1,4,16,16,256]{4,3,2,1,0:T(8,128)} %param.9) | copy-start | bytes 3145732
  35.3 11.6 %all-to-all-start.2 = ((f32[16,8,256]{2,1,0:T(8,128)}), f32[16,8,256]{2,1,0:T(8,128)S(1)}, u32[]{:S(2)}, u32[]{:S(2)}) async-start(f32[16,8,256]{2,1,0:T(8,128)} %shard_map.97), calls=%async_computation.2 | async-start | bytes 262144 | tf_op jit(solution)/shard_map/all_to_all | solution.py:264

commit v5 on v4

--- a/solution.py
+++ b/solution.py
@@ -157,12 +157,26 @@
     analyse(lambda c: up[c], phase[...], parts(forward_x), plane, out)
 
 
+def turned(modes):
+    shape = (MODES, MODES)
+    source, target = [lax.broadcasted_iota(jnp.int32, shape, axis) for axis in range(2)]
+    wanted = target // 128 * 128 + (8 - target % 128 // K) % 8 * K + target % K
+    order = (source == wanted).astype(jnp.bfloat16)
+    high, rest = split_off(modes.reshape(ROWS, MODES))
+    middle, rest = split_off(rest)
+    total = 0.0
+    for part in (rest.astype(jnp.bfloat16), middle, high):
+        total = total + jnp.dot(part, order, preferred_element_type=jnp.float32)
+    return total
+
+
+def split_off(value):
+    high = value.astype(jnp.bfloat16)
+    return high, value - high.astype(jnp.float32)
+
+
 def slabs(rows, start):
-    lane = lax.broadcasted_iota(jnp.int32, (8, 128), 1)
-    source = (8 - lane // K) % 8 * K + lane % K
-    half = jnp.take_along_axis(
-        rows[:, start : start + 128], source, axis=1, mode="promise_in_bounds"
-    )
+    half = rows[:, start : start + 128]
     return [
         pltpu.roll(jnp.broadcast_to(half[k : k + 1], (8, 128)), 0, 1, stride=K, stride_axis=0)
         for k in range(2 * C)
@@ -192,7 +206,8 @@
 
     def one_wave(p):
         factor = (1.0 if p == 0 else 2.0) / float(N) ** 3
-        first, second = modes[p], back[p] * factor
+        first, second = [v[p * 2 * C : (p + 1) * 2 * C] for v in (modes_turned, back_turned)]
+        second = second * factor
         for half in range(2):
             u, h = slabs(first, half * 128), slabs(second, half * 128)
             for i in range(C):
@@ -202,6 +217,7 @@
                     stored[0, i, o, p, half * 8 : half * 8 + 8, :] = re[:, :K]
                     stored[1, i, o, p, half * 8 : half * 8 + 8, :] = im[:, :K]
 
+    modes_turned, back_turned = turned(modes[...]), turned(back[...])
     for p in range(K):
         one_wave(p)
         if p % 4 == 3:

time: 87.7 us -> 85.5 us (0.975)
  Pallas kernels: 12.6 us -> 10.4 us
    pallas_call x1, Pallas kernels: 6.2 us -> 3.96 us  [per_device(): call(backward_kernel, [jax.ShapeDtypeStruct(cells, jnp.float32), jax.Shap...]
where the time goes in v5:
time: 85.5 us; the launch traced here: 85.1 us
  blocking collectives  62.3 us (73%)
  Pallas kernels  10.4 us (12%)
  starting transfers between devices  5.36 us (6%)
  local copies, waits for them, and re-layouts  3.52 us (4%)
  waiting for transfers between devices  2.7 us (3%)
    all_to_all x5, blocking collectives, swap(): lax.all_to_all(pieces, ('row', 'col'), 0, 0, tiled=True, axis_index_group...  62.3 us
    all_to_all x1, starting transfers between devices, swap(): lax.all_to_all(pieces, ('row', 'col'), 0, 0, tiled=True, axis_index_group...  5.36 us
    pallas_call x1, Pallas kernels, per_device(): call(backward_kernel, [jax.ShapeDtypeStruct(cells, jnp.float32), jax.Shap...  3.96 us
    reshape x1, local copies, waits for them, and re-layouts, per_device(): weights = near(spec_weights.reshape(2, C, C, K, MODES))  3.49 us
    pallas_call x1, Pallas kernels, per_device(): call(forward_kernel, [near_out(cells), near_out((K, 2 * C, MODES))], [VME...  2.93 us
    pallas_call x1, Pallas kernels, per_device(): call(analysis_kernel, [near_out((K, 2 * C, MODES)), near_out(cells)], [HB...  2.75 us
    all_to_all x1, waiting for transfers between devices, swap(): lax.all_to_all(pieces, ('row', 'col'), 0, 0, tiled=True, axis_index_group...  2.7 us
  transfers between devices with their start and end apart: 1, of which 1 were waited for; matrix products, arithmetic and copies ran while one was open for 4% of the time, Pallas kernels for 0%

profile of v5, /device:TPU:1, one launch (start us, length us, event | category | flops | bytes accessed | tf_op | source)
XLA Modules:
  0.0 85.1 jit_solution(1171951686980236681)
XLA Ops:
  0.6 0.0 copy-start
  0.6 0.0 copy-start.3
  0.7 0.0 copy-start.2
  0.7 0.0 copy-start.4
  0.7 0.0 copy-start.5
  0.7 0.0 copy-start.1
  0.7 0.1 sine_negate_fusion
  0.8 2.7 %shard_map.95 = (f32[16,8,256]{2,1,0:T(8,128)S(1)}, f32[4,256,256]{2,1,0:T(8,128)S(1)}) custom-call(f32[4,256,256]{2,1,0:T(8,128)} %bitcast.6, bf16[2,32,256]{2,1,0:T(8,128)(2,1)} %constant.53.clone.forward_x, bf16[2,256,512]{2,1,0:T(8,128)(2,1)} %constant.55.clone.plane, f32[2,256]{1,0:T(2,128)S(1)} %pad_maximum_fusion.phase), custom_call_target="tpu_custom_call" | custom-call | tf_op jit(solution)/shard_map/pallas_call | solution.py:312
  3.5 12.8 %all_to_all.30.pieces = f32[16,8,256]{2,1,0:T(8,128)S(1)} all-to-all(f32[16,8,256]{2,1,0:T(8,128)S(1)} %get-tuple-element.8), channel_id=1, replica_groups={{0,1,2,3,4,5,6,7,8,9,10,11,12,13,14,15},{16,17,18,19,20,21,22,23,24,25,..., dimensions={0} | all-to-all | bytes 262144 | tf_op jit(solution)/shard_map/all_to_all | solution.py:280
  16.3 18.3 %all_to_all.31.pieces = f32[16,8,256]{2,1,0:T(8,128)S(1)} all-to-all(f32[16,8,256]{2,1,0:T(8,128)S(1)} %shard_map.96), channel_id=1, replica_groups={{0,16,32,48,64,80,96,112,130,146,162,178,194,210,226,242},{1,17,33,49,6..., dimensions={0} | all-to-all | bytes 262144 | tf_op jit(solution)/shard_map/all_to_all | solution.py:280
  34.7 0.7 shard_map.97
  35.3 5.4 %all-to-all-start.2 = ((f32[16,8,256]{2,1,0:T(8,128)}), f32[16,8,256]{2,1,0:T(8,128)S(1)}, u32[]{:S(2)}, u32[]{:S(2)}) async-start(f32[16,8,256]{2,1,0:T(8,128)} %shard_map.97), calls=%async_computation.2 | async-start | bytes 262144 | tf_op jit(solution)/shard_map/all_to_all | solution.py:280
  40.7 3.5 %reshape.124.weights = f32[2,4,4,16,256]{4,3,2,1,0:T(8,128)S(1)} reshape(f32[2,4,4,16,16,16]{5,4,3,2,1,0:T(8,128)} %param.10) | data formatting | bytes 1048576 | tf_op jit(solution)/shard_map/reshape | solution.py:323
  44.2 2.7 %all-to-all-done.2.modes = f32[16,8,256]{2,1,0:T(8,128)S(1)} async-done(((f32[16,8,256]{2,1,0:T(8,128)}), f32[16,8,256]{2,1,0:T(8,128)S(1)}, u32[]{:S(2)}, u32[]{:S(2)}) %all-to-all-start.2) | async-done | bytes 131104 | tf_op jit(solution)/shard_map/all_to_all | solution.py:280
  46.9 0.0 copy-done
  46.9 0.0 copy-done.3
  46.9 0.0 copy-done.2
  46.9 0.0 copy-done.4
  46.9 0.0 copy-done.5
  46.9 0.0 copy-done.1
  47.0 2.9 %shard_map.98 = (f32[4,256,256]{2,1,0:T(8,128)S(1)}, f32[16,8,256]{2,1,0:T(8,128)S(1)}) custom-call(f32[16,8,256]{2,1,0:T(8,128)S(1)} %all-to-all-done.2.modes, f32[2,4,4,16,256]{4,3,2,1,0:T(8,128)S(1)} %reshape.124.weights, f32[4,256,256]{2,1,0:T(8,128)S(1)} %get-tuple-element.9.fields, f32[4,256,256]{2,1,0:T(8,128)S(1)} %bitcast.5, f32[4,4]{1,0:T(4,128)S(1)} %copy-done.4, ...), custom_call_target="tpu_custom_call" | custom-call | tf_op jit(solution)/shard_map/pallas_call | solution.py:325
  49.9 9.1 %all_to_all.32.pieces = f32[16,8,256]{2,1,0:T(8,128)S(1)} all-to-all(f32[16,8,256]{2,1,0:T(8,128)S(1)} %get-tuple-element.10), channel_id=1, replica_groups={{0,1,2,3,4,5,6,7,8,9,10,11,12,13,14,15},{16,17,18,19,20,21,22,23,24,25,..., dimensions={0} | all-to-all | bytes 262144 | tf_op jit(solution)/shard_map/all_to_all | solution.py:280
  59.0 11.4 %all_to_all.33.pieces = f32[16,8,256]{2,1,0:T(8,128)S(1)} all-to-all(f32[16,8,256]{2,1,0:T(8,128)S(1)} %shard_map.99), channel_id=1, replica_groups={{0,16,32,48,64,80,96,112,130,146,162,178,194,210,226,242},{1,17,33,49,6..., dimensions={0} | all-to-all | bytes 262144 | tf_op jit(solution)/shard_map/all_to_all | solution.py:280
  70.5 10.7 %all_to_all.34.back = f32[16,8,256]{2,1,0:T(8,128)S(1)} all-to-all(f32[16,8,256]{2,1,0:T(8,128)S(1)} %shard_map.100), channel_id=1, replica_groups={{0,1,2,3,4,5,6,7,8,9,10,11,12,13,14,15},{16,17,18,19,20,21,22,23,24,25,..., dimensions={0} | all-to-all | bytes 262144 | tf_op jit(solution)/shard_map/all_to_all | solution.py:280
  81.1 4.0 %shard_map.101 = (f32[4,256,256]{2,1,0:T(8,128)}, f32[2,4,4,16,16,16]{5,4,3,2,1,0:T(8,128)}) custom-call(f32[16,8,256]{2,1,0:T(8,128)S(1)} %all-to-all-done.2.modes, f32[16,8,256]{2,1,0:T(8,128)S(1)} %all_to_all.34.back, f32[2,4,4,16,256]{4,3,2,1,0:T(8,128)S(1)} %reshape.124.weights, f32[4,256,256]{2,1,0:T(8,128)S(1)} %get-tuple-element.11.up, ...), custom_call_target="tpu_custom_call" | custom-call | tf_op jit(solution)/shard_map/pallas_call | solution.py:342
  (4 shorter events, 0.1 us)
Async XLA Ops:
  0.6 46.3 %copy-start = (bf16[2,256,512]{2,1,0:T(8,128)(2,1)S(1)}, bf16[2,256,512]{2,1,0:T(8,128)(2,1)}, u32[]{:S(2)}) copy-start(bf16[2,256,512]{2,1,0:T(8,128)(2,1)} %constant.55.clone.plane) | copy-start | bytes 1572868
  0.6 46.3 %copy-start.3 = (bf16[2,32,256]{2,1,0:T(8,128)(2,1)S(1)}, bf16[2,32,256]{2,1,0:T(8,128)(2,1)}, u32[]{:S(2)}) copy-start(bf16[2,32,256]{2,1,0:T(8,128)(2,1)} %constant.53.clone.forward_x) | copy-start | bytes 98308
  0.7 46.3 %copy-start.2 = (bf16[2,32,256]{2,1,0:T(8,128)(2,1)S(1)}, bf16[2,32,256]{2,1,0:T(8,128)(2,1)}, u32[]{:S(2)}) copy-start(bf16[2,32,256]{2,1,0:T(8,128)(2,1)} %constant.54.clone.inverse_x) | copy-start | bytes 98308
  0.7 46.3 %copy-start.4 = (f32[4,4]{1,0:T(4,128)S(1)}, f32[4,4]{1,0:T(4,128)}, u32[]{:S(2)}) copy-start(f32[4,4]{1,0:T(4,128)} %point.3) | copy-start | bytes 196
  0.7 46.3 %copy-start.5 = (f32[4]{0:T(128)S(1)}, f32[4]{0:T(128)}, u32[]{:S(2)}) copy-start(f32[4]{0:T(128)} %bias.1) | copy-start | bytes 52
  0.7 46.3 %copy-start.1 = (f32[1,4,16,16,256]{4,3,2,1,0:T(8,128)S(1)}, f32[1,4,16,16,256]{4,3,2,1,0:T(8,128)}, u32[]{:S(2)}) copy-start(f32[1,4,16,16,256]{4,3,2,1,0:T(8,128)} %param.9) | copy-start | bytes 3145732
  35.3 11.6 %all-to-all-start.2 = ((f32[16,8,256]{2,1,0:T(8,128)}), f32[16,8,256]{2,1,0:T(8,128)S(1)}, u32[]{:S(2)}, u32[]{:S(2)}) async-start(f32[16,8,256]{2,1,0:T(8,128)} %shard_map.97), calls=%async_computation.2 | async-start | bytes 262144 | tf_op jit(solution)/shard_map/all_to_all | solution.py:280

commit v6 on v5

--- a/solution.py
+++ b/solution.py
@@ -16,6 +16,7 @@
 CELLS = LOCAL * LOCAL
 MODES = K * K
 ROWS = 2 * C * K
+HALF_ROOT = math.sqrt(0.5)
 
 VMEM = pl.BlockSpec(memory_space=pltpu.VMEM)
 HBM = pl.BlockSpec(memory_space=pltpu.HBM)
@@ -30,6 +31,11 @@
     high = np.asarray(table, jnp.bfloat16)
     low = np.asarray(table - np.asarray(high, np.float64), jnp.bfloat16)
     return np.stack([high, low])
+
+
+def joined(table):
+    high, low = two_parts(table)
+    return np.concatenate([high, high, low], 0)
 
 
 def signed_waves():
@@ -46,7 +52,8 @@
     both = one[:, None, :, None] + one[None, :, None, :]
     angle = 2.0 * np.pi / N * (both.reshape(CELLS, MODES) % N)
     plane = np.concatenate([np.cos(angle), -np.sin(angle)], 1)
-    return two_parts(forward_x), two_parts(inverse_x), two_parts(plane)
+    scaled_x, inverse_x = joined(inverse_x * np.sqrt(0.5)), joined(inverse_x * 0.5)
+    return two_parts(forward_x), scaled_x, inverse_x, two_parts(plane)
 
 
 def split(value):
@@ -55,11 +62,17 @@
     return high, low
 
 
+def dot_of(dims):
+    return functools.partial(
+        lax.dot_general, dimension_numbers=dims, preferred_element_type=jnp.float32
+    )
+
+
 def dot3(left, right, dims):
-    dot = functools.partial(
-        lax.dot_general, dimension_numbers=dims, preferred_element_type=jnp.float32
-    )
-    return dot(left[0], right[0]) + (dot(left[0], right[1]) + dot(left[1], right[0]))
+    dot = dot_of(dims)
+    rows = left[0].shape[0]
+    both = dot(jnp.concatenate(left, 0), right[0])
+    return both[:rows] + (dot(left[0], right[1]) + both[rows:])
 
 
 def analyse(channel, phase, forward_x, plane, out, ready=None):
@@ -94,7 +107,8 @@
     out = []
     for c in range(C):
         pair = jnp.concatenate([lines[c * K : (c + 1) * K], lines[half + c * K :][:K]], 0)
-        out.append(dot3(split(pair), inverse_x, TN))
+        high, low = split(pair)
+        out.append(dot_of(TN)(jnp.concatenate([high, low, high], 0), inverse_x))
     return out
 
 
@@ -102,7 +116,7 @@
     return ref[0], ref[1]
 
 
-def analysis_kernel(fields, forward_x, plane, phase, out, cells, lines, square, arrived):
+def analysis_kernel(fields, forward_x, plane, phase, out, lines, square, cells, arrived):
     table = pltpu.make_async_copy(forward_x, lines, arrived.at[C])
     table.start()
     copies = [
@@ -126,8 +140,25 @@
     out[...] = jnp.broadcast_to(total[None], out.shape)
 
 
+def local_kernel(fields, upper, point, bias, out, cotangent, cells, arrived):
+    copies = [
+        pltpu.make_async_copy(fields.at[c], cells.at[c], arrived.at[c]) for c in range(C)
+    ]
+    copies.append(pltpu.make_async_copy(upper, cotangent, arrived.at[C]))
+    for copy in copies:
+        copy.start()
+    for copy in copies[:C]:
+        copy.wait()
+    for o in range(C):
+        total = bias[o] * HALF_ROOT
+        for i in range(C):
+            total = total + (point[i, o] * HALF_ROOT) * cells[i]
+        out[o] = total
+    copies[C].wait()
+
+
 def forward_kernel(
-    modes, weights, fields, cotangent, point, bias, phase, forward_x, inverse_x, plane, up, out
+    modes, weights, local, cotangent, phase, forward_x, scaled_x, plane, up, out
 ):
     mixed_re, mixed_im = [], []
     for o in range(C):
@@ -143,17 +174,13 @@
         jnp.concatenate(mixed_re, 0),
         jnp.concatenate(mixed_im, 0),
         phase[...],
-        parts(inverse_x),
+        scaled_x[...],
         parts(plane),
     )
     for o in range(C):
-        pre = term[o] + bias[o]
-        for i in range(C):
-            pre = pre + point[i, o] * fields[i]
-        slope = 0.5 * (1.0 + lax.erf(pre * math.sqrt(0.5))) + pre * jnp.exp(
-            -0.5 * pre * pre
-        ) * (1.0 / math.sqrt(2.0 * math.pi))
-        up[o] = cotangent[o] * slope
+        s = term[o] + local[o]
+        bell = jnp.exp2(s * s * (-1.0 / math.log(2.0)))
+        up[o] = cotangent[o] * ((1.0 + lax.erf(s)) + s * (2.0 / math.sqrt(math.pi)) * bell)
     analyse(lambda c: up[c], phase[...], parts(forward_x), plane, out)
 
 
@@ -205,7 +232,7 @@
         copies[-1].start()
 
     def one_wave(p):
-        factor = (1.0 if p == 0 else 2.0) / float(N) ** 3
+        factor = (0.5 if p == 0 else 1.0) / float(N) ** 3
         first, second = [v[p * 2 * C : (p + 1) * 2 * C] for v in (modes_turned, back_turned)]
         second = second * factor
         for half in range(2):
@@ -237,13 +264,13 @@
         jnp.concatenate(adjoint_re, 0),
         jnp.concatenate(adjoint_im, 0),
         phase[...],
-        parts(inverse_x),
+        inverse_x[...],
         parts(plane),
     )
     for i in range(C):
         total = term[i]
         for o in range(C):
-            total = total + point[i, o] * up[o]
+            total = total + (point[i, o] * 0.5) * up[o]
         cells[i] = total
         send(cells.at[i], grad_fields.at[i])
     for copy in copies:
@@ -265,8 +292,8 @@
     return pltpu.with_memory_space_constraint(value, pltpu.HBM)
 
 
-def near_out(shape):
-    return pltpu.VMEM(shape, jnp.float32)
+def near_out(shape, dtype=jnp.float32):
+    return pltpu.VMEM(shape, dtype)
 
 
 def groups():
@@ -305,39 +332,36 @@
 
 
 def per_device(fields, cotangent, spec_weights, point_weights, bias):
-    forward_x, inverse_x, plane = [jnp.asarray(t) for t in tables()]
+    forward_x, scaled_x, inverse_x, plane = [jnp.asarray(t) for t in tables()]
     shape = fields.shape
     cells = (C, CELLS, N)
     phase = near(position_phase())
-    partial, fields = call(
+    partial, forward_x, plane = call(
         analysis_kernel,
-        [near_out((K, 2 * C, MODES)), near_out(cells)],
+        [
+            near_out((K, 2 * C, MODES)),
+            near_out(forward_x.shape, jnp.bfloat16),
+            near_out(plane.shape, jnp.bfloat16),
+        ],
         [HBM] * 3 + [VMEM],
-        [
-            pltpu.VMEM((2, 2 * K, N), jnp.bfloat16),
-            pltpu.VMEM((2, CELLS, 2 * MODES), jnp.bfloat16),
-            pltpu.SemaphoreType.DMA((C + 2,)),
-        ],
+        [pltpu.VMEM(cells, jnp.float32), pltpu.SemaphoreType.DMA((C + 2,))],
     )(far(fields.reshape(cells)), far(forward_x), far(plane), phase)
-    forward_x, inverse_x, plane = [near(v) for v in (forward_x, inverse_x, plane)]
+    forward_x, scaled_x, inverse_x, plane = [
+        near(v) for v in (forward_x, scaled_x, inverse_x, plane)
+    ]
     weights = near(spec_weights.reshape(2, C, C, K, MODES))
     modes = total_modes(partial)
+    local, cotangent = call(
+        local_kernel,
+        [near_out(cells)] * 2,
+        [HBM] * 2 + [SMEM] * 2,
+        [pltpu.VMEM(cells, jnp.float32), pltpu.SemaphoreType.DMA((C + 1,))],
+    )(far(fields.reshape(cells)), far(cotangent.reshape(cells)), point_weights, bias)
     upstream, partial = call(
         forward_kernel,
         [near_out(cells), near_out((K, 2 * C, MODES))],
-        [VMEM] * 4 + [SMEM] * 2 + [VMEM] * 4,
-    )(
-        modes,
-        weights,
-        near(fields),
-        near(cotangent.reshape(cells)),
-        point_weights,
-        bias,
-        phase,
-        forward_x,
-        inverse_x,
-        plane,
-    )
+        [VMEM] * 8,
+    )(modes, weights, near(local), near(cotangent), phase, forward_x, scaled_x, plane)
     back = total_modes(partial)
     grad_fields, grad_spectral = call(
         backward_kernel,

time: 85.5 us -> 85.7 us (level)
  blocking collectives: 62.3 us -> 64.6 us
  waiting for transfers between devices: 2.7 us -> 0.5 us
    all_to_all x5, blocking collectives: 62.3 us -> 64.6 us  [swap(): lax.all_to_all(pieces, ('row', 'col'), 0, 0, tiled=True, axis_index_group...]
    all_to_all x1, waiting for transfers between devices: 2.7 us -> 0.5 us  [swap(): lax.all_to_all(pieces, ('row', 'col'), 0, 0, tiled=True, axis_index_group...]
    pallas_call x1 -> x2, Pallas kernels: 2.75 us -> 4.55 us  [the longest x1 2.38 us: per_device(): call(analysis_kernel, [near_out((K, 2 * C, MODES)), near_out(forward_x.sh...]
    pallas_call x1, Pallas kernels: 2.93 us -> 1.65 us  [per_device(): call(forward_kernel, [near_out(cells), near_out((K, 2 * C, MODES))], [VME...]
  transfers between devices with their start and end apart: 1 -> 1, of which waited for: 1 -> 1; matrix products, arithmetic and copies ran while one was open for 4% -> 4% of each run, Pallas kernels for 0% -> 3%
where the time goes in v6:
time: 85.7 us; the launch traced here: 85.2 us
  blocking collectives  64.6 us (75%)
  Pallas kernels  10.5 us (12%)
  starting transfers between devices  5.36 us (6%)
  local copies, waits for them, and re-layouts  3.51 us (4%)
    all_to_all x5, blocking collectives, swap(): lax.all_to_all(pieces, ('row', 'col'), 0, 0, tiled=True, axis_index_group...  64.6 us
    all_to_all x1, starting transfers between devices, swap(): lax.all_to_all(pieces, ('row', 'col'), 0, 0, tiled=True, axis_index_group...  5.36 us
    pallas_call x1, Pallas kernels, per_device(): call(backward_kernel, [jax.ShapeDtypeStruct(cells, jnp.float32), jax.Shap...  3.54 us
    reshape x1, local copies, waits for them, and re-layouts, per_device(): weights = near(spec_weights.reshape(2, C, C, K, MODES))  3.49 us
    pallas_call x1, Pallas kernels, per_device(): call(analysis_kernel, [near_out((K, 2 * C, MODES)), near_out(forward_x.sh...  2.38 us
    pallas_call x1, Pallas kernels, per_device(): call(local_kernel, [near_out(cells)] * 2, [HBM] * 2 + [SMEM] * 2, [pltpu....  2.16 us
  transfers between devices with their start and end apart: 1, of which 1 were waited for; matrix products, arithmetic and copies ran while one was open for 4% of the time, Pallas kernels for 3%

profile of v6, /device:TPU:1, one launch (start us, length us, event | category | flops | bytes accessed | tf_op | source)
XLA Modules:
  0.0 85.2 jit_solution(7777286068708650045)
XLA Ops:
  0.6 0.0 copy-start.2
  0.6 0.0 copy-start.3
  0.7 0.1 sine_negate_fusion
  0.7 2.4 %shard_map.104 = (f32[16,8,256]{2,1,0:T(8,128)S(1)}, bf16[2,32,256]{2,1,0:T(8,128)(2,1)S(1)}, bf16[2,256,512]{2,1,0:T(8,128)(2,1)S(1)}) custom-call(f32[4,256,256]{2,1,0:T(8,128)} %bitcast.5, bf16[2,32,256]{2,1,0:T(8,128)(2,1)} %constant.55.clone.forward_x, bf16[2,256,512]{2,1,0:T(8,128)(2,1)} %constant.58.clone.plane, f32[2,256]{1,0:T(2,128)S(1)} %pad_maximum_fusion.phase), custom_call_target="tpu_custom_call" | custom-call | tf_op jit(solution)/shard_map/pallas_call | solution.py:339
  3.1 0.0 copy-start.1
  3.1 12.9 %all_to_all.30.pieces = f32[16,8,256]{2,1,0:T(8,128)S(1)} all-to-all(f32[16,8,256]{2,1,0:T(8,128)S(1)} %get-tuple-element.11), channel_id=1, replica_groups={{0,1,2,3,4,5,6,7,8,9,10,11,12,13,14,15},{16,17,18,19,20,21,22,23,24,25,..., dimensions={0} | all-to-all | bytes 262144 | tf_op jit(solution)/shard_map/all_to_all | solution.py:307
  16.0 18.4 %all_to_all.31.pieces = f32[16,8,256]{2,1,0:T(8,128)S(1)} all-to-all(f32[16,8,256]{2,1,0:T(8,128)S(1)} %shard_map.105), channel_id=1, replica_groups={{0,16,32,48,64,80,96,112,130,146,162,178,194,210,226,242},{1,17,33,49,6..., dimensions={0} | all-to-all | bytes 262144 | tf_op jit(solution)/shard_map/all_to_all | solution.py:307
  34.4 0.7 shard_map.106
  35.1 5.4 %all-to-all-start.2 = ((f32[16,8,256]{2,1,0:T(8,128)}), f32[16,8,256]{2,1,0:T(8,128)S(1)}, u32[]{:S(2)}, u32[]{:S(2)}) async-start(f32[16,8,256]{2,1,0:T(8,128)} %shard_map.106), calls=%async_computation.2 | async-start | bytes 262144 | tf_op jit(solution)/shard_map/all_to_all | solution.py:307
  40.4 3.5 %reshape.125.weights = f32[2,4,4,16,256]{4,3,2,1,0:T(8,128)S(1)} reshape(f32[2,4,4,16,16,16]{5,4,3,2,1,0:T(8,128)} %param.11) | data formatting | bytes 1048576 | tf_op jit(solution)/shard_map/reshape | solution.py:352
  43.9 0.0 copy-start
  43.9 0.0 copy-done.2
  44.0 0.0 copy-done.3
  44.0 2.2 %shard_map.107 = (f32[4,256,256]{2,1,0:T(8,128)S(1)}, f32[4,256,256]{2,1,0:T(8,128)S(1)}) custom-call(f32[4,256,256]{2,1,0:T(8,128)} %bitcast.6, f32[4,256,256]{2,1,0:T(8,128)} %bitcast.7, f32[4,4]{1,0:T(4,128)S(1)} %copy-done.2, f32[4]{0:T(128)S(1)} %copy-done.3), custom_call_target="tpu_custom_call" | custom-call | tf_op jit(solution)/shard_map/pallas_call | solution.py:354
  46.1 0.5 all-to-all-done.2.modes
  46.6 0.0 copy-done.1
  46.6 1.7 %shard_map.108 = (f32[4,256,256]{2,1,0:T(8,128)S(1)}, f32[16,8,256]{2,1,0:T(8,128)S(1)}) custom-call(f32[16,8,256]{2,1,0:T(8,128)S(1)} %all-to-all-done.2.modes, f32[2,4,4,16,256]{4,3,2,1,0:T(8,128)S(1)} %reshape.125.weights, f32[4,256,256]{2,1,0:T(8,128)S(1)} %get-tuple-element.12.local, f32[4,256,256]{2,1,0:T(8,128)S(1)} %get-tuple-element.13.cotangent, ...), custom_call_target="tpu_custom_call" | custom-call | tf_op jit(solution)/shard_map/pallas_call | solution.py:360
  48.3 11.2 %all_to_all.32.pieces = f32[16,8,256]{2,1,0:T(8,128)S(1)} all-to-all(f32[16,8,256]{2,1,0:T(8,128)S(1)} %get-tuple-element.16), channel_id=1, replica_groups={{0,1,2,3,4,5,6,7,8,9,10,11,12,13,14,15},{16,17,18,19,20,21,22,23,24,25,..., dimensions={0} | all-to-all | bytes 262144 | tf_op jit(solution)/shard_map/all_to_all | solution.py:307
  59.6 11.4 %all_to_all.33.pieces = f32[16,8,256]{2,1,0:T(8,128)S(1)} all-to-all(f32[16,8,256]{2,1,0:T(8,128)S(1)} %shard_map.109), channel_id=1, replica_groups={{0,16,32,48,64,80,96,112,130,146,162,178,194,210,226,242},{1,17,33,49,6..., dimensions={0} | all-to-all | bytes 262144 | tf_op jit(solution)/shard_map/all_to_all | solution.py:307
  71.0 10.7 %all_to_all.34.back = f32[16,8,256]{2,1,0:T(8,128)S(1)} all-to-all(f32[16,8,256]{2,1,0:T(8,128)S(1)} %shard_map.110), channel_id=1, replica_groups={{0,1,2,3,4,5,6,7,8,9,10,11,12,13,14,15},{16,17,18,19,20,21,22,23,24,25,..., dimensions={0} | all-to-all | bytes 262144 | tf_op jit(solution)/shard_map/all_to_all | solution.py:307
  81.7 0.0 copy-done
  81.7 3.5 %shard_map.111 = (f32[4,256,256]{2,1,0:T(8,128)}, f32[2,4,4,16,16,16]{5,4,3,2,1,0:T(8,128)}) custom-call(f32[16,8,256]{2,1,0:T(8,128)S(1)} %all-to-all-done.2.modes, f32[16,8,256]{2,1,0:T(8,128)S(1)} %all_to_all.34.back, f32[2,4,4,16,256]{4,3,2,1,0:T(8,128)S(1)} %reshape.125.weights, f32[4,256,256]{2,1,0:T(8,128)S(1)} %get-tuple-element.17.up, ...), custom_call_target="tpu_custom_call" | custom-call | tf_op jit(solution)/shard_map/pallas_call | solution.py:366
  (4 shorter events, 0.1 us)
Async XLA Ops:
  0.6 43.3 %copy-start.2 = (f32[4,4]{1,0:T(4,128)S(1)}, f32[4,4]{1,0:T(4,128)}, u32[]{:S(2)}) copy-start(f32[4,4]{1,0:T(4,128)} %point.3) | copy-start | bytes 196
  0.6 43.3 %copy-start.3 = (f32[4]{0:T(128)S(1)}, f32[4]{0:T(128)}, u32[]{:S(2)}) copy-start(f32[4]{0:T(128)} %bias.1) | copy-start | bytes 52
  3.1 43.5 %copy-start.1 = (bf16[96,256]{1,0:T(8,128)(2,1)S(1)}, bf16[96,256]{1,0:T(8,128)(2,1)}, u32[]{:S(2)}) copy-start(bf16[96,256]{1,0:T(8,128)(2,1)} %constant.56.clone.scaled_x) | copy-start | bytes 147460
  35.1 11.6 %all-to-all-start.2 = ((f32[16,8,256]{2,1,0:T(8,128)}), f32[16,8,256]{2,1,0:T(8,128)S(1)}, u32[]{:S(2)}, u32[]{:S(2)}) async-start(f32[16,8,256]{2,1,0:T(8,128)} %shard_map.106), calls=%async_computation.2 | async-start | bytes 262144 | tf_op jit(solution)/shard_map/all_to_all | solution.py:307
  43.9 37.8 %copy-start = (bf16[96,256]{1,0:T(8,128)(2,1)S(1)}, bf16[96,256]{1,0:T(8,128)(2,1)}, u32[]{:S(2)}) copy-start(bf16[96,256]{1,0:T(8,128)(2,1)} %constant.57.clone.inverse_x) | copy-start | bytes 147460

commit v7 on v6

--- a/solution.py
+++ b/solution.py
@@ -116,7 +116,7 @@
     return ref[0], ref[1]
 
 
-def analysis_kernel(fields, forward_x, plane, phase, out, lines, square, cells, arrived):
+def analysis_kernel(fields, forward_x, plane, phase, out, cells, lines, square, arrived):
     table = pltpu.make_async_copy(forward_x, lines, arrived.at[C])
     table.start()
     copies = [
@@ -140,21 +140,15 @@
     out[...] = jnp.broadcast_to(total[None], out.shape)
 
 
-def local_kernel(fields, upper, point, bias, out, cotangent, cells, arrived):
-    copies = [
-        pltpu.make_async_copy(fields.at[c], cells.at[c], arrived.at[c]) for c in range(C)
-    ]
-    copies.append(pltpu.make_async_copy(upper, cotangent, arrived.at[C]))
-    for copy in copies:
-        copy.start()
-    for copy in copies[:C]:
-        copy.wait()
-    for o in range(C):
-        total = bias[o] * HALF_ROOT
-        for i in range(C):
-            total = total + (point[i, o] * HALF_ROOT) * cells[i]
-        out[o] = total
-    copies[C].wait()
+def local_kernel(fields, point, bias, out):
+    del fields
+    for start in range(0, CELLS, 8):
+        cells = [out[i, start : start + 8] for i in range(C)]
+        for o in range(C):
+            total = bias[o] * HALF_ROOT
+            for i in range(C):
+                total = total + (point[i, o] * HALF_ROOT) * cells[i]
+            out[o, start : start + 8] = total
 
 
 def forward_kernel(
@@ -309,7 +303,7 @@
     )
 
 
-def call(kernel, out_shape, in_specs, scratch_shapes=()):
+def call(kernel, out_shape, in_specs, scratch_shapes=(), **more):
     where = [VMEM if not isinstance(o, jax.ShapeDtypeStruct) else HBM for o in out_shape]
     return pl.pallas_call(
         kernel,
@@ -318,6 +312,7 @@
         out_specs=tuple(where),
         scratch_shapes=scratch_shapes,
         compiler_params=PARAMS,
+        **more,
     )
 
 
@@ -336,32 +331,32 @@
     shape = fields.shape
     cells = (C, CELLS, N)
     phase = near(position_phase())
-    partial, forward_x, plane = call(
+    partial, fields, forward_x, plane = call(
         analysis_kernel,
         [
             near_out((K, 2 * C, MODES)),
+            near_out(cells),
             near_out(forward_x.shape, jnp.bfloat16),
             near_out(plane.shape, jnp.bfloat16),
         ],
         [HBM] * 3 + [VMEM],
-        [pltpu.VMEM(cells, jnp.float32), pltpu.SemaphoreType.DMA((C + 2,))],
+        [pltpu.SemaphoreType.DMA((C + 2,))],
     )(far(fields.reshape(cells)), far(forward_x), far(plane), phase)
-    forward_x, scaled_x, inverse_x, plane = [
-        near(v) for v in (forward_x, scaled_x, inverse_x, plane)
+    partial, cotangent = lax.optimization_barrier((partial, cotangent))
+    fields, cotangent, forward_x, scaled_x, inverse_x, plane = [
+        near(v)
+        for v in (fields, cotangent.reshape(cells), forward_x, scaled_x, inverse_x, plane)
     ]
     weights = near(spec_weights.reshape(2, C, C, K, MODES))
     modes = total_modes(partial)
-    local, cotangent = call(
-        local_kernel,
-        [near_out(cells)] * 2,
-        [HBM] * 2 + [SMEM] * 2,
-        [pltpu.VMEM(cells, jnp.float32), pltpu.SemaphoreType.DMA((C + 1,))],
-    )(far(fields.reshape(cells)), far(cotangent.reshape(cells)), point_weights, bias)
+    (local,) = call(
+        local_kernel, [near_out(cells)], [VMEM] + [SMEM] * 2, input_output_aliases={0: 0}
+    )(fields, point_weights, bias)
     upstream, partial = call(
         forward_kernel,
         [near_out(cells), near_out((K, 2 * C, MODES))],
         [VMEM] * 8,
-    )(modes, weights, near(local), near(cotangent), phase, forward_x, scaled_x, plane)
+    )(modes, weights, near(local), cotangent, phase, forward_x, scaled_x, plane)
     back = total_modes(partial)
     grad_fields, grad_spectral = call(
         backward_kernel,

time: 85.7 us -> 84.4 us (0.985)
  Pallas kernels: 10.5 us -> 9.2 us
  waiting for transfers between devices: 0.5 us -> 1.8 us
  blocking collectives: 64.6 us -> 63.3 us
    all_to_all x1, waiting for transfers between devices: 0.5 us -> 1.8 us  [swap(): lax.all_to_all(pieces, ('row', 'col'), 0, 0, tiled=True, axis_index_group...]
    pallas_call x2, Pallas kernels: 4.55 us -> 3.25 us  [the longest x1 2.39 us: per_device(): call(analysis_kernel, [near_out((K, 2 * C, MODES)), near_out(cells), near...]
    all_to_all x5, blocking collectives: 64.6 us -> 63.3 us  [swap(): lax.all_to_all(pieces, ('row', 'col'), 0, 0, tiled=True, axis_index_group...]
  transfers between devices with their start and end apart: 1 -> 1, of which waited for: 1 -> 1; matrix products, arithmetic and copies ran while one was open for 4% -> 4% of each run, Pallas kernels for 3% -> 1%
where the time goes in v7:
time: 84.4 us; the launch traced here: 84 us
  blocking collectives  63.3 us (75%)
  Pallas kernels  9.2 us (11%)
  starting transfers between devices  5.36 us (6%)
  local copies, waits for them, and re-layouts  3.52 us (4%)
  waiting for transfers between devices  1.8 us (2%)
    all_to_all x5, blocking collectives, swap(): lax.all_to_all(pieces, ('row', 'col'), 0, 0, tiled=True, axis_index_group...  63.3 us
    all_to_all x1, starting transfers between devices, swap(): lax.all_to_all(pieces, ('row', 'col'), 0, 0, tiled=True, axis_index_group...  5.36 us
    pallas_call x1, Pallas kernels, per_device(): call(backward_kernel, [jax.ShapeDtypeStruct(cells, jnp.float32), jax.Shap...  3.54 us
    reshape x1, local copies, waits for them, and re-layouts, per_device(): weights = near(spec_weights.reshape(2, C, C, K, MODES))  3.49 us
    pallas_call x1, Pallas kernels, per_device(): call(analysis_kernel, [near_out((K, 2 * C, MODES)), near_out(cells), near...  2.39 us
    all_to_all x1, waiting for transfers between devices, swap(): lax.all_to_all(pieces, ('row', 'col'), 0, 0, tiled=True, axis_index_group...  1.8 us
  transfers between devices with their start and end apart: 1, of which 1 were waited for; matrix products, arithmetic and copies ran while one was open for 4% of the time, Pallas kernels for 1%

profile of v7, /device:TPU:1, one launch (start us, length us, event | category | flops | bytes accessed | tf_op | source)
XLA Modules:
  0.0 84.0 jit_solution(8947333968878143830)
XLA Ops:
  0.6 0.0 copy-start.3
  0.6 0.0 copy-start.4
  0.7 0.1 sine_negate_fusion
  0.7 2.4 %shard_map.104 = (f32[16,8,256]{2,1,0:T(8,128)S(1)}, f32[4,256,256]{2,1,0:T(8,128)S(1)}, bf16[2,32,256]{2,1,0:T(8,128)(2,1)S(1)}, bf16[2,256,512]{2,1,0:T(8,128)(2,1)S(1)}) custom-call(f32[4,256,256]{2,1,0:T(8,128)} %bitcast.6, bf16[2,32,256]{2,1,0:T(8,128)(2,1)} %constant.55.clone.forward_x, bf16[2,256,512]{2,1,0:T(8,128)(2,1)} %constant.58.clone.plane, ...), custom_call_target="tpu_custom_call" | custom-call | tf_op jit(solution)/shard_map/pallas_call | solution.py:334
  3.1 0.0 copy-start
  3.1 0.0 copy-start.2
  3.2 12.9 %all_to_all.30.pieces = f32[16,8,256]{2,1,0:T(8,128)S(1)} all-to-all(f32[16,8,256]{2,1,0:T(8,128)S(1)} %get-tuple-element.13), channel_id=1, replica_groups={{0,1,2,3,4,5,6,7,8,9,10,11,12,13,14,15},{16,17,18,19,20,21,22,23,24,25,..., dimensions={0} | all-to-all | bytes 262144 | tf_op jit(solution)/shard_map/all_to_all | solution.py:301
  16.1 18.4 %all_to_all.31.pieces = f32[16,8,256]{2,1,0:T(8,128)S(1)} all-to-all(f32[16,8,256]{2,1,0:T(8,128)S(1)} %shard_map.105), channel_id=1, replica_groups={{0,16,32,48,64,80,96,112,130,146,162,178,194,210,226,242},{1,17,33,49,6..., dimensions={0} | all-to-all | bytes 262144 | tf_op jit(solution)/shard_map/all_to_all | solution.py:301
  34.4 0.7 shard_map.106
  35.1 5.4 %all-to-all-start.2 = ((f32[16,8,256]{2,1,0:T(8,128)}), f32[16,8,256]{2,1,0:T(8,128)S(1)}, u32[]{:S(2)}, u32[]{:S(2)}) async-start(f32[16,8,256]{2,1,0:T(8,128)} %shard_map.106), calls=%async_computation.2 | async-start | bytes 262144 | tf_op jit(solution)/shard_map/all_to_all | solution.py:301
  40.5 3.5 %reshape.124.weights = f32[2,4,4,16,256]{4,3,2,1,0:T(8,128)S(1)} reshape(f32[2,4,4,16,16,16]{5,4,3,2,1,0:T(8,128)} %param.11) | data formatting | bytes 1048576 | tf_op jit(solution)/shard_map/reshape | solution.py:350
  44.0 0.0 copy-start.1
  44.0 0.0 copy-done.3
  44.0 0.0 copy-done.4
  44.0 0.9 %shard_map.107.local = f32[4,256,256]{2,1,0:T(8,128)S(1)} custom-call(f32[4,256,256]{2,1,0:T(8,128)S(1)} %get-tuple-element.14.fields, f32[4,4]{1,0:T(4,128)S(1)} %copy-done.3, f32[4]{0:T(128)S(1)} %copy-done.4), custom_call_target="tpu_custom_call", output_to_operand_aliasing={{}: (0, {})} | custom-call | tf_op jit(solution)/shard_map/pallas_call | solution.py:352
  44.9 1.8 %all-to-all-done.2.modes = f32[16,8,256]{2,1,0:T(8,128)S(1)} async-done(((f32[16,8,256]{2,1,0:T(8,128)}), f32[16,8,256]{2,1,0:T(8,128)S(1)}, u32[]{:S(2)}, u32[]{:S(2)}) %all-to-all-start.2) | async-done | bytes 131104 | tf_op jit(solution)/shard_map/all_to_all | solution.py:301
  46.7 0.0 copy-done
  46.7 0.0 copy-done.2
  46.7 1.7 %shard_map.108 = (f32[4,256,256]{2,1,0:T(8,128)S(1)}, f32[16,8,256]{2,1,0:T(8,128)S(1)}) custom-call(f32[16,8,256]{2,1,0:T(8,128)S(1)} %all-to-all-done.2.modes, f32[2,4,4,16,256]{4,3,2,1,0:T(8,128)S(1)} %reshape.124.weights, f32[4,256,256]{2,1,0:T(8,128)S(1)} %shard_map.107.local, f32[4,256,256]{2,1,0:T(8,128)S(1)} %bitcast.5, ...), custom_call_target="tpu_custom_call" | custom-call | tf_op jit(solution)/shard_map/pallas_call | solution.py:355
  48.3 9.9 %all_to_all.32.pieces = f32[16,8,256]{2,1,0:T(8,128)S(1)} all-to-all(f32[16,8,256]{2,1,0:T(8,128)S(1)} %get-tuple-element.18), channel_id=1, replica_groups={{0,1,2,3,4,5,6,7,8,9,10,11,12,13,14,15},{16,17,18,19,20,21,22,23,24,25,..., dimensions={0} | all-to-all | bytes 262144 | tf_op jit(solution)/shard_map/all_to_all | solution.py:301
  58.3 11.4 %all_to_all.33.pieces = f32[16,8,256]{2,1,0:T(8,128)S(1)} all-to-all(f32[16,8,256]{2,1,0:T(8,128)S(1)} %shard_map.109), channel_id=1, replica_groups={{0,16,32,48,64,80,96,112,130,146,162,178,194,210,226,242},{1,17,33,49,6..., dimensions={0} | all-to-all | bytes 262144 | tf_op jit(solution)/shard_map/all_to_all | solution.py:301
  69.8 10.7 %all_to_all.34.back = f32[16,8,256]{2,1,0:T(8,128)S(1)} all-to-all(f32[16,8,256]{2,1,0:T(8,128)S(1)} %shard_map.110), channel_id=1, replica_groups={{0,1,2,3,4,5,6,7,8,9,10,11,12,13,14,15},{16,17,18,19,20,21,22,23,24,25,..., dimensions={0} | all-to-all | bytes 262144 | tf_op jit(solution)/shard_map/all_to_all | solution.py:301
  80.4 0.0 copy-done.1
  80.4 3.5 %shard_map.111 = (f32[4,256,256]{2,1,0:T(8,128)}, f32[2,4,4,16,16,16]{5,4,3,2,1,0:T(8,128)}) custom-call(f32[16,8,256]{2,1,0:T(8,128)S(1)} %all-to-all-done.2.modes, f32[16,8,256]{2,1,0:T(8,128)S(1)} %all_to_all.34.back, f32[2,4,4,16,256]{4,3,2,1,0:T(8,128)S(1)} %reshape.124.weights, f32[4,256,256]{2,1,0:T(8,128)S(1)} %get-tuple-element.19.up, ...), custom_call_target="tpu_custom_call" | custom-call | tf_op jit(solution)/shard_map/pallas_call | solution.py:361
  (4 shorter events, 0.1 us)
Async XLA Ops:
  0.6 43.3 %copy-start.3 = (f32[4,4]{1,0:T(4,128)S(1)}, f32[4,4]{1,0:T(4,128)}, u32[]{:S(2)}) copy-start(f32[4,4]{1,0:T(4,128)} %point.3) | copy-start | bytes 196
  0.6 43.3 %copy-start.4 = (f32[4]{0:T(128)S(1)}, f32[4]{0:T(128)}, u32[]{:S(2)}) copy-start(f32[4]{0:T(128)} %bias.1) | copy-start | bytes 52
  3.1 43.5 %copy-start = (f32[1,4,16,16,256]{4,3,2,1,0:T(8,128)S(1)}, f32[1,4,16,16,256]{4,3,2,1,0:T(8,128)}, u32[]{:S(2)}) copy-start(f32[1,4,16,16,256]{4,3,2,1,0:T(8,128)} %param.10) | copy-start | bytes 3145732
  3.1 43.5 %copy-start.2 = (bf16[96,256]{1,0:T(8,128)(2,1)S(1)}, bf16[96,256]{1,0:T(8,128)(2,1)}, u32[]{:S(2)}) copy-start(bf16[96,256]{1,0:T(8,128)(2,1)} %constant.56.clone.scaled_x) | copy-start | bytes 147460
  35.1 11.6 %all-to-all-start.2 = ((f32[16,8,256]{2,1,0:T(8,128)}), f32[16,8,256]{2,1,0:T(8,128)S(1)}, u32[]{:S(2)}, u32[]{:S(2)}) async-start(f32[16,8,256]{2,1,0:T(8,128)} %shard_map.106), calls=%async_computation.2 | async-start | bytes 262144 | tf_op jit(solution)/shard_map/all_to_all | solution.py:301
  44.0 36.5 %copy-start.1 = (bf16[96,256]{1,0:T(8,128)(2,1)S(1)}, bf16[96,256]{1,0:T(8,128)(2,1)}, u32[]{:S(2)}) copy-start(bf16[96,256]{1,0:T(8,128)(2,1)} %constant.57.clone.inverse_x) | copy-start | bytes 147460

commit v8 on v7

--- a/solution.py
+++ b/solution.py
@@ -292,7 +292,8 @@
 
 def groups():
     index = np.arange(256).reshape(2, 8, 4, 2, 2)
-    index[1] = index[1, :, :, ::-1]
+    index[0] = index[0, :, :, ::-1]
+    index = index[::-1, [4, 5, 3, 6, 2, 7, 1, 0]][:, :, [2, 3, 1, 0], :, ::-1]
     index = index.reshape(K, K)
     return index.tolist(), index.T.tolist()
 

time: 84.4 us -> 76.3 us (0.904)
  blocking collectives: 63.3 us -> 55.1 us
  starting transfers between devices: 5.36 us -> 7.17 us
  waiting for transfers between devices: 1.8 us -> 0.01 us
    all_to_all x5, blocking collectives: 63.3 us -> 55.1 us  [swap(): lax.all_to_all(pieces, ('row', 'col'), 0, 0, tiled=True, axis_index_group...]
    all_to_all x1, starting transfers between devices: 5.36 us -> 7.17 us  [swap(): lax.all_to_all(pieces, ('row', 'col'), 0, 0, tiled=True, axis_index_group...]
    all_to_all x1, waiting for transfers between devices: 1.8 us -> 0.01 us  [swap(): lax.all_to_all(pieces, ('row', 'col'), 0, 0, tiled=True, axis_index_group...]
  transfers between devices with their start and end apart: 1 -> 1, of which waited for: 1 -> 0; matrix products, arithmetic and copies ran while one was open for 4% -> 5% of each run, Pallas kernels for 1% -> 1%
where the time goes in v8:
time: 76.3 us; the launch traced here: 75.9 us
  blocking collectives  55.1 us (72%)
  Pallas kernels  9.21 us (12%)
  starting transfers between devices  7.17 us (9%)
  local copies, waits for them, and re-layouts  3.52 us (5%)
  between operations  0.77 us (1%)
    all_to_all x5, blocking collectives, swap(): lax.all_to_all(pieces, ('row', 'col'), 0, 0, tiled=True, axis_index_group...  55.1 us
    all_to_all x1, starting transfers between devices, swap(): lax.all_to_all(pieces, ('row', 'col'), 0, 0, tiled=True, axis_index_group...  7.17 us
    pallas_call x1, Pallas kernels, per_device(): call(backward_kernel, [jax.ShapeDtypeStruct(cells, jnp.float32), jax.Shap...  3.54 us
    reshape x1, local copies, waits for them, and re-layouts, per_device(): weights = near(spec_weights.reshape(2, C, C, K, MODES))  3.49 us
    pallas_call x1, Pallas kernels, per_device(): call(analysis_kernel, [near_out((K, 2 * C, MODES)), near_out(cells), near...  2.39 us
    pallas_call x1, Pallas kernels, per_device(): call(forward_kernel, [near_out(cells), near_out((K, 2 * C, MODES))], [VME...  1.65 us
  transfers between devices with their start and end apart: 1, of which 0 were waited for; matrix products, arithmetic and copies ran while one was open for 5% of the time, Pallas kernels for 1%

profile of v8, /device:TPU:1, one launch (start us, length us, event | category | flops | bytes accessed | tf_op | source)
XLA Modules:
  0.0 75.9 jit_solution(1512625243057150171)
XLA Ops:
  0.6 0.0 copy-start.3
  0.6 0.0 copy-start.4
  0.7 0.1 sine_negate_fusion
  0.7 2.4 %shard_map.104 = (f32[16,8,256]{2,1,0:T(8,128)S(1)}, f32[4,256,256]{2,1,0:T(8,128)S(1)}, bf16[2,32,256]{2,1,0:T(8,128)(2,1)S(1)}, bf16[2,256,512]{2,1,0:T(8,128)(2,1)S(1)}) custom-call(f32[4,256,256]{2,1,0:T(8,128)} %bitcast.6, bf16[2,32,256]{2,1,0:T(8,128)(2,1)} %constant.55.clone.forward_x, bf16[2,256,512]{2,1,0:T(8,128)(2,1)} %constant.58.clone.plane, ...), custom_call_target="tpu_custom_call" | custom-call | tf_op jit(solution)/shard_map/pallas_call | solution.py:335
  3.1 0.0 copy-start
  3.1 0.0 copy-start.2
  3.2 11.0 %all_to_all.30.pieces = f32[16,8,256]{2,1,0:T(8,128)S(1)} all-to-all(f32[16,8,256]{2,1,0:T(8,128)S(1)} %get-tuple-element.13), channel_id=1, replica_groups={{201,200,203,202,205,204,207,206,197,196,199,198,193,192,195,194},{217,..., dimensions={0} | all-to-all | bytes 262144 | tf_op jit(solution)/shard_map/all_to_all | solution.py:302
  14.2 14.4 %all_to_all.31.pieces = f32[16,8,256]{2,1,0:T(8,128)S(1)} all-to-all(f32[16,8,256]{2,1,0:T(8,128)S(1)} %shard_map.105), channel_id=1, replica_groups={{201,217,185,233,169,249,153,137,75,91,59,107,43,123,27,11},{200,216,18..., dimensions={0} | all-to-all | bytes 262144 | tf_op jit(solution)/shard_map/all_to_all | solution.py:302
  28.6 0.7 shard_map.106
  29.3 7.2 %all-to-all-start.2 = ((f32[16,8,256]{2,1,0:T(8,128)}), f32[16,8,256]{2,1,0:T(8,128)S(1)}, u32[]{:S(2)}, u32[]{:S(2)}) async-start(f32[16,8,256]{2,1,0:T(8,128)} %shard_map.106), calls=%async_computation.2 | async-start | bytes 262144 | tf_op jit(solution)/shard_map/all_to_all | solution.py:302
  36.4 3.5 %reshape.124.weights = f32[2,4,4,16,256]{4,3,2,1,0:T(8,128)S(1)} reshape(f32[2,4,4,16,16,16]{5,4,3,2,1,0:T(8,128)} %param.11) | data formatting | bytes 1048576 | tf_op jit(solution)/shard_map/reshape | solution.py:351
  39.9 0.0 copy-start.1
  39.9 0.0 copy-done.3
  39.9 0.0 copy-done.4
  40.0 0.9 %shard_map.107.local = f32[4,256,256]{2,1,0:T(8,128)S(1)} custom-call(f32[4,256,256]{2,1,0:T(8,128)S(1)} %get-tuple-element.14.fields, f32[4,4]{1,0:T(4,128)S(1)} %copy-done.3, f32[4]{0:T(128)S(1)} %copy-done.4), custom_call_target="tpu_custom_call", output_to_operand_aliasing={{}: (0, {})} | custom-call | tf_op jit(solution)/shard_map/pallas_call | solution.py:353
  40.8 0.0 all-to-all-done.2.modes
  40.8 0.0 copy-done
  40.8 0.0 copy-done.2
  40.9 1.7 %shard_map.108 = (f32[4,256,256]{2,1,0:T(8,128)S(1)}, f32[16,8,256]{2,1,0:T(8,128)S(1)}) custom-call(f32[16,8,256]{2,1,0:T(8,128)S(1)} %all-to-all-done.2.modes, f32[2,4,4,16,256]{4,3,2,1,0:T(8,128)S(1)} %reshape.124.weights, f32[4,256,256]{2,1,0:T(8,128)S(1)} %shard_map.107.local, f32[4,256,256]{2,1,0:T(8,128)S(1)} %bitcast.5, ...), custom_call_target="tpu_custom_call" | custom-call | tf_op jit(solution)/shard_map/pallas_call | solution.py:356
  42.5 8.1 %all_to_all.32.pieces = f32[16,8,256]{2,1,0:T(8,128)S(1)} all-to-all(f32[16,8,256]{2,1,0:T(8,128)S(1)} %get-tuple-element.18), channel_id=1, replica_groups={{201,200,203,202,205,204,207,206,197,196,199,198,193,192,195,194},{217,..., dimensions={0} | all-to-all | bytes 262144 | tf_op jit(solution)/shard_map/all_to_all | solution.py:302
  50.6 11.9 %all_to_all.33.pieces = f32[16,8,256]{2,1,0:T(8,128)S(1)} all-to-all(f32[16,8,256]{2,1,0:T(8,128)S(1)} %shard_map.109), channel_id=1, replica_groups={{201,217,185,233,169,249,153,137,75,91,59,107,43,123,27,11},{200,216,18..., dimensions={0} | all-to-all | bytes 262144 | tf_op jit(solution)/shard_map/all_to_all | solution.py:302
  62.6 9.8 %all_to_all.34.back = f32[16,8,256]{2,1,0:T(8,128)S(1)} all-to-all(f32[16,8,256]{2,1,0:T(8,128)S(1)} %shard_map.110), channel_id=1, replica_groups={{201,200,203,202,205,204,207,206,197,196,199,198,193,192,195,194},{217,..., dimensions={0} | all-to-all | bytes 262144 | tf_op jit(solution)/shard_map/all_to_all | solution.py:302
  72.3 0.0 copy-done.1
  72.3 3.5 %shard_map.111 = (f32[4,256,256]{2,1,0:T(8,128)}, f32[2,4,4,16,16,16]{5,4,3,2,1,0:T(8,128)}) custom-call(f32[16,8,256]{2,1,0:T(8,128)S(1)} %all-to-all-done.2.modes, f32[16,8,256]{2,1,0:T(8,128)S(1)} %all_to_all.34.back, f32[2,4,4,16,256]{4,3,2,1,0:T(8,128)S(1)} %reshape.124.weights, f32[4,256,256]{2,1,0:T(8,128)S(1)} %get-tuple-element.19.up, ...), custom_call_target="tpu_custom_call" | custom-call | tf_op jit(solution)/shard_map/pallas_call | solution.py:362
  (4 shorter events, 0.1 us)
Async XLA Ops:
  0.6 39.3 %copy-start.3 = (f32[4,4]{1,0:T(4,128)S(1)}, f32[4,4]{1,0:T(4,128)}, u32[]{:S(2)}) copy-start(f32[4,4]{1,0:T(4,128)} %point.3) | copy-start | bytes 196
  0.6 39.3 %copy-start.4 = (f32[4]{0:T(128)S(1)}, f32[4]{0:T(128)}, u32[]{:S(2)}) copy-start(f32[4]{0:T(128)} %bias.1) | copy-start | bytes 52
  3.1 37.7 %copy-start = (f32[1,4,16,16,256]{4,3,2,1,0:T(8,128)S(1)}, f32[1,4,16,16,256]{4,3,2,1,0:T(8,128)}, u32[]{:S(2)}) copy-start(f32[1,4,16,16,256]{4,3,2,1,0:T(8,128)} %param.10) | copy-start | bytes 3145732
  3.1 37.7 %copy-start.2 = (bf16[96,256]{1,0:T(8,128)(2,1)S(1)}, bf16[96,256]{1,0:T(8,128)(2,1)}, u32[]{:S(2)}) copy-start(bf16[96,256]{1,0:T(8,128)(2,1)} %constant.56.clone.scaled_x) | copy-start | bytes 147460
  29.3 11.6 %all-to-all-start.2 = ((f32[16,8,256]{2,1,0:T(8,128)}), f32[16,8,256]{2,1,0:T(8,128)S(1)}, u32[]{:S(2)}, u32[]{:S(2)}) async-start(f32[16,8,256]{2,1,0:T(8,128)} %shard_map.106), calls=%async_computation.2 | async-start | bytes 262144 | tf_op jit(solution)/shard_map/all_to_all | solution.py:302
  39.9 32.4 %copy-start.1 = (bf16[96,256]{1,0:T(8,128)(2,1)S(1)}, bf16[96,256]{1,0:T(8,128)(2,1)}, u32[]{:S(2)}) copy-start(bf16[96,256]{1,0:T(8,128)(2,1)} %constant.57.clone.inverse_x) | copy-start | bytes 147460

commit v9 on v8

--- a/solution.py
+++ b/solution.py
@@ -317,14 +317,15 @@
     )
 
 
-def total_modes(partial):
+def total_modes(partial, *beside):
     shape = (K, 2 * C, MODES)
     near_by, alike = groups()
     pieces = near(swap(partial, near_by))
     (pieces,) = call(spread_kernel, [near_out(shape)], [VMEM])(pieces)
-    pieces = near(swap(pieces, alike))
+    pieces, *beside = lax.optimization_barrier((swap(pieces, alike), *beside))
+    pieces = near(pieces)
     (pieces,) = call(spread_kernel, [near_out(shape)], [VMEM])(pieces)
-    return near(swap(pieces, near_by))
+    return near(swap(pieces, near_by)), *beside
 
 
 def per_device(fields, cotangent, spec_weights, point_weights, bias):
@@ -348,17 +349,18 @@
         near(v)
         for v in (fields, cotangent.reshape(cells), forward_x, scaled_x, inverse_x, plane)
     ]
-    weights = near(spec_weights.reshape(2, C, C, K, MODES))
-    modes = total_modes(partial)
+    weights = spec_weights.reshape(2, C, C, K, MODES)
     (local,) = call(
         local_kernel, [near_out(cells)], [VMEM] + [SMEM] * 2, input_output_aliases={0: 0}
     )(fields, point_weights, bias)
+    modes, weights, local = total_modes(partial, weights, local)
+    weights = near(weights)
     upstream, partial = call(
         forward_kernel,
         [near_out(cells), near_out((K, 2 * C, MODES))],
         [VMEM] * 8,
     )(modes, weights, near(local), cotangent, phase, forward_x, scaled_x, plane)
-    back = total_modes(partial)
+    (back,) = total_modes(partial)
     grad_fields, grad_spectral = call(
         backward_kernel,
         [

time: 76.3 us -> 75.8 us (level)
  blocking collectives: 55.1 us -> 50.1 us
  starting transfers between devices: 7.17 us -> 11.7 us
    all_to_all x5, blocking collectives: 55.1 us -> 50.1 us  [swap(): lax.all_to_all(pieces, ('row', 'col'), 0, 0, tiled=True, axis_index_group...]
    all_to_all x1, starting transfers between devices: 7.17 us -> 11.7 us  [swap(): lax.all_to_all(pieces, ('row', 'col'), 0, 0, tiled=True, axis_index_group...]
where the time goes in v9:
time: 75.8 us; the launch traced here: 75.4 us
  blocking collectives  50.1 us (66%)
  starting transfers between devices  11.7 us (15%)
  Pallas kernels  9.22 us (12%)
  local copies, waits for them, and re-layouts  3.52 us (5%)
  between operations  0.76 us (1%)
    all_to_all x5, blocking collectives, swap(): lax.all_to_all(pieces, ('row', 'col'), 0, 0, tiled=True, axis_index_group...  50.1 us
    all_to_all x1, starting transfers between devices, swap(): lax.all_to_all(pieces, ('row', 'col'), 0, 0, tiled=True, axis_index_group...  11.7 us
    pallas_call x1, Pallas kernels, per_device(): call(backward_kernel, [jax.ShapeDtypeStruct(cells, jnp.float32), jax.Shap...  3.54 us
    reshape x1, local copies, waits for them, and re-layouts, per_device(): weights = spec_weights.reshape(2, C, C, K, MODES)  3.49 us
    pallas_call x1, Pallas kernels, per_device(): call(analysis_kernel, [near_out((K, 2 * C, MODES)), near_out(cells), near...  2.39 us
    pallas_call x1, Pallas kernels, per_device(): call(forward_kernel, [near_out(cells), near_out((K, 2 * C, MODES))], [VME...  1.68 us
  transfers between devices with their start and end apart: 1, of which 0 were waited for; matrix products, arithmetic and copies ran while one was open for 5% of the time, Pallas kernels for 1%

profile of v9, /device:TPU:1, one launch (start us, length us, event | category | flops | bytes accessed | tf_op | source)
XLA Modules:
  0.0 75.4 jit_solution(8919804148796453571)
XLA Ops:
  0.6 0.0 copy-start.3
  0.6 0.0 copy-start.4
  0.7 0.1 sine_negate_fusion
  0.7 2.4 %shard_map.104 = (f32[16,8,256]{2,1,0:T(8,128)S(1)}, f32[4,256,256]{2,1,0:T(8,128)S(1)}, bf16[2,32,256]{2,1,0:T(8,128)(2,1)S(1)}, bf16[2,256,512]{2,1,0:T(8,128)(2,1)S(1)}) custom-call(f32[4,256,256]{2,1,0:T(8,128)} %bitcast.6, bf16[2,32,256]{2,1,0:T(8,128)(2,1)} %constant.55.clone.forward_x, bf16[2,256,512]{2,1,0:T(8,128)(2,1)} %constant.58.clone.plane, ...), custom_call_target="tpu_custom_call" | custom-call | tf_op jit(solution)/shard_map/pallas_call | solution.py:336
  3.1 0.0 copy-start
  3.1 0.0 copy-start.2
  3.2 11.0 %all_to_all.30.pieces = f32[16,8,256]{2,1,0:T(8,128)S(1)} all-to-all(f32[16,8,256]{2,1,0:T(8,128)S(1)} %get-tuple-element.16), channel_id=1, replica_groups={{201,200,203,202,205,204,207,206,197,196,199,198,193,192,195,194},{217,..., dimensions={0} | all-to-all | bytes 262144 | tf_op jit(solution)/shard_map/all_to_all | solution.py:302
  14.2 0.7 shard_map.105
  14.8 11.7 %all-to-all-start.1 = ((f32[16,8,256]{2,1,0:T(8,128)}), f32[16,8,256]{2,1,0:T(8,128)S(1)}, u32[]{:S(2)}, u32[]{:S(2)}) async-start(f32[16,8,256]{2,1,0:T(8,128)} %shard_map.105), calls=%async_computation.1 | async-start | bytes 262144 | tf_op jit(solution)/shard_map/all_to_all | solution.py:302
  26.6 3.5 %reshape.124.weights = f32[2,4,4,16,256]{4,3,2,1,0:T(8,128)S(1)} reshape(f32[2,4,4,16,16,16]{5,4,3,2,1,0:T(8,128)} %param.11) | data formatting | bytes 1048576 | tf_op jit(solution)/shard_map/reshape | solution.py:352
  30.1 0.0 copy-start.1
  30.1 0.0 copy-done.3
  30.1 0.0 copy-done.4
  30.1 0.9 %shard_map.106.local = f32[4,256,256]{2,1,0:T(8,128)S(1)} custom-call(f32[4,256,256]{2,1,0:T(8,128)S(1)} %get-tuple-element.17.fields, f32[4,4]{1,0:T(4,128)S(1)} %copy-done.3, f32[4]{0:T(128)S(1)} %copy-done.4), custom_call_target="tpu_custom_call", output_to_operand_aliasing={{}: (0, {})} | custom-call | tf_op jit(solution)/shard_map/pallas_call | solution.py:353
  31.0 0.0 all-to-all-done.1.pieces
  31.0 8.8 %all_to_all.31.modes = f32[16,8,256]{2,1,0:T(8,128)S(1)} all-to-all(f32[16,8,256]{2,1,0:T(8,128)S(1)} %shard_map.107), channel_id=1, replica_groups={{201,200,203,202,205,204,207,206,197,196,199,198,193,192,195,194},{217,..., dimensions={0} | all-to-all | bytes 262144 | tf_op jit(solution)/shard_map/all_to_all | solution.py:302
  39.9 0.0 copy-done
  39.9 0.0 copy-done.2
  39.9 1.7 %shard_map.108 = (f32[4,256,256]{2,1,0:T(8,128)S(1)}, f32[16,8,256]{2,1,0:T(8,128)S(1)}) custom-call(f32[16,8,256]{2,1,0:T(8,128)S(1)} %all_to_all.31.modes, f32[2,4,4,16,256]{4,3,2,1,0:T(8,128)S(1)} %reshape.124.weights, f32[4,256,256]{2,1,0:T(8,128)S(1)} %shard_map.106.local, f32[4,256,256]{2,1,0:T(8,128)S(1)} %bitcast.5, ...), custom_call_target="tpu_custom_call" | custom-call | tf_op jit(solution)/shard_map/pallas_call | solution.py:358
  41.6 8.7 %all_to_all.32.pieces = f32[16,8,256]{2,1,0:T(8,128)S(1)} all-to-all(f32[16,8,256]{2,1,0:T(8,128)S(1)} %get-tuple-element.24), channel_id=1, replica_groups={{201,200,203,202,205,204,207,206,197,196,199,198,193,192,195,194},{217,..., dimensions={0} | all-to-all | bytes 262144 | tf_op jit(solution)/shard_map/all_to_all | solution.py:302
  50.3 11.9 %all_to_all.33.pieces = f32[16,8,256]{2,1,0:T(8,128)S(1)} all-to-all(f32[16,8,256]{2,1,0:T(8,128)S(1)} %shard_map.109), channel_id=1, replica_groups={{201,217,185,233,169,249,153,137,75,91,59,107,43,123,27,11},{200,216,18..., dimensions={0} | all-to-all | bytes 262144 | tf_op jit(solution)/shard_map/all_to_all | solution.py:302
  62.2 9.6 %all_to_all.34.back = f32[16,8,256]{2,1,0:T(8,128)S(1)} all-to-all(f32[16,8,256]{2,1,0:T(8,128)S(1)} %shard_map.110), channel_id=1, replica_groups={{201,200,203,202,205,204,207,206,197,196,199,198,193,192,195,194},{217,..., dimensions={0} | all-to-all | bytes 262144 | tf_op jit(solution)/shard_map/all_to_all | solution.py:302
  71.8 0.0 copy-done.1
  71.8 3.5 %shard_map.111 = (f32[4,256,256]{2,1,0:T(8,128)}, f32[2,4,4,16,16,16]{5,4,3,2,1,0:T(8,128)}) custom-call(f32[16,8,256]{2,1,0:T(8,128)S(1)} %all_to_all.31.modes, f32[16,8,256]{2,1,0:T(8,128)S(1)} %all_to_all.34.back, f32[2,4,4,16,256]{4,3,2,1,0:T(8,128)S(1)} %reshape.124.weights, f32[4,256,256]{2,1,0:T(8,128)S(1)} %get-tuple-element.25.up, ...), custom_call_target="tpu_custom_call" | custom-call | tf_op jit(solution)/shard_map/pallas_call | solution.py:364
  (4 shorter events, 0.1 us)
Async XLA Ops:
  0.6 29.5 %copy-start.3 = (f32[4,4]{1,0:T(4,128)S(1)}, f32[4,4]{1,0:T(4,128)}, u32[]{:S(2)}) copy-start(f32[4,4]{1,0:T(4,128)} %point.3) | copy-start | bytes 196
  0.6 29.5 %copy-start.4 = (f32[4]{0:T(128)S(1)}, f32[4]{0:T(128)}, u32[]{:S(2)}) copy-start(f32[4]{0:T(128)} %bias.1) | copy-start | bytes 52
  3.1 36.7 %copy-start = (f32[1,4,16,16,256]{4,3,2,1,0:T(8,128)S(1)}, f32[1,4,16,16,256]{4,3,2,1,0:T(8,128)}, u32[]{:S(2)}) copy-start(f32[1,4,16,16,256]{4,3,2,1,0:T(8,128)} %param.10) | copy-start | bytes 3145732
  3.1 36.7 %copy-start.2 = (bf16[96,256]{1,0:T(8,128)(2,1)S(1)}, bf16[96,256]{1,0:T(8,128)(2,1)}, u32[]{:S(2)}) copy-start(bf16[96,256]{1,0:T(8,128)(2,1)} %constant.56.clone.scaled_x) | copy-start | bytes 147460
  14.8 16.1 %all-to-all-start.1 = ((f32[16,8,256]{2,1,0:T(8,128)}), f32[16,8,256]{2,1,0:T(8,128)S(1)}, u32[]{:S(2)}, u32[]{:S(2)}) async-start(f32[16,8,256]{2,1,0:T(8,128)} %shard_map.105), calls=%async_computation.1 | async-start | bytes 262144 | tf_op jit(solution)/shard_map/all_to_all | solution.py:302
  30.1 41.8 %copy-start.1 = (bf16[96,256]{1,0:T(8,128)(2,1)S(1)}, bf16[96,256]{1,0:T(8,128)(2,1)}, u32[]{:S(2)}) copy-start(bf16[96,256]{1,0:T(8,128)(2,1)} %constant.57.clone.inverse_x) | copy-start | bytes 147460

commit v10 on v9

--- a/solution.py
+++ b/solution.py
@@ -129,7 +129,9 @@
     table.wait()
 
     def channel(c):
-        copies[c].wait()
+        if c % 2 == 0:
+            copies[c].wait()
+            copies[c + 1].wait()
         return cells[c]
 
     analyse(channel, phase[...], parts(lines), square, out, second.wait)
@@ -241,8 +243,8 @@
     modes_turned, back_turned = turned(modes[...]), turned(back[...])
     for p in range(K):
         one_wave(p)
-        if p % 4 == 3:
-            some = pl.ds(p - 3, 4)
+        if p % 2 == 1:
+            some = pl.ds(p - 1, 2)
             send(stored.at[:, :, :, some], grad_spectral.at[:, :, :, some])
     adjoint_re, adjoint_im = [], []
     for i in range(C):
@@ -371,7 +373,7 @@
         [
             pltpu.VMEM(cells, jnp.float32),
             pltpu.VMEM((2, C, C, K, K, K), jnp.float32),
-            pltpu.SemaphoreType.DMA((8,)),
+            pltpu.SemaphoreType.DMA((12,)),
         ],
     )(modes, back, weights, near(upstream), point_weights, phase, inverse_x, plane)
     return grad_fields.reshape(shape), grad_spectral

time: 75.8 us -> 75.4 us (level)
  no operation moved by 1% of the time
where the time goes in v10:
time: 75.4 us; the launch traced here: 75 us
  blocking collectives  50.1 us (66%)
  starting transfers between devices  11.7 us (16%)
  Pallas kernels  8.85 us (12%)
  local copies, waits for them, and re-layouts  3.52 us (5%)
  between operations  0.76 us (1%)
    all_to_all x5, blocking collectives, swap(): lax.all_to_all(pieces, ('row', 'col'), 0, 0, tiled=True, axis_index_group...  50.1 us
    all_to_all x1, starting transfers between devices, swap(): lax.all_to_all(pieces, ('row', 'col'), 0, 0, tiled=True, axis_index_group...  11.7 us
    reshape x1, local copies, waits for them, and re-layouts, per_device(): weights = spec_weights.reshape(2, C, C, K, MODES)  3.49 us
    pallas_call x1, Pallas kernels, per_device(): call(backward_kernel, [jax.ShapeDtypeStruct(cells, jnp.float32), jax.Shap...  3.46 us
    pallas_call x1, Pallas kernels, per_device(): call(analysis_kernel, [near_out((K, 2 * C, MODES)), near_out(cells), near...  2.09 us
    pallas_call x1, Pallas kernels, per_device(): call(forward_kernel, [near_out(cells), near_out((K, 2 * C, MODES))], [VME...  1.67 us
  transfers between devices with their start and end apart: 1, of which 0 were waited for; matrix products, arithmetic and copies ran while one was open for 5% of the time, Pallas kernels for 1%

profile of v10, /device:TPU:1, one launch (start us, length us, event | category | flops | bytes accessed | tf_op | source)
XLA Modules:
  0.0 75.0 jit_solution(17650118101944644970)
XLA Ops:
  0.6 0.0 copy-start.3
  0.6 0.0 copy-start.4
  0.7 0.1 sine_negate_fusion
  0.7 2.1 %shard_map.104 = (f32[16,8,256]{2,1,0:T(8,128)S(1)}, f32[4,256,256]{2,1,0:T(8,128)S(1)}, bf16[2,32,256]{2,1,0:T(8,128)(2,1)S(1)}, bf16[2,256,512]{2,1,0:T(8,128)(2,1)S(1)}) custom-call(f32[4,256,256]{2,1,0:T(8,128)} %bitcast.6, bf16[2,32,256]{2,1,0:T(8,128)(2,1)} %constant.55.clone.forward_x, bf16[2,256,512]{2,1,0:T(8,128)(2,1)} %constant.58.clone.plane, ...), custom_call_target="tpu_custom_call" | custom-call | tf_op jit(solution)/shard_map/pallas_call | solution.py:338
  2.8 0.0 copy-start
  2.8 0.0 copy-start.2
  2.9 11.0 %all_to_all.30.pieces = f32[16,8,256]{2,1,0:T(8,128)S(1)} all-to-all(f32[16,8,256]{2,1,0:T(8,128)S(1)} %get-tuple-element.16), channel_id=1, replica_groups={{201,200,203,202,205,204,207,206,197,196,199,198,193,192,195,194},{217,..., dimensions={0} | all-to-all | bytes 262144 | tf_op jit(solution)/shard_map/all_to_all | solution.py:304
  13.9 0.7 shard_map.105
  14.5 11.7 %all-to-all-start.1 = ((f32[16,8,256]{2,1,0:T(8,128)}), f32[16,8,256]{2,1,0:T(8,128)S(1)}, u32[]{:S(2)}, u32[]{:S(2)}) async-start(f32[16,8,256]{2,1,0:T(8,128)} %shard_map.105), calls=%async_computation.1 | async-start | bytes 262144 | tf_op jit(solution)/shard_map/all_to_all | solution.py:304
  26.3 3.5 %reshape.124.weights = f32[2,4,4,16,256]{4,3,2,1,0:T(8,128)S(1)} reshape(f32[2,4,4,16,16,16]{5,4,3,2,1,0:T(8,128)} %param.11) | data formatting | bytes 1048576 | tf_op jit(solution)/shard_map/reshape | solution.py:354
  29.8 0.0 copy-start.1
  29.8 0.0 copy-done.3
  29.8 0.0 copy-done.4
  29.8 0.9 %shard_map.106.local = f32[4,256,256]{2,1,0:T(8,128)S(1)} custom-call(f32[4,256,256]{2,1,0:T(8,128)S(1)} %get-tuple-element.17.fields, f32[4,4]{1,0:T(4,128)S(1)} %copy-done.3, f32[4]{0:T(128)S(1)} %copy-done.4), custom_call_target="tpu_custom_call", output_to_operand_aliasing={{}: (0, {})} | custom-call | tf_op jit(solution)/shard_map/pallas_call | solution.py:355
  30.7 0.0 all-to-all-done.1.pieces
  30.7 8.8 %all_to_all.31.modes = f32[16,8,256]{2,1,0:T(8,128)S(1)} all-to-all(f32[16,8,256]{2,1,0:T(8,128)S(1)} %shard_map.107), channel_id=1, replica_groups={{201,200,203,202,205,204,207,206,197,196,199,198,193,192,195,194},{217,..., dimensions={0} | all-to-all | bytes 262144 | tf_op jit(solution)/shard_map/all_to_all | solution.py:304
  39.6 0.0 copy-done
  39.6 0.0 copy-done.2
  39.6 1.7 %shard_map.108 = (f32[4,256,256]{2,1,0:T(8,128)S(1)}, f32[16,8,256]{2,1,0:T(8,128)S(1)}) custom-call(f32[16,8,256]{2,1,0:T(8,128)S(1)} %all_to_all.31.modes, f32[2,4,4,16,256]{4,3,2,1,0:T(8,128)S(1)} %reshape.124.weights, f32[4,256,256]{2,1,0:T(8,128)S(1)} %shard_map.106.local, f32[4,256,256]{2,1,0:T(8,128)S(1)} %bitcast.5, ...), custom_call_target="tpu_custom_call" | custom-call | tf_op jit(solution)/shard_map/pallas_call | solution.py:360
  41.3 8.7 %all_to_all.32.pieces = f32[16,8,256]{2,1,0:T(8,128)S(1)} all-to-all(f32[16,8,256]{2,1,0:T(8,128)S(1)} %get-tuple-element.24), channel_id=1, replica_groups={{201,200,203,202,205,204,207,206,197,196,199,198,193,192,195,194},{217,..., dimensions={0} | all-to-all | bytes 262144 | tf_op jit(solution)/shard_map/all_to_all | solution.py:304
  50.0 11.9 %all_to_all.33.pieces = f32[16,8,256]{2,1,0:T(8,128)S(1)} all-to-all(f32[16,8,256]{2,1,0:T(8,128)S(1)} %shard_map.109), channel_id=1, replica_groups={{201,217,185,233,169,249,153,137,75,91,59,107,43,123,27,11},{200,216,18..., dimensions={0} | all-to-all | bytes 262144 | tf_op jit(solution)/shard_map/all_to_all | solution.py:304
  61.9 9.6 %all_to_all.34.back = f32[16,8,256]{2,1,0:T(8,128)S(1)} all-to-all(f32[16,8,256]{2,1,0:T(8,128)S(1)} %shard_map.110), channel_id=1, replica_groups={{201,200,203,202,205,204,207,206,197,196,199,198,193,192,195,194},{217,..., dimensions={0} | all-to-all | bytes 262144 | tf_op jit(solution)/shard_map/all_to_all | solution.py:304
  71.5 0.0 copy-done.1
  71.6 3.5 %shard_map.111 = (f32[4,256,256]{2,1,0:T(8,128)}, f32[2,4,4,16,16,16]{5,4,3,2,1,0:T(8,128)}) custom-call(f32[16,8,256]{2,1,0:T(8,128)S(1)} %all_to_all.31.modes, f32[16,8,256]{2,1,0:T(8,128)S(1)} %all_to_all.34.back, f32[2,4,4,16,256]{4,3,2,1,0:T(8,128)S(1)} %reshape.124.weights, f32[4,256,256]{2,1,0:T(8,128)S(1)} %get-tuple-element.25.up, ...), custom_call_target="tpu_custom_call" | custom-call | tf_op jit(solution)/shard_map/pallas_call | solution.py:366
  (4 shorter events, 0.1 us)
Async XLA Ops:
  0.6 29.2 %copy-start.3 = (f32[4,4]{1,0:T(4,128)S(1)}, f32[4,4]{1,0:T(4,128)}, u32[]{:S(2)}) copy-start(f32[4,4]{1,0:T(4,128)} %point.3) | copy-start | bytes 196
  0.6 29.2 %copy-start.4 = (f32[4]{0:T(128)S(1)}, f32[4]{0:T(128)}, u32[]{:S(2)}) copy-start(f32[4]{0:T(128)} %bias.1) | copy-start | bytes 52
  2.8 36.7 %copy-start = (f32[1,4,16,16,256]{4,3,2,1,0:T(8,128)S(1)}, f32[1,4,16,16,256]{4,3,2,1,0:T(8,128)}, u32[]{:S(2)}) copy-start(f32[1,4,16,16,256]{4,3,2,1,0:T(8,128)} %param.10) | copy-start | bytes 3145732
  2.8 36.7 %copy-start.2 = (bf16[96,256]{1,0:T(8,128)(2,1)S(1)}, bf16[96,256]{1,0:T(8,128)(2,1)}, u32[]{:S(2)}) copy-start(bf16[96,256]{1,0:T(8,128)(2,1)} %constant.56.clone.scaled_x) | copy-start | bytes 147460
  14.5 16.1 %all-to-all-start.1 = ((f32[16,8,256]{2,1,0:T(8,128)}), f32[16,8,256]{2,1,0:T(8,128)S(1)}, u32[]{:S(2)}, u32[]{:S(2)}) async-start(f32[16,8,256]{2,1,0:T(8,128)} %shard_map.105), calls=%async_computation.1 | async-start | bytes 262144 | tf_op jit(solution)/shard_map/all_to_all | solution.py:304
  29.8 41.8 %copy-start.1 = (bf16[96,256]{1,0:T(8,128)(2,1)S(1)}, bf16[96,256]{1,0:T(8,128)(2,1)}, u32[]{:S(2)}) copy-start(bf16[96,256]{1,0:T(8,128)(2,1)} %constant.57.clone.inverse_x) | copy-start | bytes 147460

commit v11 on v10

--- a/solution.py
+++ b/solution.py
@@ -116,7 +116,7 @@
     return ref[0], ref[1]
 
 
-def analysis_kernel(fields, forward_x, plane, phase, out, cells, lines, square, arrived):
+def analysis_kernel(fields, forward_x, plane, out, cells, lines, square, phase, arrived):
     table = pltpu.make_async_copy(forward_x, lines, arrived.at[C])
     table.start()
     copies = [
@@ -126,6 +126,7 @@
         copy.start()
     second = pltpu.make_async_copy(plane, square, arrived.at[C + 1])
     second.start()
+    phase[...] = position_phase()
     table.wait()
 
     def channel(c):
@@ -274,10 +275,12 @@
 
 
 def position_phase():
-    lane = jnp.arange(MODES, dtype=jnp.int32)
+    shape = (2, MODES)
+    lane = lax.broadcasted_iota(jnp.int32, shape, 1)
     steps = (lane // K) * lax.axis_index("row") + (lane % K) * lax.axis_index("col")
     angle = (steps % K).astype(jnp.float32) * (2.0 * math.pi / K)
-    return jnp.stack([jnp.cos(angle), -jnp.sin(angle)], 0)
+    row = lax.broadcasted_iota(jnp.int32, shape, 0)
+    return jnp.where(row == 0, jnp.cos(angle), -jnp.sin(angle))
 
 
 def near(value):
@@ -334,22 +337,24 @@
     forward_x, scaled_x, inverse_x, plane = [jnp.asarray(t) for t in tables()]
     shape = fields.shape
     cells = (C, CELLS, N)
-    phase = near(position_phase())
-    partial, fields, forward_x, plane = call(
+    partial, fields, forward_x, plane, phase = call(
         analysis_kernel,
         [
             near_out((K, 2 * C, MODES)),
             near_out(cells),
             near_out(forward_x.shape, jnp.bfloat16),
             near_out(plane.shape, jnp.bfloat16),
+            near_out((2, MODES)),
         ],
-        [HBM] * 3 + [VMEM],
+        [HBM] * 3,
         [pltpu.SemaphoreType.DMA((C + 2,))],
-    )(far(fields.reshape(cells)), far(forward_x), far(plane), phase)
+    )(far(fields.reshape(cells)), far(forward_x), far(plane))
     partial, cotangent = lax.optimization_barrier((partial, cotangent))
-    fields, cotangent, forward_x, scaled_x, inverse_x, plane = [
+    fields, cotangent, forward_x, scaled_x, inverse_x, plane, phase = [
         near(v)
-        for v in (fields, cotangent.reshape(cells), forward_x, scaled_x, inverse_x, plane)
+        for v in (
+            fields, cotangent.reshape(cells), forward_x, scaled_x, inverse_x, plane, phase
+        )
     ]
     weights = spec_weights.reshape(2, C, C, K, MODES)
     (local,) = call(

time: 75.4 us -> 75.4 us (level)
  no operation moved by 1% of the time
where the time goes in v11:
time: 75.4 us; the launch traced here: 74.9 us
  blocking collectives  50.1 us (66%)
  starting transfers between devices  11.7 us (16%)
  Pallas kernels  8.87 us (12%)
  local copies, waits for them, and re-layouts  3.52 us (5%)
    all_to_all x5, blocking collectives, swap(): lax.all_to_all(pieces, ('row', 'col'), 0, 0, tiled=True, axis_index_group...  50.1 us
    all_to_all x1, starting transfers between devices, swap(): lax.all_to_all(pieces, ('row', 'col'), 0, 0, tiled=True, axis_index_group...  11.7 us
    reshape x1, local copies, waits for them, and re-layouts, per_device(): weights = spec_weights.reshape(2, C, C, K, MODES)  3.49 us
    pallas_call x1, Pallas kernels, per_device(): call(backward_kernel, [jax.ShapeDtypeStruct(cells, jnp.float32), jax.Shap...  3.48 us
    pallas_call x1, Pallas kernels, per_device(): call(analysis_kernel, [near_out((K, 2 * C, MODES)), near_out(cells), near...  2.1 us
    pallas_call x1, Pallas kernels, per_device(): call(forward_kernel, [near_out(cells), near_out((K, 2 * C, MODES))], [VME...  1.66 us
  transfers between devices with their start and end apart: 1, of which 0 were waited for; matrix products, arithmetic and copies ran while one was open for 5% of the time, Pallas kernels for 1%

profile of v11, /device:TPU:1, one launch (start us, length us, event | category | flops | bytes accessed | tf_op | source)
XLA Modules:
  0.0 74.9 jit_solution(11966806629864965133)
XLA Ops:
  0.6 0.0 copy-start.3
  0.6 0.0 copy-start.4
  0.6 2.1 %shard_map.104 = (f32[16,8,256]{2,1,0:T(8,128)S(1)}, f32[4,256,256]{2,1,0:T(8,128)S(1)}, bf16[2,32,256]{2,1,0:T(8,128)(2,1)S(1)}, bf16[2,256,512]{2,1,0:T(8,128)(2,1)S(1)}, f32[2,256]{1,0:T(2,128)S(1)}) custom-call(f32[4,256,256]{2,1,0:T(8,128)} %bitcast.6, bf16[2,32,256]{2,1,0:T(8,128)(2,1)} %constant.8.clone.forward_x, ...), custom_call_target="tpu_custom_call" | custom-call | tf_op jit(solution)/shard_map/pallas_call | solution.py:340
  2.8 0.0 copy-start
  2.8 0.0 copy-start.2
  2.8 11.0 %all_to_all.30.pieces = f32[16,8,256]{2,1,0:T(8,128)S(1)} all-to-all(f32[16,8,256]{2,1,0:T(8,128)S(1)} %get-tuple-element.17), channel_id=1, replica_groups={{201,200,203,202,205,204,207,206,197,196,199,198,193,192,195,194},{217,..., dimensions={0} | all-to-all | bytes 262144 | tf_op jit(solution)/shard_map/all_to_all | solution.py:307
  13.8 0.7 shard_map.105
  14.5 11.7 %all-to-all-start.1 = ((f32[16,8,256]{2,1,0:T(8,128)}), f32[16,8,256]{2,1,0:T(8,128)S(1)}, u32[]{:S(2)}, u32[]{:S(2)}) async-start(f32[16,8,256]{2,1,0:T(8,128)} %shard_map.105), calls=%async_computation.1 | async-start | bytes 262144 | tf_op jit(solution)/shard_map/all_to_all | solution.py:307
  26.2 3.5 %reshape.17.weights = f32[2,4,4,16,256]{4,3,2,1,0:T(8,128)S(1)} reshape(f32[2,4,4,16,16,16]{5,4,3,2,1,0:T(8,128)} %param.11) | data formatting | bytes 1048576 | tf_op jit(solution)/shard_map/reshape | solution.py:359
  29.7 0.0 copy-start.1
  29.7 0.0 copy-done.3
  29.7 0.0 copy-done.4
  29.7 0.9 %shard_map.106.local = f32[4,256,256]{2,1,0:T(8,128)S(1)} custom-call(f32[4,256,256]{2,1,0:T(8,128)S(1)} %get-tuple-element.18.fields, f32[4,4]{1,0:T(4,128)S(1)} %copy-done.3, f32[4]{0:T(128)S(1)} %copy-done.4), custom_call_target="tpu_custom_call", output_to_operand_aliasing={{}: (0, {})} | custom-call | tf_op jit(solution)/shard_map/pallas_call | solution.py:360
  30.6 0.0 all-to-all-done.1.pieces
  30.7 8.8 %all_to_all.31.modes = f32[16,8,256]{2,1,0:T(8,128)S(1)} all-to-all(f32[16,8,256]{2,1,0:T(8,128)S(1)} %shard_map.107), channel_id=1, replica_groups={{201,200,203,202,205,204,207,206,197,196,199,198,193,192,195,194},{217,..., dimensions={0} | all-to-all | bytes 262144 | tf_op jit(solution)/shard_map/all_to_all | solution.py:307
  39.5 0.0 copy-done
  39.5 0.0 copy-done.2
  39.5 1.7 %shard_map.108 = (f32[4,256,256]{2,1,0:T(8,128)S(1)}, f32[16,8,256]{2,1,0:T(8,128)S(1)}) custom-call(f32[16,8,256]{2,1,0:T(8,128)S(1)} %all_to_all.31.modes, f32[2,4,4,16,256]{4,3,2,1,0:T(8,128)S(1)} %reshape.17.weights, f32[4,256,256]{2,1,0:T(8,128)S(1)} %shard_map.106.local, f32[4,256,256]{2,1,0:T(8,128)S(1)} %bitcast.5, ...), custom_call_target="tpu_custom_call" | custom-call | tf_op jit(solution)/shard_map/pallas_call | solution.py:365
  41.2 8.7 %all_to_all.32.pieces = f32[16,8,256]{2,1,0:T(8,128)S(1)} all-to-all(f32[16,8,256]{2,1,0:T(8,128)S(1)} %get-tuple-element.26), channel_id=1, replica_groups={{201,200,203,202,205,204,207,206,197,196,199,198,193,192,195,194},{217,..., dimensions={0} | all-to-all | bytes 262144 | tf_op jit(solution)/shard_map/all_to_all | solution.py:307
  49.9 11.9 %all_to_all.33.pieces = f32[16,8,256]{2,1,0:T(8,128)S(1)} all-to-all(f32[16,8,256]{2,1,0:T(8,128)S(1)} %shard_map.109), channel_id=1, replica_groups={{201,217,185,233,169,249,153,137,75,91,59,107,43,123,27,11},{200,216,18..., dimensions={0} | all-to-all | bytes 262144 | tf_op jit(solution)/shard_map/all_to_all | solution.py:307
  61.8 9.6 %all_to_all.34.back = f32[16,8,256]{2,1,0:T(8,128)S(1)} all-to-all(f32[16,8,256]{2,1,0:T(8,128)S(1)} %shard_map.110), channel_id=1, replica_groups={{201,200,203,202,205,204,207,206,197,196,199,198,193,192,195,194},{217,..., dimensions={0} | all-to-all | bytes 262144 | tf_op jit(solution)/shard_map/all_to_all | solution.py:307
  71.5 0.0 copy-done.1
  71.5 3.5 %shard_map.111 = (f32[4,256,256]{2,1,0:T(8,128)}, f32[2,4,4,16,16,16]{5,4,3,2,1,0:T(8,128)}) custom-call(f32[16,8,256]{2,1,0:T(8,128)S(1)} %all_to_all.31.modes, f32[16,8,256]{2,1,0:T(8,128)S(1)} %all_to_all.34.back, f32[2,4,4,16,256]{4,3,2,1,0:T(8,128)S(1)} %reshape.17.weights, f32[4,256,256]{2,1,0:T(8,128)S(1)} %get-tuple-element.27.up, ...), custom_call_target="tpu_custom_call" | custom-call | tf_op jit(solution)/shard_map/pallas_call | solution.py:371
  (3 shorter events, 0.1 us)
Async XLA Ops:
  0.6 29.1 %copy-start.3 = (f32[4,4]{1,0:T(4,128)S(1)}, f32[4,4]{1,0:T(4,128)}, u32[]{:S(2)}) copy-start(f32[4,4]{1,0:T(4,128)} %point.3) | copy-start | bytes 196
  0.6 29.1 %copy-start.4 = (f32[4]{0:T(128)S(1)}, f32[4]{0:T(128)}, u32[]{:S(2)}) copy-start(f32[4]{0:T(128)} %bias.1) | copy-start | bytes 52
  2.8 36.7 %copy-start = (f32[1,4,16,16,256]{4,3,2,1,0:T(8,128)S(1)}, f32[1,4,16,16,256]{4,3,2,1,0:T(8,128)}, u32[]{:S(2)}) copy-start(f32[1,4,16,16,256]{4,3,2,1,0:T(8,128)} %param.10) | copy-start | bytes 3145732
  2.8 36.7 %copy-start.2 = (bf16[96,256]{1,0:T(8,128)(2,1)S(1)}, bf16[96,256]{1,0:T(8,128)(2,1)}, u32[]{:S(2)}) copy-start(bf16[96,256]{1,0:T(8,128)(2,1)} %constant.9.clone.scaled_x) | copy-start | bytes 147460
  14.5 16.1 %all-to-all-start.1 = ((f32[16,8,256]{2,1,0:T(8,128)}), f32[16,8,256]{2,1,0:T(8,128)S(1)}, u32[]{:S(2)}, u32[]{:S(2)}) async-start(f32[16,8,256]{2,1,0:T(8,128)} %shard_map.105), calls=%async_computation.1 | async-start | bytes 262144 | tf_op jit(solution)/shard_map/all_to_all | solution.py:307
  29.7 41.8 %copy-start.1 = (bf16[96,256]{1,0:T(8,128)(2,1)S(1)}, bf16[96,256]{1,0:T(8,128)(2,1)}, u32[]{:S(2)}) copy-start(bf16[96,256]{1,0:T(8,128)(2,1)} %constant.10.clone.inverse_x) | copy-start | bytes 147460

commit v12 on v11

--- a/solution.py
+++ b/solution.py
@@ -244,9 +244,8 @@
     modes_turned, back_turned = turned(modes[...]), turned(back[...])
     for p in range(K):
         one_wave(p)
-        if p % 2 == 1:
-            some = pl.ds(p - 1, 2)
-            send(stored.at[:, :, :, some], grad_spectral.at[:, :, :, some])
+        some = pl.ds(p, 1)
+        send(stored.at[:, :, :, some], grad_spectral.at[:, :, :, some])
     adjoint_re, adjoint_im = [], []
     for i in range(C):
         re = im = 0.0
@@ -378,7 +377,7 @@
         [
             pltpu.VMEM(cells, jnp.float32),
             pltpu.VMEM((2, C, C, K, K, K), jnp.float32),
-            pltpu.SemaphoreType.DMA((12,)),
+            pltpu.SemaphoreType.DMA((K + C,)),
         ],
     )(modes, back, weights, near(upstream), point_weights, phase, inverse_x, plane)
     return grad_fields.reshape(shape), grad_spectral

time: 75.4 us -> 75.4 us (level)
  no operation moved by 1% of the time
where the time goes in v12:
time: 75.4 us; the launch traced here: 75 us
  blocking collectives  50.1 us (66%)
  starting transfers between devices  11.7 us (16%)
  Pallas kernels  8.88 us (12%)
  local copies, waits for them, and re-layouts  3.52 us (5%)
    all_to_all x5, blocking collectives, swap(): lax.all_to_all(pieces, ('row', 'col'), 0, 0, tiled=True, axis_index_group...  50.1 us
    all_to_all x1, starting transfers between devices, swap(): lax.all_to_all(pieces, ('row', 'col'), 0, 0, tiled=True, axis_index_group...  11.7 us
    pallas_call x1, Pallas kernels, per_device(): call(backward_kernel, [jax.ShapeDtypeStruct(cells, jnp.float32), jax.Shap...  3.5 us
    reshape x1, local copies, waits for them, and re-layouts, per_device(): weights = spec_weights.reshape(2, C, C, K, MODES)  3.49 us
    pallas_call x1, Pallas kernels, per_device(): call(analysis_kernel, [near_out((K, 2 * C, MODES)), near_out(cells), near...  2.1 us
    pallas_call x1, Pallas kernels, per_device(): call(forward_kernel, [near_out(cells), near_out((K, 2 * C, MODES))], [VME...  1.66 us
  transfers between devices with their start and end apart: 1, of which 0 were waited for; matrix products, arithmetic and copies ran while one was open for 5% of the time, Pallas kernels for 1%

profile of v12, /device:TPU:1, one launch (start us, length us, event | category | flops | bytes accessed | tf_op | source)
XLA Modules:
  0.0 75.0 jit_solution(13089314394152076465)
XLA Ops:
  0.6 0.0 copy-start.3
  0.6 0.0 copy-start.4
  0.6 2.1 %shard_map.104 = (f32[16,8,256]{2,1,0:T(8,128)S(1)}, f32[4,256,256]{2,1,0:T(8,128)S(1)}, bf16[2,32,256]{2,1,0:T(8,128)(2,1)S(1)}, bf16[2,256,512]{2,1,0:T(8,128)(2,1)S(1)}, f32[2,256]{1,0:T(2,128)S(1)}) custom-call(f32[4,256,256]{2,1,0:T(8,128)} %bitcast.6, bf16[2,32,256]{2,1,0:T(8,128)(2,1)} %constant.8.clone.forward_x, ...), custom_call_target="tpu_custom_call" | custom-call | tf_op jit(solution)/shard_map/pallas_call | solution.py:339
  2.8 0.0 copy-start
  2.8 0.0 copy-start.2
  2.8 11.0 %all_to_all.30.pieces = f32[16,8,256]{2,1,0:T(8,128)S(1)} all-to-all(f32[16,8,256]{2,1,0:T(8,128)S(1)} %get-tuple-element.17), channel_id=1, replica_groups={{201,200,203,202,205,204,207,206,197,196,199,198,193,192,195,194},{217,..., dimensions={0} | all-to-all | bytes 262144 | tf_op jit(solution)/shard_map/all_to_all | solution.py:306
  13.8 0.7 shard_map.105
  14.5 11.7 %all-to-all-start.1 = ((f32[16,8,256]{2,1,0:T(8,128)}), f32[16,8,256]{2,1,0:T(8,128)S(1)}, u32[]{:S(2)}, u32[]{:S(2)}) async-start(f32[16,8,256]{2,1,0:T(8,128)} %shard_map.105), calls=%async_computation.1 | async-start | bytes 262144 | tf_op jit(solution)/shard_map/all_to_all | solution.py:306
  26.2 3.5 %reshape.17.weights = f32[2,4,4,16,256]{4,3,2,1,0:T(8,128)S(1)} reshape(f32[2,4,4,16,16,16]{5,4,3,2,1,0:T(8,128)} %param.11) | data formatting | bytes 1048576 | tf_op jit(solution)/shard_map/reshape | solution.py:358
  29.7 0.0 copy-start.1
  29.7 0.0 copy-done.3
  29.7 0.0 copy-done.4
  29.7 0.9 %shard_map.106.local = f32[4,256,256]{2,1,0:T(8,128)S(1)} custom-call(f32[4,256,256]{2,1,0:T(8,128)S(1)} %get-tuple-element.18.fields, f32[4,4]{1,0:T(4,128)S(1)} %copy-done.3, f32[4]{0:T(128)S(1)} %copy-done.4), custom_call_target="tpu_custom_call", output_to_operand_aliasing={{}: (0, {})} | custom-call | tf_op jit(solution)/shard_map/pallas_call | solution.py:359
  30.6 0.0 all-to-all-done.1.pieces
  30.7 8.8 %all_to_all.31.modes = f32[16,8,256]{2,1,0:T(8,128)S(1)} all-to-all(f32[16,8,256]{2,1,0:T(8,128)S(1)} %shard_map.107), channel_id=1, replica_groups={{201,200,203,202,205,204,207,206,197,196,199,198,193,192,195,194},{217,..., dimensions={0} | all-to-all | bytes 262144 | tf_op jit(solution)/shard_map/all_to_all | solution.py:306
  39.5 0.0 copy-done
  39.5 0.0 copy-done.2
  39.5 1.7 %shard_map.108 = (f32[4,256,256]{2,1,0:T(8,128)S(1)}, f32[16,8,256]{2,1,0:T(8,128)S(1)}) custom-call(f32[16,8,256]{2,1,0:T(8,128)S(1)} %all_to_all.31.modes, f32[2,4,4,16,256]{4,3,2,1,0:T(8,128)S(1)} %reshape.17.weights, f32[4,256,256]{2,1,0:T(8,128)S(1)} %shard_map.106.local, f32[4,256,256]{2,1,0:T(8,128)S(1)} %bitcast.5, ...), custom_call_target="tpu_custom_call" | custom-call | tf_op jit(solution)/shard_map/pallas_call | solution.py:364
  41.2 8.7 %all_to_all.32.pieces = f32[16,8,256]{2,1,0:T(8,128)S(1)} all-to-all(f32[16,8,256]{2,1,0:T(8,128)S(1)} %get-tuple-element.26), channel_id=1, replica_groups={{201,200,203,202,205,204,207,206,197,196,199,198,193,192,195,194},{217,..., dimensions={0} | all-to-all | bytes 262144 | tf_op jit(solution)/shard_map/all_to_all | solution.py:306
  49.9 11.9 %all_to_all.33.pieces = f32[16,8,256]{2,1,0:T(8,128)S(1)} all-to-all(f32[16,8,256]{2,1,0:T(8,128)S(1)} %shard_map.109), channel_id=1, replica_groups={{201,217,185,233,169,249,153,137,75,91,59,107,43,123,27,11},{200,216,18..., dimensions={0} | all-to-all | bytes 262144 | tf_op jit(solution)/shard_map/all_to_all | solution.py:306
  61.8 9.6 %all_to_all.34.back = f32[16,8,256]{2,1,0:T(8,128)S(1)} all-to-all(f32[16,8,256]{2,1,0:T(8,128)S(1)} %shard_map.110), channel_id=1, replica_groups={{201,200,203,202,205,204,207,206,197,196,199,198,193,192,195,194},{217,..., dimensions={0} | all-to-all | bytes 262144 | tf_op jit(solution)/shard_map/all_to_all | solution.py:306
  71.5 0.0 copy-done.1
  71.5 3.5 %shard_map.111 = (f32[4,256,256]{2,1,0:T(8,128)}, f32[2,4,4,16,16,16]{5,4,3,2,1,0:T(8,128)}) custom-call(f32[16,8,256]{2,1,0:T(8,128)S(1)} %all_to_all.31.modes, f32[16,8,256]{2,1,0:T(8,128)S(1)} %all_to_all.34.back, f32[2,4,4,16,256]{4,3,2,1,0:T(8,128)S(1)} %reshape.17.weights, f32[4,256,256]{2,1,0:T(8,128)S(1)} %get-tuple-element.27.up, ...), custom_call_target="tpu_custom_call" | custom-call | tf_op jit(solution)/shard_map/pallas_call | solution.py:370
  (3 shorter events, 0.1 us)
Async XLA Ops:
  0.6 29.1 %copy-start.3 = (f32[4,4]{1,0:T(4,128)S(1)}, f32[4,4]{1,0:T(4,128)}, u32[]{:S(2)}) copy-start(f32[4,4]{1,0:T(4,128)} %point.3) | copy-start | bytes 196
  0.6 29.1 %copy-start.4 = (f32[4]{0:T(128)S(1)}, f32[4]{0:T(128)}, u32[]{:S(2)}) copy-start(f32[4]{0:T(128)} %bias.1) | copy-start | bytes 52
  2.8 36.7 %copy-start = (f32[1,4,16,16,256]{4,3,2,1,0:T(8,128)S(1)}, f32[1,4,16,16,256]{4,3,2,1,0:T(8,128)}, u32[]{:S(2)}) copy-start(f32[1,4,16,16,256]{4,3,2,1,0:T(8,128)} %param.10) | copy-start | bytes 3145732
  2.8 36.7 %copy-start.2 = (bf16[96,256]{1,0:T(8,128)(2,1)S(1)}, bf16[96,256]{1,0:T(8,128)(2,1)}, u32[]{:S(2)}) copy-start(bf16[96,256]{1,0:T(8,128)(2,1)} %constant.9.clone.scaled_x) | copy-start | bytes 147460
  14.5 16.1 %all-to-all-start.1 = ((f32[16,8,256]{2,1,0:T(8,128)}), f32[16,8,256]{2,1,0:T(8,128)S(1)}, u32[]{:S(2)}, u32[]{:S(2)}) async-start(f32[16,8,256]{2,1,0:T(8,128)} %shard_map.105), calls=%async_computation.1 | async-start | bytes 262144 | tf_op jit(solution)/shard_map/all_to_all | solution.py:306
  29.7 41.8 %copy-start.1 = (bf16[96,256]{1,0:T(8,128)(2,1)S(1)}, bf16[96,256]{1,0:T(8,128)(2,1)}, u32[]{:S(2)}) copy-start(bf16[96,256]{1,0:T(8,128)(2,1)} %constant.10.clone.inverse_x) | copy-start | bytes 147460
